TPU v7x, 8 devices: a whole 2x2x1 slice. The times are simulated.
8 devices in a mesh: dp: 1 (over z), sp: 8 (over y, x, core).
Axes of the slice: x: 2, y: 2, z: 1, core: 2. Of those that a mesh axis runs over, the one named last changes fastest.
Arguments:
- x_in: bfloat16 [4, 2048, 4608], P('dp', 'sp')
- dy_in: bfloat16 [4, 2048, 4608], P('dp', 'sp')
- positions: int32 [2048], P(('dp', 'sp'))
- w_q: bfloat16 [4608, 4096], replicated
- w_k: bfloat16 [4608, 2048], replicated
- w_v: bfloat16 [4608, 2048], replicated
- w_o: bfloat16 [4096, 4608], replicated
- w_pre: float32 [4608], replicated
- w_post: float32 [4608], replicated
- q_norm: float32 [128], replicated
- k_norm: float32 [128], replicated
Outputs:
- output 1: bfloat16 [4, 2048, 4608], P('dp', 'sp')
- output 2: bfloat16 [4, 2048, 4608], P('dp', 'sp')
- output 3: bfloat16 [4608, 4096], P('dp')
- output 4: bfloat16 [4608, 2048], P('dp')
- output 5: bfloat16 [4608, 2048], P('dp')
- output 6: bfloat16 [4096, 4608], P('dp')
- output 7: float32 [4608], P('dp')
- output 8: float32 [4608], P('dp')
- output 9: float32 [128], P('dp')
- output 10: float32 [128], P('dp')
All inputs are finite; a program needn't handle non-finite values.
Results may differ from a plain program's by a relative error of at most 0.02.
Values are sent between devices in bfloat16 or wider.
A program may use at most 1 GiB of HBM per device.

v0:
```python
import functools
import jax
import jax.numpy as jnp
from jax import lax
from jax.sharding import PartitionSpec as P

EPS = 1e-6
ROPE_BASE = 1000000.0
ROPE_SCALE = 8.0
NEG_BIG = -1e30
Q_BLOCK = 1024


def rms_scale(x_f32, weight):
    inv_rms = lax.rsqrt(jnp.mean(x_f32 * x_f32, axis=-1, keepdims=True) + EPS)
    return x_f32 * inv_rms * (1.0 + weight)


def pre_norm(x_f32, weight):
    return rms_scale(x_f32, weight).astype(jnp.bfloat16)


def post_norm(proj, weight):
    return rms_scale(proj.astype(jnp.float32), weight)


def rope_tables(positions, head):
    half_dim = head // 2
    inv_freq = ROPE_BASE ** (-jnp.arange(half_dim, dtype=jnp.float32) * 2.0 / head)
    angles = (positions.astype(jnp.float32) / ROPE_SCALE)[:, None] * inv_freq[None, :]
    return jnp.cos(angles), jnp.sin(angles)


def norm_rope(heads_bf, weight, cosines, sines):
    half_dim = heads_bf.shape[-1] // 2
    normed = rms_scale(heads_bf.astype(jnp.float32), weight)
    first = normed[..., :half_dim]
    second = normed[..., half_dim:]
    cos_b = cosines[None, :, None, :]
    sin_b = sines[None, :, None, :]
    rotated = jnp.concatenate([first * cos_b - second * sin_b, second * cos_b + first * sin_b], axis=-1)
    return rotated.astype(jnp.bfloat16)


def causal_mask(start, block, end):
    row_ids = start + jnp.arange(block)
    col_ids = jnp.arange(end)
    return row_ids[:, None] >= col_ids[None, :]


def attention_fwd(q_all, k_all, v_all):
    batch, seq, q_heads, head = q_all.shape
    kv_loc = k_all.shape[2]
    scale = head ** -0.5
    block = min(Q_BLOCK, seq)
    q_grp = q_all.reshape(batch, seq, kv_loc, q_heads // kv_loc, head)
    pieces = []
    row_lse = []
    for index in range(seq // block):
        start = index * block
        end = start + block
        scores = jnp.einsum('bqkgh,bskh->bkgqs', q_grp[:, start:end], k_all[:, :end], preferred_element_type=jnp.float32) * scale
        scores = jnp.where(causal_mask(start, block, end), scores, NEG_BIG)
        row_max = jnp.max(scores, axis=-1, keepdims=True)
        exp_scores = jnp.exp(scores - row_max)
        row_sum = jnp.sum(exp_scores, axis=-1, keepdims=True)
        attn_prob = (exp_scores / row_sum).astype(jnp.bfloat16)
        pieces.append(jnp.einsum('bkgqs,bskh->bqkgh', attn_prob, v_all[:, :end], preferred_element_type=jnp.float32).astype(jnp.bfloat16))
        row_lse.append(row_max + jnp.log(row_sum))
    return jnp.concatenate(pieces, axis=1).reshape(batch, seq, q_heads, head), row_lse


def attention_bwd(q_all, k_all, v_all, row_lse, d_out):
    batch, seq, q_heads, head = q_all.shape
    kv_loc = k_all.shape[2]
    per_kv = q_heads // kv_loc
    scale = head ** -0.5
    block = min(Q_BLOCK, seq)
    q_grp = q_all.reshape(batch, seq, kv_loc, per_kv, head)
    do_grp = d_out.reshape(batch, seq, kv_loc, per_kv, head)
    dk_acc = jnp.zeros(k_all.shape, jnp.float32)
    dv_acc = jnp.zeros(v_all.shape, jnp.float32)
    dq_pieces = []
    for index in range(seq // block):
        start = index * block
        end = start + block
        q_blk = q_grp[:, start:end]
        do_blk = do_grp[:, start:end]
        k_pre = k_all[:, :end]
        v_pre = v_all[:, :end]
        scores = jnp.einsum('bqkgh,bskh->bkgqs', q_blk, k_pre, preferred_element_type=jnp.float32) * scale
        scores = jnp.where(causal_mask(start, block, end), scores, NEG_BIG)
        attn_prob = jnp.exp(scores - row_lse[index])
        d_prob = jnp.einsum('bqkgh,bskh->bkgqs', do_blk, v_pre, preferred_element_type=jnp.float32)
        d_score = (attn_prob * (d_prob - jnp.sum(d_prob * attn_prob, axis=-1, keepdims=True)) * scale).astype(jnp.bfloat16)
        dq_pieces.append(jnp.einsum('bkgqs,bskh->bqkgh', d_score, k_pre, preferred_element_type=jnp.float32).astype(jnp.bfloat16))
        dk_part = jnp.einsum('bkgqs,bqkgh->bskh', d_score, q_blk, preferred_element_type=jnp.float32)
        dv_part = jnp.einsum('bkgqs,bqkgh->bskh', attn_prob.astype(jnp.bfloat16), do_blk, preferred_element_type=jnp.float32)
        dk_acc = lax.dynamic_update_slice(dk_acc, dk_acc[:, :end] + dk_part, (0, 0, 0, 0))
        dv_acc = lax.dynamic_update_slice(dv_acc, dv_acc[:, :end] + dv_part, (0, 0, 0, 0))
    dq_all = jnp.concatenate(dq_pieces, axis=1).reshape(batch, seq, q_heads, head)
    return dq_all, dk_acc.astype(jnp.bfloat16), dv_acc.astype(jnp.bfloat16)


def fold_copies(grad_wide, kv_heads, rep):
    if rep == 1:
        return grad_wide
    batch, seq_loc, wide, head = grad_wide.shape
    summed = jnp.sum(grad_wide.reshape(batch, seq_loc, kv_heads, rep, head), axis=3, dtype=jnp.float32)
    return summed.astype(jnp.bfloat16)


def solution(mesh):
    group = mesh.shape['sp']

    def to_heads(arr):
        return lax.all_to_all(arr, 'sp', 2, 1, tiled=True)

    def to_tokens(arr):
        return lax.all_to_all(arr, 'sp', 1, 2, tiled=True)

    def device_step(x_in, dy_in, positions, w_q, w_k, w_v, w_o, w_pre, w_post, q_norm, k_norm):
        batch, seq_loc, width = x_in.shape
        head = q_norm.shape[0]
        heads = w_q.shape[1] // head
        kv_heads = w_k.shape[1] // head
        rep = max(1, group // kv_heads)
        x_f32 = x_in.astype(jnp.float32)
        normed, pre_pull = jax.vjp(pre_norm, x_f32, w_pre)
        q_proj = jnp.einsum('bsd,dn->bsn', normed, w_q, preferred_element_type=jnp.float32).astype(jnp.bfloat16).reshape(batch, seq_loc, heads, head)
        k_proj = jnp.einsum('bsd,dn->bsn', normed, w_k, preferred_element_type=jnp.float32).astype(jnp.bfloat16).reshape(batch, seq_loc, kv_heads, head)
        v_proj = jnp.einsum('bsd,dn->bsn', normed, w_v, preferred_element_type=jnp.float32).astype(jnp.bfloat16).reshape(batch, seq_loc, kv_heads, head)
        cosines, sines = rope_tables(positions, head)
        q_rot, q_pull = jax.vjp(functools.partial(norm_rope, cosines=cosines, sines=sines), q_proj, q_norm)
        k_rot, k_pull = jax.vjp(functools.partial(norm_rope, cosines=cosines, sines=sines), k_proj, k_norm)
        q_all = to_heads(q_rot)
        k_all = to_heads(jnp.repeat(k_rot, rep, axis=2))
        v_all = to_heads(jnp.repeat(v_proj, rep, axis=2))
        o_all, row_lse = attention_fwd(q_all, k_all, v_all)
        o_flat = to_tokens(o_all).reshape(batch, seq_loc, heads * head)
        proj = jnp.einsum('bsn,nd->bsd', o_flat, w_o, preferred_element_type=jnp.float32).astype(jnp.bfloat16)
        post, post_pull = jax.vjp(post_norm, proj, w_post)
        y_out = (x_f32 + post).astype(jnp.bfloat16)
        dy_f32 = dy_in.astype(jnp.float32)
        d_proj, dw_post = post_pull(dy_f32)
        dw_o = jnp.einsum('bsn,bsd->nd', o_flat, d_proj, preferred_element_type=jnp.float32)
        d_oflat = jnp.einsum('bsd,nd->bsn', d_proj, w_o, preferred_element_type=jnp.float32).astype(jnp.bfloat16)
        d_oall = to_heads(d_oflat.reshape(batch, seq_loc, heads, head))
        dq_all, dk_all, dv_all = attention_bwd(q_all, k_all, v_all, row_lse, d_oall)
        dq_rot = to_tokens(dq_all)
        dk_rot = fold_copies(to_tokens(dk_all), kv_heads, rep)
        dv_proj = fold_copies(to_tokens(dv_all), kv_heads, rep)
        dq_proj, dq_norm = q_pull(dq_rot)
        dk_proj, dk_norm = k_pull(dk_rot)
        dq_flat = dq_proj.reshape(batch, seq_loc, heads * head)
        dk_flat = dk_proj.reshape(batch, seq_loc, kv_heads * head)
        dv_flat = dv_proj.reshape(batch, seq_loc, kv_heads * head)
        dw_q = jnp.einsum('bsd,bsn->dn', normed, dq_flat, preferred_element_type=jnp.float32)
        dw_k = jnp.einsum('bsd,bsn->dn', normed, dk_flat, preferred_element_type=jnp.float32)
        dw_v = jnp.einsum('bsd,bsn->dn', normed, dv_flat, preferred_element_type=jnp.float32)
        d_normed = (jnp.einsum('bsn,dn->bsd', dq_flat, w_q, preferred_element_type=jnp.float32)
                    + jnp.einsum('bsn,dn->bsd', dk_flat, w_k, preferred_element_type=jnp.float32)
                    + jnp.einsum('bsn,dn->bsd', dv_flat, w_v, preferred_element_type=jnp.float32)).astype(jnp.bfloat16)
        dx_norm, dw_pre = pre_pull(d_normed)
        dx_out = (dy_f32 + dx_norm).astype(jnp.bfloat16)
        sums = lax.psum((dw_q, dw_k, dw_v, dw_o, dw_pre, dw_post, dq_norm, dk_norm), 'sp')
        return (y_out, dx_out, sums[0].astype(jnp.bfloat16), sums[1].astype(jnp.bfloat16), sums[2].astype(jnp.bfloat16), sums[3].astype(jnp.bfloat16), sums[4], sums[5], sums[6], sums[7])

    token_spec = P('dp', 'sp', None)
    return jax.shard_map(device_step, mesh=mesh,
                         in_specs=(token_spec, token_spec, P(('dp', 'sp')), P(None, None), P(None, None), P(None, None), P(None, None), P(None), P(None), P(None), P(None)),
                         out_specs=(token_spec, token_spec, P('dp', None), P('dp', None), P('dp', None), P('dp', None), P('dp'), P('dp'), P('dp'), P('dp')),
                         check_vma=False)
```

profile of v0, /device:TPU:0, one launch (start us, length us, event | category | flops | bytes accessed | tf_op | source)
XLA Modules:
  0.0 4569.9 jit_solution(5033643229115430905)
XLA Ops:
  0.7 5.7 fusion.45
  7.2 22.8 convert_bitcast_fusion.5
  37.8 24.3 convert_convert_fusion.1
  70.6 10.3 copy.240
  90.0 6.4 copy.241
  96.4 48.2 %convert_convert_fusion = f32[4,256,4096]{2,1,0:T(8,128)} fusion(bf16[4608,4096]{1,0:T(8,128)(2,1)} %param.14, bf16[4,256,4608]{2,1,0:T(8,128)(2,1)} %param.11, f32[4608]{0:T(1024)S(1)} %broadcast_add_fusion.1, f32[4,256]{1,0:T(4,128)S(1)} %fusion.99), kind=kOutput, calls=%fused_computation.115 | convolution fusion | flops 38681968640 | bytes 63985664 | tf_op jit(solution)/shard_map/bsd,dn->bsn/dot_general | solution.py:130
  144.6 14.2 copy.328
  162.3 8.2 multiply_reduce_fusion.2
  170.7 19.3 copy.244
  190.7 7.4 multiply_multiply_fusion
  198.2 4.9 subtract_convert_fusion
  203.1 8.0 pad_maximum_fusion
  211.0 11.9 copy.245
  228.8 7.8 copy.238
  236.7 7.4 all_to_all.87
  244.1 7.4 reshape.250
  256.1 64.6 %all-to-all-done.2 = bf16[4,256,32,128]{3,1,0,2:T(8,128)(2,1)} async-done(((bf16[4,256,32,128]{3,1,0,2:T(8,128)(2,1)}), bf16[4,256,32,128]{3,1,0,2:T(8,128)(2,1)}, u32[]{:S(2)}, u32[]{:S(2)}) %all-to-all-start.2) | async-done | bytes 8388640 | tf_op jit(solution)/shard_map/all_to_all | solution.py:117
  320.7 7.9 copy.246
  328.6 27.4 fusion.118
  356.0 21.0 fusion.14
  377.1 26.2 convert_bitcast_fusion.4
  403.2 48.6 %fusion.117 = (f32[4,2,2,1024]{3,2,1,0:T(2,128)S(1)}, f32[4,2,2,1024,2048]{3,4,2,1,0:T(8,128)}) fusion(bf16[4,2048,2,128,1]{3,1,4,2,0:T(8,128)(2,1)} %bitcast.297, bf16[4,2048,2,2,128]{4,1,3,2,0:T(8,128)(2,1)} %bitcast.290, pred[1024,2048]{0,1:T(8,128)(4,1)S(1)} %iota_compare_fusion), kind=kOutput, calls=%fused_computation.179 | convolution fusion | flops 8690581504 | bytes 144769024 | tf_op jit(solution)/shard_map/bqkgh,bskh->bkgqs/dot_general | solution.py:62
  451.8 40.8 fusion.5
  492.7 45.9 %convert_bitcast_fusion.3 = bf16[4,1024,2,2,128]{1,4,3,2,0:T(8,128)(2,1)} fusion(f32[4,2,2,1024,2048]{3,4,2,1,0:T(8,128)} %get-tuple-element.38, f32[4,2,2,1024]{3,2,1,0:T(2,128)S(1)} %fusion.5, f32[4,2,2,1024]{3,2,1,0:T(2,128)S(1)} %get-tuple-element.37, bf16[4,2048,2,128,1]{1,3,2,0,4:T(8,128)(2,1)} %reshape.250), kind=kOutput, calls=%fused_computation.128 | convolution fusion | flops 8692695040 | bytes 142737408 | tf_op jit(solution)/shard_map/bkgqs,bskh->bqkgh/dot_general | solution.py:68
  538.6 8.3 pad_maximum_fusion.1
  546.9 14.5 copy.249
  565.7 94.0 %all-to-all-done.3 = bf16[4,2048,4,128]{3,2,0,1:T(4,128)(2,1)} async-done(((bf16[4,2048,4,128]{3,2,0,1:T(4,128)(2,1)}), bf16[4,2048,4,128]{3,2,0,1:T(4,128)(2,1)}, u32[]{:S(2)}, u32[]{:S(2)}) %all-to-all-start.3) | async-done | bytes 8388640 | tf_op jit(solution)/shard_map/all_to_all | solution.py:120
  659.7 8.1 copy.334
  667.7 14.5 reshape.231
  682.2 45.8 %fusion.43 = (f32[4,256]{1,0:T(4,128)S(1)}, bf16[4,256,4608]{2,1,0:T(8,128)(2,1)S(1)}) fusion(bf16[4,256,4096]{2,1,0:T(8,128)(2,1)} %reshape.231, bf16[4096,4608]{1,0:T(8,128)(2,1)} %param.17), kind=kOutput, calls=%fused_computation.74 | convolution fusion | flops 38673580032 | bytes 55578624 | tf_op jit(solution)/shard_map/bsn,nd->bsd/dot_general | solution.py:141
  728.1 17.2 fusion.41
  745.3 67.6 %convert_bitcast_fusion = bf16[4,32,32,8,128]{4,3,2,1,0:T(8,128)(2,1)} fusion(bf16[4096,4608]{1,0:T(8,128)(2,1)} %param.17, bf16[4,256,4608]{2,1,0:T(8,128)(2,1)} %param.12, bf16[4,256,4608]{2,1,0:T(8,128)(2,1)} %copy-done.3, f32[4,256]{1,0:T(4,128)S(1)} %multiply_multiply_fusion.5, f32[4608]{0:T(1024)S(1)} %broadcast_add_fusion, f32[4,256]{1,0:T(4,128)S(1)} %fusion.100), kind=kOutput, calls=%fused_computation.111 | convolution fusion | flops 38696648704 | bytes 65038336 | tf_op jit(solution)/shard_map/bsd,nd->bsn/dot_general | solution.py:147
  812.9 9.0 copy.333
  826.3 52.9 %convolution_bitcast_fusion = f32[4096,4608]{1,0:T(8,128)} fusion(bf16[4,256,4096]{2,1,0:T(8,128)(2,1)} %reshape.231, bf16[4,256,4608]{2,1,0:T(8,128)(2,1)} %param.12, bf16[4,256,4608]{2,1,0:T(8,128)(2,1)} %copy-done.3, f32[4,256]{1,0:T(4,128)S(1)} %multiply_multiply_fusion.5, f32[4608]{0:T(1024)S(1)} %broadcast_add_fusion, f32[4,256]{1,0:T(4,128)S(1)} %fusion.100), kind=kOutput, calls=%fused_computation.28 | convolution fusion | flops 38692454400 | bytes 102787072 | tf_op jit(solution)/shard_map/bsn,bsd->nd/dot_general | solution.py:146
  879.1 40.9 all-to-all-done.4
  920.1 8.0 copy.252
  928.1 25.4 fusion.81
  953.5 45.9 %fusion.71 = f32[4,2,2048,1024,2]{3,2,4,1,0:T(8,128)} fusion(bf16[4,2048,2,128]{1,3,2,0:T(8,128)(2,1)S(1)} %copy-done.2, bf16[4,2048,2,2,128]{4,1,3,2,0:T(8,128)(2,1)} %bitcast.265), kind=kOutput, calls=%fused_computation.120 | convolution fusion | flops 8589934592 | bytes 142606336 | tf_op jit(solution)/shard_map/bqkgh,bskh->bkgqs/dot_general | solution.py:94
  999.4 26.6 fusion.92
  1026.0 47.1 %fusion.63 = bf16[4,2048,2,128]{1,3,2,0:T(8,128)(2,1)} fusion(f32[4,1024,2,128]{1,3,2,0:T(8,128)} %fusion.92, f32[4,2,2,1024,2048]{3,4,2,1,0:T(8,128)} %get-tuple-element.38, f32[4,2,2,1024]{3,2,1,0:T(2,128)S(1)} %log_add_fusion, bf16[4,2048,2,2,128]{4,1,3,2,0:T(8,128)(2,1)} %bitcast.267), kind=kOutput, calls=%fused_computation.102 | convolution fusion | flops 8661237760 | bytes 146866176 | tf_op jit(solution)/shard_map/bkgqs,bqkgh->bskh/dot_general | solution.py:98
  1073.0 11.1 copy.277
  1087.6 163.9 %convert_bitcast_fusion.1 = bf16[4,1024,2,2,128]{1,4,3,2,0:T(8,128)(2,1)} fusion(bf16[4,2048,2,128,1]{3,1,4,2,0:T(8,128)(2,1)} %bitcast.298, f32[4,2,2048,1024,2]{3,2,4,1,0:T(8,128)} %fusion.71, f32[4,2,2,1024,2048]{3,4,2,1,0:T(8,128)} %get-tuple-element.38, f32[4,2,2,1024]{3,2,1,0:T(2,128)S(1)} %log_add_fusion), kind=kOutput, calls=%fused_computation.126 | convolution fusion | flops 8826931200 | bytes 276889600 | tf_op jit(solution)/shard_map/bkgqs,bskh->bqkgh/dot_general | solution.py:96
  1251.5 84.0 %convert_bitcast_fusion.2 = bf16[4,1024,2,2,128]{1,4,3,2,0:T(8,128)(2,1)} fusion(f32[4,2,1024,1024,2]{3,2,4,1,0:T(8,128)} %fusion.81, f32[4,2,2,1024,1024]{3,4,2,1,0:T(8,128)} %get-tuple-element.40, f32[4,2,2,1024]{3,2,1,0:T(2,128)S(1)} %log_add_fusion.1, bf16[4,2048,2,128]{3,1,2,0:T(8,128)(2,1)} %bitcast.299), kind=kOutput, calls=%fused_computation.127 | convolution fusion | flops 4414522368 | bytes 274857984 | tf_op jit(solution)/shard_map/bkgqs,bskh->bqkgh/dot_general | solution.py:96
  1335.5 8.3 pad_maximum_fusion.2
  1343.8 14.6 copy.259
  1358.4 85.5 %fusion.89 = f32[4,1024,2,128]{1,3,2,0:T(8,128)} fusion(f32[4,2,1024,1024,2]{3,2,4,1,0:T(8,128)} %fusion.81, f32[4,2,2,1024,1024]{3,4,2,1,0:T(8,128)} %get-tuple-element.40, f32[4,2,2,1024]{3,2,1,0:T(2,128)S(1)} %log_add_fusion.1, bf16[4,2048,2,2,128]{4,1,3,2,0:T(8,128)(2,1)} %bitcast.291), kind=kOutput, calls=%fused_computation.144 | convolution fusion | flops 4412425216 | bytes 276955136 | tf_op jit(solution)/shard_map/bkgqs,bqkgh->bskh/dot_general | solution.py:97
  1443.9 165.3 %fusion.64 = bf16[4,2048,2,128]{1,3,2,0:T(8,128)(2,1)} fusion(f32[4,1024,2,128]{1,3,2,0:T(8,128)} %fusion.89, f32[4,2,2048,1024,2]{3,2,4,1,0:T(8,128)} %fusion.71, f32[4,2,2,1024,2048]{3,4,2,1,0:T(8,128)} %get-tuple-element.38, f32[4,2,2,1024]{3,2,1,0:T(2,128)S(1)} %log_add_fusion, bf16[4,2048,2,2,128]{4,1,3,2,0:T(8,128)(2,1)} %bitcast.292), kind=kOutput, calls=%fused_computation.104 | convolution fusion | flops 8829028352 | bytes 549584896 | tf_op jit(solution)/shard_map/bkgqs,bqkgh->bskh/dot_general | solution.py:97
  1609.2 11.1 copy.268
  1623.7 7.1 copy.336
  1630.8 7.8 reshape.237
  1638.6 28.4 convolution_bitcast_fusion.2
  1666.9 5.8 all-to-all-done.6
  1676.9 12.2 copy.269
  1704.3 25.7 fusion.48
  1730.0 29.0 convolution_bitcast_fusion.3
  1759.1 25.6 fusion.52
  1784.7 15.6 copy.260
  1800.4 14.0 multiply_add_fusion.1
  1816.8 9.7 multiply_reduce_fusion
  1826.5 11.0 fusion.56
  1837.6 50.6 %convolution_bitcast_fusion.1 = f32[4608,4096]{1,0:T(8,128)} fusion(bf16[4,256,4096]{1,2,0:T(8,128)(2,1)} %bitcast.294, bf16[4,256,4608]{2,1,0:T(8,128)(2,1)} %param.11, f32[4608]{0:T(1024)S(1)} %copy-done.28, f32[4,256]{1,0:T(4,128)S(1)} %copy-done.33), kind=kOutput, calls=%fused_computation.29 | convolution fusion | flops 38673580032 | bytes 93345792 | tf_op jit(solution)/shard_map/bsd,bsn->dn/dot_general | solution.py:158
  1888.1 54.6 %fusion.39 = (f32[4608]{0:T(1024)S(1)}, f32[4,256]{1,0:T(4,128)S(1)}, bf16[4,256,4608]{2,1,0:T(8,128)(2,1)}) fusion(bf16[4,256,4608]{2,1,0:T(8,128)(2,1)} %param.11, f32[4,256]{1,0:T(4,128)S(1)} %copy-done.33, f32[4608]{0:T(1024)S(1)} %copy-done.28, f32[4,256,4608]{2,1,0:T(8,128)} %fusion.52, f32[4,256,4608]{2,1,0:T(8,128)} %fusion.48, ...), kind=kOutput, calls=%fused_computation.70 | convolution fusion | flops 38706606080 | bytes 102805504 | tf_op jit(solution)/shard_map/bsn,dn->bsd/dot_general | solution.py:161
  1942.8 14.7 fusion.40
  1957.5 2612.2 %all-reduce.8 = (bf16[4608,4096]{1,0:T(8,128)(2,1)}, bf16[4608,2048]{1,0:T(8,128)(2,1)}, bf16[4608,2048]{1,0:T(8,128)(2,1)}, bf16[4096,4608]{1,0:T(8,128)(2,1)},...) all-reduce(f32[4608,4096]{1,0:T(8,128)} %convolution_bitcast_fusion, ...), channel_id=1, replica_groups=mesh['dp'=1,'sp'=8] {'sp'}, use_global_device_ids=true, to_apply=%region_14.15 | all-reduce | flops 56632576 | bytes 339814400 | tf_op jit(solution)/shard_map/psum | solution.py:166
  (151 shorter events, 78.1 us)
Async XLA Ops:
  0.6 6.5 copy-start
  6.4 23.6 copy-start.29
  6.4 90.0 %copy-start.32 = (f32[4,256]{1,0:T(4,128)}, f32[4,256]{1,0:T(4,128)S(1)}, u32[]{:S(2)}) copy-start(f32[4,256]{1,0:T(4,128)S(1)} %fusion.99) | copy-start | bytes 12292
  7.1 89.3 %copy-start.27 = (f32[4608]{0:T(1024)}, f32[4608]{0:T(1024)S(1)}, u32[]{:S(2)}) copy-start(f32[4608]{0:T(1024)S(1)} %broadcast_add_fusion.1) | copy-start | bytes 55300
  30.0 7.8 copy-start.41
  30.0 7.8 copy-start.40
  33.2 125.6 %all-to-all-start = ((bf16[4,256,16,128]{3,1,0,2:T(8,128)(2,1)}), bf16[4,256,16,128]{3,1,0,2:T(8,128)(2,1)}, u32[]{:S(2)}, u32[]{:S(2)}) async-start(bf16[4,256,16,128]{3,1,0,2:T(8,128)(2,1)} %bitcast.287), calls=%async_computation | async-start | bytes 8388608 | tf_op jit(solution)/shard_map/all_to_all | solution.py:117
  37.8 43.4 copy-start.34
  64.2 3.4 copy-start.1
  70.0 0.6 copy-start.16
  70.0 16.0 copy-start.14
  81.2 117.0 %copy-start.8 = (f32[256,64]{0,1:T(8,128)}, f32[256,64]{0,1:T(8,128)S(1)}, u32[]{:S(2)}) copy-start(f32[256,64]{0,1:T(8,128)S(1)} %get-tuple-element.35) | copy-start | bytes 196612
  81.2 117.0 %copy-start.10 = (f32[256,64]{0,1:T(8,128)}, f32[256,64]{0,1:T(8,128)S(1)}, u32[]{:S(2)}) copy-start(f32[256,64]{0,1:T(8,128)S(1)} %get-tuple-element.36) | copy-start | bytes 196612
  158.8 64.2 %all-to-all-start.1 = ((bf16[4,256,16,128]{3,1,0,2:T(8,128)(2,1)}), bf16[4,256,16,128]{3,1,0,2:T(8,128)(2,1)}, u32[]{:S(2)}, u32[]{:S(2)}) async-start(bf16[4,256,16,128]{3,1,0,2:T(8,128)(2,1)} %copy.241), calls=%async_computation.1 | async-start | bytes 8388608 | tf_op jit(solution)/shard_map/all_to_all | solution.py:117
  170.7 19.3 copy-start.12
  170.7 19.3 copy-start.42
  190.0 8.2 copy-start.36
  190.1 0.6 copy-start.6
  223.0 97.7 %all-to-all-start.2 = ((bf16[4,256,32,128]{3,1,0,2:T(8,128)(2,1)}), bf16[4,256,32,128]{3,1,0,2:T(8,128)(2,1)}, u32[]{:S(2)}, u32[]{:S(2)}) async-start(bf16[4,256,32,128]{3,1,0,2:T(8,128)(2,1)} %copy.245), calls=%async_computation.2 | async-start | bytes 16777216 | tf_op jit(solution)/shard_map/all_to_all | solution.py:117
  356.0 21.0 copy-start.22
  377.0 26.2 copy-start.24
  451.8 40.8 copy-start.18
  492.7 45.9 %copy-start.20 = (f32[4,2,2,1024]{3,2,1,0:T(2,128)}, f32[4,2,2,1024]{3,2,1,0:T(2,128)S(1)}, u32[]{:S(2)}) copy-start(f32[4,2,2,1024]{3,2,1,0:T(2,128)S(1)} %fusion.5) | copy-start | bytes 196612
  561.4 4.3 copy-start.31
  561.4 98.2 %all-to-all-start.3 = ((bf16[4,2048,4,128]{3,2,0,1:T(4,128)(2,1)}), bf16[4,2048,4,128]{3,2,0,1:T(4,128)(2,1)}, u32[]{:S(2)}, u32[]{:S(2)}) async-start(bf16[4,2048,4,128]{3,2,0,1:T(4,128)(2,1)} %copy.249), calls=%async_computation.3 | async-start | bytes 16777216 | tf_op jit(solution)/shard_map/all_to_all | solution.py:120
  667.7 60.3 %slice-start.6 = ((s8[9437184]{0:T(1024)(128)(4,1)}), s8[1048576]{0:T(1024)(128)(4,1)S(1)}, s32[]{:S(2)}) async-start(s8[9437184]{0:T(1024)(128)(4,1)} %bitcast.274), calls=%async_computation.14 | async-start | bytes 2097152
  682.2 45.8 %slice-start.7 = ((s8[9437184]{0:T(1024)(128)(4,1)}), s8[4194304]{0:T(1024)(128)(4,1)S(1)}, s32[]{:S(2)}) async-start(s8[9437184]{0:T(1024)(128)(4,1)} %bitcast.274), calls=%async_computation.15 | async-start | bytes 8388608
  682.2 45.8 %slice-start.8 = ((s8[9437184]{0:T(1024)(128)(4,1)}), s8[4194304]{0:T(1024)(128)(4,1)S(1)}, s32[]{:S(2)}) async-start(s8[9437184]{0:T(1024)(128)(4,1)} %bitcast.274), calls=%async_computation.16 | async-start | bytes 8388608
  728.0 17.3 copy-start.3
  821.9 4.2 copy-start.23
  822.0 4.2 copy-start.25
  822.0 4.2 copy-start.19
  822.0 4.2 copy-start.21
  822.0 98.1 %all-to-all-start.4 = ((bf16[4,256,32,128]{3,1,0,2:T(8,128)(2,1)}), bf16[4,256,32,128]{3,1,0,2:T(8,128)(2,1)}, u32[]{:S(2)}, u32[]{:S(2)}) async-start(bf16[4,256,32,128]{3,1,0,2:T(8,128)(2,1)} %bitcast.281), calls=%async_computation.4 | async-start | bytes 16777216 | tf_op jit(solution)/shard_map/all_to_all | solution.py:117
  920.1 8.0 copy-start.2
  1084.2 536.2 %all-to-all-start.7 = ((bf16[4,2048,2,128]{3,2,0,1:T(2,128)(2,1)}), bf16[4,2048,2,128]{3,2,0,1:T(2,128)(2,1)}, u32[]{:S(2)}, u32[]{:S(2)}) async-start(bf16[4,2048,2,128]{3,2,0,1:T(2,128)(2,1)} %copy.277), calls=%async_computation.7 | async-start | bytes 8388608 | tf_op jit(solution)/shard_map/all_to_all | solution.py:120
  1620.3 52.4 %all-to-all-start.6 = ((bf16[4,2048,2,128]{3,2,0,1:T(2,128)(2,1)}), bf16[4,2048,2,128]{3,2,0,1:T(2,128)(2,1)}, u32[]{:S(2)}, u32[]{:S(2)}) async-start(bf16[4,2048,2,128]{3,2,0,1:T(2,128)(2,1)} %copy.268), calls=%async_computation.6 | async-start | bytes 8388608 | tf_op jit(solution)/shard_map/all_to_all | solution.py:120
  1623.7 14.9 copy-start.28
  1623.7 14.9 copy-start.33
  1672.7 112.0 %all-to-all-start.5 = ((bf16[4,2048,4,128]{3,2,0,1:T(4,128)(2,1)}), bf16[4,2048,4,128]{3,2,0,1:T(4,128)(2,1)}, u32[]{:S(2)}, u32[]{:S(2)}) async-start(bf16[4,2048,4,128]{3,2,0,1:T(4,128)(2,1)} %copy.259), calls=%async_computation.5 | async-start | bytes 16777216 | tf_op jit(solution)/shard_map/all_to_all | solution.py:120
  1676.9 12.2 copy-start.9
  1676.9 12.2 copy-start.11
  1689.1 4.9 slice-start.4
  1689.1 4.9 copy-start.15
  1689.1 4.9 copy-start.35
  1689.1 5.9 slice-start.5
  1694.0 5.7 copy-start.17
  1702.3 2.0 copy-start.5
  1730.0 29.0 copy-start.4
  1800.3 14.1 slice-start
  1800.3 14.1 slice-start.1
  1800.3 15.2 slice-start.2
  1800.3 16.4 slice-start.3
  1800.3 16.4 copy-start.7
  1800.3 16.4 copy-start.37
  1816.8 9.7 copy-start.13
  1888.1 54.6 %copy-start.30 = (f32[4,256]{1,0:T(4,128)S(1)}, f32[4,256]{1,0:T(4,128)}, u32[]{:S(2)}) copy-start(f32[4,256]{1,0:T(4,128)} %copy-done.29) | copy-start | bytes 12292
  1942.8 14.8 copy-start.26
  1942.8 14.8 copy-start.38
  1942.8 14.7 copy-start.39
where the time goes:
time: 4580 us; the launch traced here: 4570 us
  blocking collectives  2610 us (57%)
  matrix products  1270 us (28%)
  local copies, waits for them, and re-layouts  247 us (5%)
  other arithmetic  206 us (4%)
  waiting for transfers between devices  205 us (4%)
    psum x1, blocking collectives, device_step(): lax.psum((dw_q, dw_k, dw_v, dw_o, dw_pre, dw_post, dq_norm, dk_norm), 'sp')  2610 us
    dot_general x2, matrix products, attention_bwd(): jnp.einsum('bkgqs,bqkgh->bskh', d_score, q_blk, preferred_element_type=jn...  251 us
    dot_general x2, matrix products, attention_bwd(): jnp.einsum('bkgqs,bskh->bqkgh', d_score, k_pre, preferred_element_type=jn...  248 us
    all_to_all x4, waiting for transfers between devices, to_heads(): return lax.all_to_all(arr, 'sp', 2, 1, tiled=True)  106 us
    all_to_all x4, waiting for transfers between devices, to_tokens(): return lax.all_to_all(arr, 'sp', 1, 2, tiled=True)  99.7 us
  transfers between devices with their start and end apart: 8, of which 4 were waited for; matrix products, arithmetic and copies ran while one was open for 20% of the time, Pallas kernels for 0%

commit v1 on v0

v1 whole, which is shorter than its diff:
```python
import functools
import jax
import jax.numpy as jnp
from jax import lax
from jax.experimental import pallas as pl
from jax.experimental.pallas import tpu as pltpu
from jax.sharding import PartitionSpec as P

EPS = 1e-6
ROPE_BASE = 1000000.0
ROPE_SCALE = 8.0
NEG_BIG = -1e30
LOG2E = 1.4426950408889634
ROWS = 256
CHUNKS = (2, 2)


def rms_scale(x_f32, weight):
    inv_rms = lax.rsqrt(jnp.mean(x_f32 * x_f32, axis=-1, keepdims=True) + EPS)
    return x_f32 * inv_rms * (1.0 + weight)


def pre_norm(x_f32, weight):
    return rms_scale(x_f32, weight).astype(jnp.bfloat16)


def post_norm(proj, weight):
    return rms_scale(proj.astype(jnp.float32), weight)


def rope_tables(positions, head):
    half_dim = head // 2
    inv_freq = ROPE_BASE ** (-jnp.arange(half_dim, dtype=jnp.float32) * 2.0 / head)
    angles = (positions.astype(jnp.float32) / ROPE_SCALE)[:, None] * inv_freq[None, :]
    cosines = jnp.cos(angles)
    sines = jnp.sin(angles)
    return jnp.concatenate([cosines, cosines], axis=-1), jnp.concatenate([-sines, sines], axis=-1)


def dot_nt(a, b):
    return lax.dot_general(a, b, (((1,), (1,)), ((), ())), preferred_element_type=jnp.float32)


def dot_tn(a, b):
    return lax.dot_general(a, b, (((0,), (0,)), ((), ())), preferred_element_type=jnp.float32)


def dot_nn(a, b):
    return lax.dot_general(a, b, (((1,), (0,)), ((), ())), preferred_element_type=jnp.float32)


def rotate(x_bf, weight, cos_t, sin_t):
    normed = rms_scale(x_bf.astype(jnp.float32), weight)
    return (normed * cos_t + pltpu.roll(normed, normed.shape[-1] // 2, 1) * sin_t).astype(jnp.bfloat16)


def rotate_bwd(d_rot, x_bf, weight, cos_t, sin_t):
    d_f32 = d_rot.astype(jnp.float32)
    d_norm = d_f32 * cos_t - pltpu.roll(d_f32, d_f32.shape[-1] // 2, 1) * sin_t
    x = x_bf.astype(jnp.float32)
    inv_rms = lax.rsqrt(jnp.mean(x * x, axis=-1, keepdims=True) + EPS)
    unit = x * inv_rms
    scaled = d_norm * (1.0 + weight)
    dx = (scaled - unit * jnp.mean(scaled * unit, axis=-1, keepdims=True)) * inv_rms
    d_weight = jnp.sum((d_norm * unit).reshape(-1, 8, x.shape[-1]), axis=0)
    return dx.astype(jnp.bfloat16), d_weight


def causal(scores, fill):
    row_ids = lax.broadcasted_iota(jnp.int32, scores.shape, 0)
    col_ids = lax.broadcasted_iota(jnp.int32, scores.shape, 1)
    return jnp.where(row_ids >= col_ids, scores, fill)


def fwd_kernel(group, q_ref, k_ref, v_ref, cos_ref, sin_ref, wq_ref, wk_ref, o_ref, lse_ref, k_rot):
    seq, head = k_rot.shape
    member = lax.rem(pl.program_id(1), group)
    coef = head ** -0.5 * LOG2E
    wq = wq_ref[...]

    @pl.when(member == 0)
    def _():
        for start in range(0, seq, ROWS):
            rows = slice(start, start + ROWS)
            k_rot[rows, :] = rotate(k_ref[0, rows, :], wk_ref[...], cos_ref[rows, :], sin_ref[rows, :])

    for start in range(0, seq, ROWS):
        rows = slice(start, start + ROWS)
        q_rot = rotate(q_ref[0, rows, :], wq, cos_ref[rows, :], sin_ref[rows, :])
        s_diag = causal(dot_nt(q_rot, k_rot[rows, :]), NEG_BIG)
        row_max = jnp.max(s_diag, axis=-1, keepdims=True)
        if start:
            s_off = dot_nt(q_rot, k_rot[:start, :])
            row_max = jnp.maximum(row_max, jnp.max(s_off, axis=-1, keepdims=True))
        e_diag = jnp.exp2((s_diag - row_max) * coef)
        row_sum = jnp.sum(e_diag, axis=-1, keepdims=True)
        if start:
            e_off = jnp.exp2((s_off - row_max) * coef)
            row_sum = row_sum + jnp.sum(e_off, axis=-1, keepdims=True)
        inv_sum = 1.0 / row_sum
        out = dot_nn((e_diag * inv_sum).astype(jnp.bfloat16), v_ref[0, rows, :])
        if start:
            out = out + dot_nn((e_off * inv_sum).astype(jnp.bfloat16), v_ref[0, :start, :])
        o_ref[0, rows, :] = out.astype(jnp.bfloat16)
        lse = jnp.broadcast_to(row_max * coef + jnp.log2(row_sum), (ROWS, head))
        lanes = lax.broadcasted_iota(jnp.int32, (ROWS, head), 1)
        owner = lax.div(lanes, head // group)
        lse_ref[0, 0, rows, :] = jnp.where(owner >= member, lse, lse_ref[0, 0, rows, :])


def bwd_kernel(group, q_ref, k_ref, v_ref, do_ref, lse_ref, cos_ref, sin_ref, wq_ref, wk_ref,
               dq_ref, dk_ref, dv_ref, dwq_ref, dwk_ref, k_rot, dk_acc, dv_acc):
    seq, head = k_rot.shape
    member = lax.rem(pl.program_id(1), group)
    scale = head ** -0.5
    coef = scale * LOG2E
    wq = wq_ref[...]
    wk = wk_ref[...]

    @pl.when(jnp.logical_and(pl.program_id(0) == 0, pl.program_id(1) == 0))
    def _():
        dwq_ref[...] = jnp.zeros_like(dwq_ref)
        dwk_ref[...] = jnp.zeros_like(dwk_ref)

    @pl.when(member == 0)
    def _():
        dk_acc[...] = jnp.zeros_like(dk_acc)
        dv_acc[...] = jnp.zeros_like(dv_acc)
        for start in range(0, seq, ROWS):
            rows = slice(start, start + ROWS)
            k_rot[rows, :] = rotate(k_ref[0, rows, :], wk, cos_ref[rows, :], sin_ref[rows, :])

    for start in range(0, seq, ROWS):
        rows = slice(start, start + ROWS)
        q_raw = q_ref[0, rows, :]
        q_rot = rotate(q_raw, wq, cos_ref[rows, :], sin_ref[rows, :])
        d_out = do_ref[0, rows, :]
        lse_all = lse_ref[0, 0, rows, :]
        lse = lse_all[:, :1]
        for other in range(1, group):
            at = other * (head // group)
            lse = jnp.where(member == other, lse_all[:, at:at + 1], lse)
        p_diag = causal(jnp.exp2(dot_nt(q_rot, k_rot[rows, :]) * coef - lse), 0.0)
        dp_diag = dot_nt(d_out, v_ref[0, rows, :])
        delta = jnp.sum(p_diag * dp_diag, axis=-1, keepdims=True)
        if start:
            p_off = jnp.exp2(dot_nt(q_rot, k_rot[:start, :]) * coef - lse)
            dp_off = dot_nt(d_out, v_ref[0, :start, :])
            delta = delta + jnp.sum(p_off * dp_off, axis=-1, keepdims=True)
        ds_diag = (p_diag * (dp_diag - delta) * scale).astype(jnp.bfloat16)
        dq = dot_nn(ds_diag, k_rot[rows, :])
        dk_acc[rows, :] += dot_tn(ds_diag, q_rot)
        dv_acc[rows, :] += dot_tn(p_diag.astype(jnp.bfloat16), d_out)
        if start:
            ds_off = (p_off * (dp_off - delta) * scale).astype(jnp.bfloat16)
            dq = dq + dot_nn(ds_off, k_rot[:start, :])
            dk_acc[:start, :] += dot_tn(ds_off, q_rot)
            dv_acc[:start, :] += dot_tn(p_off.astype(jnp.bfloat16), d_out)
        dq_ref[0, rows, :], dw = rotate_bwd(dq.astype(jnp.bfloat16), q_raw, wq, cos_ref[rows, :], sin_ref[rows, :])
        dwq_ref[...] += dw

    @pl.when(member == group - 1)
    def _():
        for start in range(0, seq, ROWS):
            rows = slice(start, start + ROWS)
            dk_ref[0, rows, :], dw = rotate_bwd(dk_acc[rows, :].astype(jnp.bfloat16), k_ref[0, rows, :], wk, cos_ref[rows, :], sin_ref[rows, :])
            dwk_ref[...] += dw
            dv_ref[0, rows, :] = dv_acc[rows, :].astype(jnp.bfloat16)


def attention_specs(seq, head, heads, group):
    kv = heads // group
    q_spec = pl.BlockSpec((1, seq, head), lambda b, h: (b, 0, h))
    k_spec = pl.BlockSpec((1, seq, head), lambda b, h: (b, 0, heads + h // group))
    v_spec = pl.BlockSpec((1, seq, head), lambda b, h: (b, 0, heads + kv + h // group))
    kv_spec = pl.BlockSpec((1, seq, head), lambda b, h: (b, 0, h // group))
    lse_spec = pl.BlockSpec((1, 1, seq, head), lambda b, h: (b, h // group, 0, 0))
    tab_spec = pl.BlockSpec((seq, head), lambda b, h: (0, 0))
    w_spec = pl.BlockSpec((1, head), lambda b, h: (0, 0))
    dw_spec = pl.BlockSpec((8, head), lambda b, h: (0, 0))
    return q_spec, k_spec, v_spec, kv_spec, lse_spec, tab_spec, w_spec, dw_spec


def attention_fwd(qkv, cos_t, sin_t, wq, wk, heads, group):
    batch, seq, _ = qkv.shape
    head = cos_t.shape[1]
    q_spec, k_spec, v_spec, _, lse_spec, tab_spec, w_spec, _ = attention_specs(seq, head, heads, group)
    flops = batch * heads * seq * seq * head * 2
    return pl.pallas_call(
        functools.partial(fwd_kernel, group),
        grid=(batch, heads),
        in_specs=[q_spec, k_spec, v_spec, tab_spec, tab_spec, w_spec, w_spec],
        out_specs=[q_spec, lse_spec],
        out_shape=[jax.ShapeDtypeStruct((batch, seq, heads * head), jnp.bfloat16),
                   jax.ShapeDtypeStruct((batch, heads // group, seq, head), jnp.float32)],
        scratch_shapes=[pltpu.VMEM((seq, head), jnp.bfloat16)],
        compiler_params=pltpu.CompilerParams(dimension_semantics=('arbitrary', 'arbitrary'), vmem_limit_bytes=56 * 2 ** 20),
        cost_estimate=pl.CostEstimate(flops=flops, bytes_accessed=batch * seq * 3000, transcendentals=batch * heads * seq * seq // 2),
        name='attention_fwd',
    )(qkv, qkv, qkv, cos_t, sin_t, wq, wk)


def attention_bwd(qkv, d_out, lse, cos_t, sin_t, wq, wk, heads, group):
    batch, seq, _ = qkv.shape
    head = cos_t.shape[1]
    kv = heads // group
    q_spec, k_spec, v_spec, kv_spec, lse_spec, tab_spec, w_spec, dw_spec = attention_specs(seq, head, heads, group)
    flops = batch * heads * seq * seq * head * 5
    return pl.pallas_call(
        functools.partial(bwd_kernel, group),
        grid=(batch, heads),
        in_specs=[q_spec, k_spec, v_spec, q_spec, lse_spec, tab_spec, tab_spec, w_spec, w_spec],
        out_specs=[q_spec, kv_spec, kv_spec, dw_spec, dw_spec],
        out_shape=[jax.ShapeDtypeStruct((batch, seq, heads * head), jnp.bfloat16),
                   jax.ShapeDtypeStruct((batch, seq, kv * head), jnp.bfloat16),
                   jax.ShapeDtypeStruct((batch, seq, kv * head), jnp.bfloat16),
                   jax.ShapeDtypeStruct((8, head), jnp.float32),
                   jax.ShapeDtypeStruct((8, head), jnp.float32)],
        scratch_shapes=[pltpu.VMEM((seq, head), jnp.bfloat16), pltpu.VMEM((seq, head), jnp.float32), pltpu.VMEM((seq, head), jnp.float32)],
        compiler_params=pltpu.CompilerParams(dimension_semantics=('arbitrary', 'arbitrary'), vmem_limit_bytes=56 * 2 ** 20),
        cost_estimate=pl.CostEstimate(flops=flops, bytes_accessed=batch * seq * 6000, transcendentals=batch * heads * seq * seq // 2),
        name='attention_bwd',
    )(qkv, qkv, qkv, d_out, lse, cos_t, sin_t, wq, wk)


def ein(spec, a, b):
    return jnp.einsum(spec, a, b, preferred_element_type=jnp.float32)


def solution(mesh):
    n_dev = mesh.shape['sp']

    def to_tokens(arr):
        return lax.all_to_all(arr, 'sp', 1, 2, tiled=True)

    def gather_tokens(arr):
        return lax.all_gather(arr, 'sp', axis=1, tiled=True)

    def device_step(x_in, dy_in, positions, w_q, w_k, w_v, w_o, w_pre, w_post, q_norm, k_norm):
        head = q_norm.shape[0]
        q_cols = w_q.shape[1] // n_dev
        kv_cols = w_k.shape[1] // n_dev
        heads = q_cols // head
        group = q_cols // kv_cols
        me = lax.axis_index('sp')
        bounds = []
        at = 0
        for size in CHUNKS:
            bounds.append((at, at + size))
            at += size
        parts = range(len(bounds))

        x_f32 = [x_in[lo:hi].astype(jnp.float32) for lo, hi in bounds]
        pre = [jax.vjp(pre_norm, x, w_pre) for x in x_f32]
        normed = [gather_tokens(p[0]) for p in pre]
        cos_t, sin_t = rope_tables(lax.all_gather(positions, 'sp', axis=0, tiled=True), head)
        w_loc = jnp.concatenate([lax.dynamic_slice_in_dim(w_q, me * q_cols, q_cols, 1),
                                 lax.dynamic_slice_in_dim(w_k, me * kv_cols, kv_cols, 1),
                                 lax.dynamic_slice_in_dim(w_v, me * kv_cols, kv_cols, 1)], axis=1)
        wo_loc = lax.dynamic_slice_in_dim(w_o, me * q_cols, q_cols, 0)
        wq_row = q_norm[None, :]
        wk_row = k_norm[None, :]

        qkv, o_loc, lse, y_parts, d_proj, d_proj_all = [], [], [], [], [], []
        dw_post = 0.0
        for c in parts:
            lo, hi = bounds[c]
            qkv.append(ein('bsd,dn->bsn', normed[c], w_loc).astype(jnp.bfloat16))
            o_c, lse_c = attention_fwd(qkv[c], cos_t, sin_t, wq_row, wk_row, heads, group)
            o_loc.append(o_c)
            lse.append(lse_c)
            proj = ein('bsn,nd->bsd', to_tokens(o_c), w_o).astype(jnp.bfloat16)
            post, post_pull = jax.vjp(post_norm, proj, w_post)
            y_parts.append((x_f32[c] + post).astype(jnp.bfloat16))
            d_c, dwp = post_pull(dy_in[lo:hi].astype(jnp.float32))
            dw_post = dw_post + dwp
            d_proj_all.append(gather_tokens(d_c))

        d_qkv, d_tok = [], []
        dq_norm = 0.0
        dk_norm = 0.0
        for c in parts:
            d_o = ein('bsd,nd->bsn', d_proj_all[c], wo_loc).astype(jnp.bfloat16)
            dq, dk, dv, dwq, dwk = attention_bwd(qkv[c], d_o, lse[c], cos_t, sin_t, wq_row, wk_row, heads, group)
            dq_norm = dq_norm + jnp.sum(dwq, axis=0)
            dk_norm = dk_norm + jnp.sum(dwk, axis=0)
            d_qkv.append((dq, dk, dv))
            d_tok.append((to_tokens(dq), to_tokens(dk), to_tokens(dv)))

        dw_o = sum(ein('bsn,bsd->nd', o_loc[c], d_proj_all[c]) for c in parts).astype(jnp.bfloat16)
        dw_o = lax.all_gather(dw_o, 'sp', axis=0, tiled=True)
        dw = []
        for j in range(3):
            local = sum(ein('bsd,bsn->dn', normed[c], d_qkv[c][j]) for c in parts).astype(jnp.bfloat16)
            dw.append(lax.all_gather(local, 'sp', axis=1, tiled=True))

        dx_parts = []
        dw_pre = 0.0
        for c in parts:
            lo, hi = bounds[c]
            dq, dk, dv = d_tok[c]
            d_normed = (ein('bsn,dn->bsd', dq, w_q) + ein('bsn,dn->bsd', dk, w_k) + ein('bsn,dn->bsd', dv, w_v)).astype(jnp.bfloat16)
            dx_norm, dwp = pre[c][1](d_normed)
            dw_pre = dw_pre + dwp
            dx_parts.append((dy_in[lo:hi].astype(jnp.float32) + dx_norm).astype(jnp.bfloat16))

        sums = lax.psum((dw_pre, dw_post, dq_norm, dk_norm), 'sp')
        return (jnp.concatenate(y_parts, axis=0), jnp.concatenate(dx_parts, axis=0), dw[0], dw[1], dw[2], dw_o) + sums

    token_spec = P('dp', 'sp', None)
    return jax.shard_map(device_step, mesh=mesh,
                         in_specs=(token_spec, token_spec, P(('dp', 'sp')), P(None, None), P(None, None), P(None, None), P(None, None), P(None), P(None), P(None), P(None)),
                         out_specs=(token_spec, token_spec, P('dp', None), P('dp', None), P('dp', None), P('dp', None), P('dp'), P('dp'), P('dp'), P('dp')),
                         check_vma=False)
```

time: 4580 us -> 1980 us (0.43)
  blocking collectives: 2610 us -> 37.6 us
  matrix products: 1270 us -> 525 us
  waiting for transfers between devices: 205 us -> 735 us
  Pallas kernels: 0 us -> 320 us
  other arithmetic: 206 us -> 70.6 us
    psum x1, blocking collectives: 2610 us -> 24.1 us  [device_step(): sums = lax.psum((dw_pre, dw_post, dq_norm, dk_norm), 'sp')]
    dot_general x24 -> x20, matrix products: 1270 us -> 525 us  [ein(): return jnp.einsum(spec, a, b, preferred_element_type=jnp.float32)]
    all_gather x0 -> x8, waiting for transfers between devices: none -> 496 us  [the longest x4 464 us: gather_tokens(): return lax.all_gather(arr, 'sp', axis=1, tiled=True)]
    pallas_call x0 -> x4, Pallas kernels: none -> 320 us  [the longest x2 195 us: attention_bwd(): pl.pallas_call(functools.partial(bwd_kernel, group), grid=(batch, heads),...]
    all_to_all x4 -> x8, waiting for transfers between devices: 99.7 us -> 238 us  [to_tokens(): return lax.all_to_all(arr, 'sp', 1, 2, tiled=True)]
    all_to_all x4 -> x0, waiting for transfers between devices: 106 us -> none  [to_heads(): return lax.all_to_all(arr, 'sp', 2, 1, tiled=True)]
    convert_element_type x6 -> x0, local copies, waits for them, and re-layouts: 79.7 us -> none  [the longest x2 29.6 us: norm_rope(): normed = rms_scale(heads_bf.astype(jnp.float32), weight)]
    pallas_call x0 -> x8, local copies, waits for them, and re-layouts: none -> 72.1 us  [the longest x6 51.8 us: attention_bwd(): pl.pallas_call(functools.partial(bwd_kernel, group), grid=(batch, heads),...]
  transfers between devices with their start and end apart: 8 -> 16, of which waited for: 4 -> 12; matrix products, arithmetic and copies ran while one was open for 20% -> 29% of each run, Pallas kernels for 0% -> 11%
where the time goes in v1:
time: 1980 us; the launch traced here: 1970 us
  waiting for transfers between devices  735 us (37%)
  matrix products  525 us (27%)
  Pallas kernels  320 us (16%)
  local copies, waits for them, and re-layouts  238 us (12%)
  other arithmetic  70.6 us (4%)
  blocking collectives  37.6 us (2%)
  starting transfers between devices  26 us (1%)
    dot_general x20, matrix products, ein(): return jnp.einsum(spec, a, b, preferred_element_type=jnp.float32)  525 us
    all_gather x4, waiting for transfers between devices, gather_tokens(): return lax.all_gather(arr, 'sp', axis=1, tiled=True)  464 us
    all_to_all x8, waiting for transfers between devices, to_tokens(): return lax.all_to_all(arr, 'sp', 1, 2, tiled=True)  238 us
    pallas_call x2, Pallas kernels, attention_bwd(): pl.pallas_call(functools.partial(bwd_kernel, group), grid=(batch, heads),...  195 us
    pallas_call x2, Pallas kernels, attention_fwd(): pl.pallas_call(functools.partial(fwd_kernel, group), grid=(batch, heads),...  125 us
    unnamed x74, local copies, waits for them, and re-layouts  78.5 us
    all_to_all x16, local copies, waits for them, and re-layouts, to_tokens(): return lax.all_to_all(arr, 'sp', 1, 2, tiled=True)  77.8 us
    pallas_call x6, local copies, waits for them, and re-layouts, attention_bwd(): pl.pallas_call(functools.partial(bwd_kernel, group), grid=(batch, heads),...  51.8 us
  transfers between devices with their start and end apart: 16, of which 12 were waited for; matrix products, arithmetic and copies ran while one was open for 29% of the time, Pallas kernels for 11%

profile of v1, /device:TPU:0, one launch (start us, length us, event | category | flops | bytes accessed | tf_op | source)
XLA Modules:
  0.0 1967.6 jit_solution(3791023184033389316)
XLA Ops:
  7.2 4.9 fusion.38
  13.7 5.2 fusion.25
  19.8 13.5 all-gather
  50.2 144.9 %all-gather.10.cloned.1.call-done = bf16[2,2048,4608]{2,1,0:T(8,128)(2,1)} async-done(((bf16[2,256,4608]{2,1,0:T(8,128)(2,1)}), bf16[2,2048,4608]{2,1,0:T(8,128)(2,1)}) %all-gather.10.cloned.1.call-update) | async-done | bytes 37748752 | tf_op jit(solution)/shard_map/all_gather | solution.py:237
  195.2 47.1 %convolution_convert_fusion.1.q_ref.k_ref.v_ref = bf16[2,2048,1024]{2,1,0:T(8,128)(2,1)} fusion(bf16[2,2048,4608]{2,1,0:T(8,128)(2,1)} %all-gather.10.cloned.1.call-done, bf16[4608,256]{1,0:T(8,128)(2,1)} %constant_dynamic-slice_fusion, bf16[4608,256]{1,0:T(8,128)(2,1)S(1)} %constant_dynamic-slice_fusion.1, bf16[4608,512]{1,0:T(8,128)(2,1)} %constant_dynamic-slice_fusion.2), kind=kOutput, calls=%fused_computation.96 | convolution fusion | flops 38687211520 | bytes 55574528 | tf_op jit(solution)/shard_map/bsd,dn->bsn/dot_general | solution.py:227
  242.2 62.3 %attention_fwd.2 = (bf16[2,2048,512]{2,1,0:T(8,128)(2,1)}, f32[2,2,2048,128]{3,2,1,0:T(8,128)}) custom-call(bf16[2,2048,1024]{2,1,0:T(8,128)(2,1)} %convolution_convert_fusion.1.q_ref.k_ref.v_ref, bf16[2,2048,1024]{2,1,0:T(8,128)(2,1)} %convolution_convert_fusion.1.q_ref.k_ref.v_ref, bf16[2,2048,1024]{2,1,0:T(8,128)(2,1)} %convolution_convert_fusion.1.q_ref.k_ref.v_ref, ...), custom_call_target="tpu_custom_call" | custom-call | flops 8589934592 | bytes 12288000 | tf_op jit(solution)/shard_map/attention_fwd/pallas_call | solution.py:189
  304.6 10.1 copy.37
  318.5 96.8 %all-gather.12.cloned.1.call-done = bf16[2,2048,4608]{2,1,0:T(8,128)(2,1)} async-done(((bf16[2,256,4608]{2,1,0:T(8,128)(2,1)}), bf16[2,2048,4608]{2,1,0:T(8,128)(2,1)}) %all-gather.12.cloned.1.call-update) | async-done | bytes 37748752 | tf_op jit(solution)/shard_map/all_gather | solution.py:237
  415.3 46.7 %convolution_convert_fusion.q_ref.k_ref.v_ref = bf16[2,2048,1024]{2,1,0:T(8,128)(2,1)} fusion(bf16[2,2048,4608]{2,1,0:T(8,128)(2,1)} %all-gather.12.cloned.1.call-done, bf16[4608,256]{1,0:T(8,128)(2,1)} %constant_dynamic-slice_fusion, bf16[4608,256]{1,0:T(8,128)(2,1)S(1)} %constant_dynamic-slice_fusion.1, bf16[4608,512]{1,0:T(8,128)(2,1)} %constant_dynamic-slice_fusion.2), kind=kOutput, calls=%fused_computation.95 | convolution fusion | flops 38687211520 | bytes 55574528 | tf_op jit(solution)/shard_map/bsd,dn->bsn/dot_general | solution.py:227
  461.9 62.4 %attention_fwd.3 = (bf16[2,2048,512]{2,1,0:T(8,128)(2,1)}, f32[2,2,2048,128]{3,2,1,0:T(8,128)}) custom-call(bf16[2,2048,1024]{2,1,0:T(8,128)(2,1)} %convolution_convert_fusion.q_ref.k_ref.v_ref, bf16[2,2048,1024]{2,1,0:T(8,128)(2,1)} %convolution_convert_fusion.q_ref.k_ref.v_ref, bf16[2,2048,1024]{2,1,0:T(8,128)(2,1)} %convolution_convert_fusion.q_ref.k_ref.v_ref, ...), custom_call_target="tpu_custom_call" | custom-call | flops 8589934592 | bytes 12288000 | tf_op jit(solution)/shard_map/attention_fwd/pallas_call | solution.py:189
  524.3 10.3 copy.39
  537.9 6.5 copy.80
  544.4 7.4 all_to_all.107
  551.8 27.0 %fusion.34 = (f32[2,256]{1,0:T(2,128)S(1)}, bf16[2,256,4608]{2,1,0:T(8,128)(2,1)}) fusion(bf16[2,256,4096]{2,1,0:T(8,128)(2,1)} %all_to_all.107, bf16[4096,4608]{1,0:T(8,128)(2,1)} %param.17), kind=kOutput, calls=%fused_computation.66 | convolution fusion | flops 19336790016 | bytes 46663680 | tf_op jit(solution)/shard_map/bsn,nd->bsd/dot_general | solution.py:227
  578.9 8.0 all-to-all-done.1
  586.9 6.5 copy.79
  593.4 7.5 all_to_all.111
  600.9 27.2 %fusion.36 = (f32[2,256]{1,0:T(2,128)S(1)}, bf16[2,256,4608]{2,1,0:T(8,128)(2,1)}) fusion(bf16[2,256,4096]{2,1,0:T(8,128)(2,1)} %all_to_all.111, bf16[4096,4608]{1,0:T(8,128)(2,1)} %param.17), kind=kOutput, calls=%fused_computation.68 | convolution fusion | flops 19336790016 | bytes 46663680 | tf_op jit(solution)/shard_map/bsn,nd->bsd/dot_general | solution.py:227
  628.1 13.0 fusion.29
  641.2 15.2 fusion.39
  657.0 171.8 %all-gather.16.cloned.1.call-done = bf16[2,2048,4608]{2,1,0:T(8,128)(2,1)} async-done(((bf16[2,256,4608]{2,1,0:T(8,128)(2,1)}), bf16[2,2048,4608]{2,1,0:T(8,128)(2,1)}) %all-gather.16.cloned.1.call-update) | async-done | bytes 37748752 | tf_op jit(solution)/shard_map/all_gather | solution.py:237
  828.8 27.5 %fusion.69.do_ref = bf16[2,2048,512]{2,1,0:T(8,128)(2,1)} fusion(bf16[2,2048,4608]{2,1,0:T(8,128)(2,1)} %all-gather.16.cloned.1.call-done, bf16[4096,4608]{1,0:T(8,128)(2,1)} %param.17, s32[]{:T(128)S(6)} %select_n.8), kind=kOutput, calls=%fused_computation.108 | convolution fusion | flops 19329449984 | bytes 46661636 | tf_op jit(solution)/shard_map/bsd,nd->bsn/dot_general | solution.py:227
  856.3 97.9 %attention_bwd.3 = (bf16[2,2048,512]{2,1,0:T(8,128)(2,1)}, bf16[2,2048,256]{2,1,0:T(8,128)(2,1)}, bf16[2,2048,256]{2,1,0:T(8,128)(2,1)}, f32[8,128]{1,0:T(8,128)}, f32[8,128]{1,0:T(8,128)}) custom-call(bf16[2,2048,1024]{2,1,0:T(8,128)(2,1)} %convolution_convert_fusion.q_ref.k_ref.v_ref, bf16[2,2048,1024]{2,1,0:T(8,128)(2,1)} %convolution_convert_fusion.q_ref.k_ref.v_ref, ...), custom_call_target="tpu_custom_call" | custom-call | flops 21474836480 | bytes 24576000 | tf_op jit(solution)/shard_map/attention_bwd/pallas_call | solution.py:209
  954.2 50.1 %all-gather.14.cloned.1.call-done = bf16[2,2048,4608]{2,1,0:T(8,128)(2,1)} async-done(((bf16[2,256,4608]{2,1,0:T(8,128)(2,1)}), bf16[2,2048,4608]{2,1,0:T(8,128)(2,1)}) %all-gather.14.cloned.1.call-update) | async-done | bytes 37748752 | tf_op jit(solution)/shard_map/all_gather | solution.py:237
  1004.3 27.8 %fusion.66.do_ref = bf16[2,2048,512]{2,1,0:T(8,128)(2,1)} fusion(bf16[2,2048,4608]{2,1,0:T(8,128)(2,1)} %all-gather.14.cloned.1.call-done, bf16[4096,4608]{1,0:T(8,128)(2,1)} %param.17, s32[]{:T(128)S(6)} %select_n.8), kind=kOutput, calls=%fused_computation.107 | convolution fusion | flops 19329449984 | bytes 46661636 | tf_op jit(solution)/shard_map/bsd,nd->bsn/dot_general | solution.py:227
  1032.0 97.6 %attention_bwd.2 = (bf16[2,2048,512]{2,1,0:T(8,128)(2,1)}, bf16[2,2048,256]{2,1,0:T(8,128)(2,1)}, bf16[2,2048,256]{2,1,0:T(8,128)(2,1)}, f32[8,128]{1,0:T(8,128)}, f32[8,128]{1,0:T(8,128)}) custom-call(bf16[2,2048,1024]{2,1,0:T(8,128)(2,1)} %convolution_convert_fusion.1.q_ref.k_ref.v_ref, bf16[2,2048,1024]{2,1,0:T(8,128)(2,1)} %convolution_convert_fusion.1.q_ref.k_ref.v_ref, ...), custom_call_target="tpu_custom_call" | custom-call | flops 21474836480 | bytes 24576000 | tf_op jit(solution)/shard_map/attention_bwd/pallas_call | solution.py:209
  1129.7 19.2 convolution_bitcast_fusion.1
  1148.9 18.9 fusion.59
  1167.9 19.3 convolution_bitcast_fusion.3
  1187.2 18.9 fusion.58
  1206.1 28.3 %fusion.82 = f32[512,4608,1]{1,0,2:T(8,128)} fusion(bf16[2,2048,512]{2,1,0:T(8,128)(2,1)} %get-tuple-element.24, bf16[2,2048,4608]{2,1,0:T(8,128)(2,1)} %all-gather.14.cloned.1.call-done), kind=kOutput, calls=%fused_computation.142 | convolution fusion | flops 19327352832 | bytes 51380224 | tf_op jit(solution)/shard_map/bsn,bsd->nd/dot_general | solution.py:227
  1234.5 27.4 %fusion.44 = bf16[512,4608]{1,0:T(8,128)(2,1)} fusion(f32[512,4608,1]{1,0,2:T(8,128)} %fusion.82, bf16[2,2048,512]{2,1,0:T(8,128)(2,1)S(1)} %copy-done.3, bf16[2,2048,4608]{2,1,0:T(8,128)(2,1)} %all-gather.16.cloned.1.call-done), kind=kOutput, calls=%fused_computation.80 | convolution fusion | flops 19332071424 | bytes 56098816 | tf_op jit(solution)/shard_map/bsn,bsd->nd/dot_general | solution.py:227
  1261.9 28.0 %fusion.81 = f32[4608,512,1]{1,0,2:T(8,128)} fusion(bf16[2,2048,4608]{2,1,0:T(8,128)(2,1)} %all-gather.10.cloned.1.call-done, bf16[2,2048,512]{2,1,0:T(8,128)(2,1)} %get-tuple-element.27), kind=kOutput, calls=%fused_computation.141 | convolution fusion | flops 19327352832 | bytes 51380224 | tf_op jit(solution)/shard_map/bsd,bsn->dn/dot_general | solution.py:227
  1289.9 27.0 %fusion.45 = bf16[4608,512]{1,0:T(8,128)(2,1)} fusion(f32[4608,512,1]{1,0,2:T(8,128)} %fusion.81, bf16[2,2048,4608]{2,1,0:T(8,128)(2,1)} %all-gather.12.cloned.1.call-done, bf16[2,2048,512]{2,1,0:T(8,128)(2,1)S(1)} %copy-done.4), kind=kOutput, calls=%fused_computation.82 | convolution fusion | flops 19332071424 | bytes 56098816 | tf_op jit(solution)/shard_map/bsd,bsn->dn/dot_general | solution.py:227
  1317.0 14.2 copy.49
  1333.6 5.8 copy.51
  1339.4 40.8 %all-to-all-done.6 = bf16[2,2048,256]{2,0,1:T(2,128)(2,1)S(1)} async-done(((bf16[2,2048,256]{2,0,1:T(2,128)(2,1)}), bf16[2,2048,256]{2,0,1:T(2,128)(2,1)S(1)}, u32[]{:S(2)}, u32[]{:S(2)}) %all-to-all-start.6) | async-done | bytes 2097184 | tf_op jit(solution)/shard_map/all_to_all | solution.py:234
  1383.3 5.8 copy.43
  1389.1 28.3 %all-to-all-done.7 = bf16[2,2048,256]{2,0,1:T(2,128)(2,1)} async-done(((bf16[2,2048,256]{2,0,1:T(2,128)(2,1)}), bf16[2,2048,256]{2,0,1:T(2,128)(2,1)}, u32[]{:S(2)}, u32[]{:S(2)}) %all-to-all-start.7) | async-done | bytes 2097184 | tf_op jit(solution)/shard_map/all_to_all | solution.py:234
  1420.5 5.8 copy.45
  1426.2 43.3 %all-to-all-done.3 = bf16[2,2048,256]{2,0,1:T(2,128)(2,1)} async-done(((bf16[2,2048,256]{2,0,1:T(2,128)(2,1)}), bf16[2,2048,256]{2,0,1:T(2,128)(2,1)}, u32[]{:S(2)}, u32[]{:S(2)}) %all-to-all-start.3) | async-done | bytes 2097184 | tf_op jit(solution)/shard_map/all_to_all | solution.py:234
  1472.7 10.1 copy.41
  1482.8 27.7 %all-to-all-done.4 = bf16[2,2048,256]{2,0,1:T(2,128)(2,1)} async-done(((bf16[2,2048,256]{2,0,1:T(2,128)(2,1)}), bf16[2,2048,256]{2,0,1:T(2,128)(2,1)}, u32[]{:S(2)}, u32[]{:S(2)}) %all-to-all-start.4) | async-done | bytes 2097184 | tf_op jit(solution)/shard_map/all_to_all | solution.py:234
  1513.8 10.1 copy.47
  1523.9 84.0 %all-to-all-done.2 = bf16[2,2048,512]{2,0,1:T(2,128)(2,1)} async-done(((bf16[2,2048,512]{2,0,1:T(2,128)(2,1)}), bf16[2,2048,512]{2,0,1:T(2,128)(2,1)}, u32[]{:S(2)}, u32[]{:S(2)}) %all-to-all-start.2) | async-done | bytes 4194336 | tf_op jit(solution)/shard_map/all_to_all | solution.py:234
  1611.6 7.7 pad_maximum_fusion
  1643.2 16.8 fusion.10
  1660.0 16.3 fusion.8
  1676.2 6.5 copy.78
  1682.8 7.4 all_to_all.115
  1690.1 6.1 all-to-all-done.5
  1696.2 6.5 copy.77
  1702.8 7.4 all_to_all.127
  1710.1 27.7 %fusion = f32[2,256,4608]{2,1,0:T(8,128)} fusion(bf16[2,256,4096]{2,1,0:T(8,128)(2,1)} %all_to_all.127, bf16[4608,4096]{1,0:T(8,128)(2,1)} %param.14), kind=kOutput, calls=%fused_computation | convolution fusion | flops 19327352832 | bytes 51380224 | tf_op jit(solution)/shard_map/bsn,dn->bsd/dot_general | solution.py:227
  1737.9 27.5 %fusion.2 = f32[2,256,4608]{2,1,0:T(8,128)} fusion(bf16[2,256,4096]{2,1,0:T(8,128)(2,1)} %all_to_all.115, bf16[4608,4096]{1,0:T(8,128)(2,1)} %param.14), kind=kOutput, calls=%fused_computation.2 | convolution fusion | flops 19327352832 | bytes 51380224 | tf_op jit(solution)/shard_map/bsn,dn->bsd/dot_general | solution.py:227
  1765.4 20.3 %add_convert_fusion = bf16[2,256,4608]{2,1,0:T(8,128)(2,1)} fusion(f32[2,256,4608]{2,1,0:T(8,128)} %fusion.8, f32[2,256,4608]{2,1,0:T(8,128)} %fusion, bf16[2,256,2048]{2,1,0:T(8,128)(2,1)} %all_to_all.131, bf16[4608,2048]{1,0:T(8,128)(2,1)} %param.15), kind=kOutput, calls=%fused_computation.83 | convolution fusion | flops 9670754304 | bytes 44564480 | tf_op jit(solution)/shard_map/bsn,dn->bsd/dot_general | solution.py:227
  1785.8 25.7 %fusion.26 = (f32[4608]{0:T(1024)S(1)}, f32[2,256]{1,0:T(2,128)S(1)}, f32[2,256]{1,0:T(2,128)S(1)}, f32[4608]{0:T(1024)S(1)}, bf16[2,256,4608]{2,1,0:T(8,128)(2,1)}) fusion(f32[2,256]{1,0:T(2,128)S(1)} %copy-done.18, bf16[4,256,4608]{2,1,0:T(8,128)(2,1)} %param.11, f32[4608]{0:T(1024)S(1)} %copy-done.10, bf16[2,256,4608]{2,1,0:T(8,128)(2,1)} %add_convert_fusion, ...), kind=kOutput, calls=%fused_computation.58 | convolution fusion | flops 9708494848 | bytes 58783744 | tf_op jit(solution)/shard_map/bsn,dn->bsd/dot_general | solution.py:227
  1811.5 24.1 %all-reduce = (f32[4608]{0:T(1024)}, f32[4608]{0:T(1024)}, f32[128]{0:T(128)}, f32[128]{0:T(128)}) all-reduce(f32[4608]{0:T(1024)S(1)} %add.132, f32[4608]{0:T(1024)S(1)} %copy-done.14, f32[128]{0:T(128)S(1)} %copy-done.30, f32[128]{0:T(128)S(1)} %copy-done.31), channel_id=1, replica_groups=mesh['dp'=1,'sp'=8] {'sp'}, use_global_device_ids=true, to_apply=%region_10.0 | all-reduce | flops 9472 | bytes 75776 | tf_op jit(solution)/shard_map/psum | solution.py:307
  1835.6 11.6 fusion.28
  1851.3 32.1 %all-gather.18.cloned.1.call-done = bf16[4608,4096]{1,0:T(8,128)(2,1)} async-done(((bf16[4608,512]{1,0:T(8,128)(2,1)}), bf16[4608,4096]{1,0:T(8,128)(2,1)}) %all-gather.18.cloned.1.call-update) | async-done | bytes 37748752 | tf_op jit(solution)/shard_map/all_gather | solution.py:295
  1883.4 25.6 %copy.89 = bf16[4608,4096]{1,0:T(8,128)(2,1)} copy(bf16[4608,4096]{1,0:T(8,128)(2,1)} %all-gather.18.cloned.1.call-done) | data formatting | bytes 75497472
  1909.0 17.9 copy.90
  1927.8 6.8 copy.91
  1934.7 25.6 %copy.92 = bf16[4096,4608]{1,0:T(8,128)(2,1)} copy(bf16[4096,4608]{1,0:T(8,128)(2,1)} %all-gather.24.cloned.1.call-done) | data formatting | bytes 75497472
  (133 shorter events, 74.7 us)
Async XLA Ops:
  7.2 5.6 copy-start.15
  7.2 188.0 %all-gather.10.cloned.1.call-start = ((), (), s32[]{:S(2)}) async-start(), calls=%async_computation.8 | async-start | bytes 42467328 | tf_op jit(solution)/shard_map/all_gather | solution.py:237
  7.2 6.5 copy-start
  12.2 0.6 copy-start.21
  12.2 0.6 copy-start.23
  12.2 6.8 copy-start.17
  12.8 6.2 copy-start.19
  13.7 5.3 copy-start.9
  18.9 0.8 copy-start.29
  19.0 14.4 copy-start.16
  19.0 396.3 %all-gather.12.cloned.1.call-start = ((), (), s32[]{:S(2)}) async-start(), calls=%async_computation.9 | async-start | bytes 42467328 | tf_op jit(solution)/shard_map/all_gather | solution.py:237
  314.7 219.9 %all-to-all-start = ((bf16[2,2048,512]{2,0,1:T(2,128)(2,1)}), bf16[2,2048,512]{2,0,1:T(2,128)(2,1)}, u32[]{:S(2)}, u32[]{:S(2)}) async-start(bf16[2,2048,512]{2,0,1:T(2,128)(2,1)} %copy.37), calls=%async_computation | async-start | bytes 8388608 | tf_op jit(solution)/shard_map/all_to_all | solution.py:234
  534.5 52.3 %all-to-all-start.1 = ((bf16[2,2048,512]{2,0,1:T(2,128)(2,1)}), bf16[2,2048,512]{2,0,1:T(2,128)(2,1)}, u32[]{:S(2)}, u32[]{:S(2)}) async-start(bf16[2,2048,512]{2,0,1:T(2,128)(2,1)} %copy.39), calls=%async_computation.1 | async-start | bytes 8388608 | tf_op jit(solution)/shard_map/all_to_all | solution.py:234
  537.9 290.9 %all-gather.16.cloned.1.call-start = ((), (), s32[]{:S(2)}) async-start(), calls=%async_computation.11 | async-start | bytes 42467328 | tf_op jit(solution)/shard_map/all_gather | solution.py:237
  593.4 47.7 %slice-start = ((s8[9437184]{0:T(1024)(128)(4,1)}), s8[1048576]{0:T(1024)(128)(4,1)S(1)}, s32[]{:S(2)}) async-start(s8[9437184]{0:T(1024)(128)(4,1)} %bitcast.158), calls=%async_computation.16 | async-start | bytes 2097152
  600.9 27.2 %copy-start.11 = (f32[4608]{0:T(1024)S(1)}, f32[4608]{0:T(1024)}, u32[]{:S(2)}) copy-start(f32[4608]{0:T(1024)} %broadcast_add_fusion) | copy-start | bytes 55300
  600.9 40.3 %slice-start.1 = ((s8[9437184]{0:T(1024)(128)(4,1)}), s8[4194304]{0:T(1024)(128)(4,1)S(1)}, s32[]{:S(2)}) async-start(s8[9437184]{0:T(1024)(128)(4,1)} %bitcast.158), calls=%async_computation.17 | async-start | bytes 8388608
  600.9 40.3 %slice-start.2 = ((s8[9437184]{0:T(1024)(128)(4,1)}), s8[4194304]{0:T(1024)(128)(4,1)S(1)}, s32[]{:S(2)}) async-start(s8[9437184]{0:T(1024)(128)(4,1)} %bitcast.158), calls=%async_computation.18 | async-start | bytes 8388608
  628.1 13.1 copy-start.1
  656.4 347.9 %all-gather.14.cloned.1.call-start = ((), (), s32[]{:S(2)}) async-start(), calls=%async_computation.10 | async-start | bytes 42467328 | tf_op jit(solution)/shard_map/all_gather | solution.py:237
  657.0 1194.3 %all-gather.22.cloned.1.call-start = ((), (), s32[]{:S(2)}) async-start(), calls=%async_computation.14 | async-start | bytes 21233664 | tf_op jit(solution)/shard_map/all_gather | solution.py:295
  1129.7 19.3 copy-start.5
  1167.8 683.5 %all-gather.20.cloned.1.call-start = ((), (), s32[]{:S(2)}) async-start(), calls=%async_computation.13 | async-start | bytes 21233664 | tf_op jit(solution)/shard_map/all_gather | solution.py:295
  1167.9 19.3 copy-start.6
  1206.1 645.2 %all-gather.24.cloned.1.call-start = ((), (), s32[]{:S(2)}) async-start(), calls=%async_computation.15 | async-start | bytes 42467328 | tf_op jit(solution)/shard_map/all_gather | solution.py:291
  1206.1 28.3 %copy-start.3 = (bf16[2,2048,512]{2,1,0:T(8,128)(2,1)S(1)}, bf16[2,2048,512]{2,1,0:T(8,128)(2,1)}, u32[]{:S(2)}) copy-start(bf16[2,2048,512]{2,1,0:T(8,128)(2,1)} %get-tuple-element.25) | copy-start | bytes 12582916
  1261.9 621.5 %all-gather.18.cloned.1.call-start = ((), (), s32[]{:S(2)}) async-start(), calls=%async_computation.12 | async-start | bytes 42467328 | tf_op jit(solution)/shard_map/all_gather | solution.py:295
  1261.9 28.0 %copy-start.4 = (bf16[2,2048,512]{2,1,0:T(8,128)(2,1)S(1)}, bf16[2,2048,512]{2,1,0:T(8,128)(2,1)}, u32[]{:S(2)}) copy-start(bf16[2,2048,512]{2,1,0:T(8,128)(2,1)} %get-tuple-element.31) | copy-start | bytes 12582916
  1331.2 49.0 %all-to-all-start.6 = ((bf16[2,2048,256]{2,0,1:T(2,128)(2,1)}), bf16[2,2048,256]{2,0,1:T(2,128)(2,1)S(1)}, u32[]{:S(2)}, u32[]{:S(2)}) async-start(bf16[2,2048,256]{2,0,1:T(2,128)(2,1)} %copy.49), calls=%async_computation.6 | async-start | bytes 4194304 | tf_op jit(solution)/shard_map/all_to_all | solution.py:234
  1380.2 37.2 %all-to-all-start.7 = ((bf16[2,2048,256]{2,0,1:T(2,128)(2,1)}), bf16[2,2048,256]{2,0,1:T(2,128)(2,1)}, u32[]{:S(2)}, u32[]{:S(2)}) async-start(bf16[2,2048,256]{2,0,1:T(2,128)(2,1)} %copy.51), calls=%async_computation.7 | async-start | bytes 4194304 | tf_op jit(solution)/shard_map/all_to_all | solution.py:234
  1417.4 52.2 %all-to-all-start.3 = ((bf16[2,2048,256]{2,0,1:T(2,128)(2,1)}), bf16[2,2048,256]{2,0,1:T(2,128)(2,1)}, u32[]{:S(2)}, u32[]{:S(2)}) async-start(bf16[2,2048,256]{2,0,1:T(2,128)(2,1)} %copy.43), calls=%async_computation.3 | async-start | bytes 4194304 | tf_op jit(solution)/shard_map/all_to_all | solution.py:234
  1469.6 40.9 %all-to-all-start.4 = ((bf16[2,2048,256]{2,0,1:T(2,128)(2,1)}), bf16[2,2048,256]{2,0,1:T(2,128)(2,1)}, u32[]{:S(2)}, u32[]{:S(2)}) async-start(bf16[2,2048,256]{2,0,1:T(2,128)(2,1)} %copy.45), calls=%async_computation.4 | async-start | bytes 4194304 | tf_op jit(solution)/shard_map/all_to_all | solution.py:234
  1510.5 97.3 %all-to-all-start.2 = ((bf16[2,2048,512]{2,0,1:T(2,128)(2,1)}), bf16[2,2048,512]{2,0,1:T(2,128)(2,1)}, u32[]{:S(2)}, u32[]{:S(2)}) async-start(bf16[2,2048,512]{2,0,1:T(2,128)(2,1)} %copy.41), calls=%async_computation.2 | async-start | bytes 8388608 | tf_op jit(solution)/shard_map/all_to_all | solution.py:234
  1607.8 88.4 %all-to-all-start.5 = ((bf16[2,2048,512]{2,0,1:T(2,128)(2,1)}), bf16[2,2048,512]{2,0,1:T(2,128)(2,1)}, u32[]{:S(2)}, u32[]{:S(2)}) async-start(bf16[2,2048,512]{2,0,1:T(2,128)(2,1)} %copy.47), calls=%async_computation.5 | async-start | bytes 8388608 | tf_op jit(solution)/shard_map/all_to_all | solution.py:234
  1611.5 7.8 copy-start.12
  1611.5 7.8 copy-start.13
  1611.6 8.4 copy-start.28
  1611.6 8.4 copy-start.26
  1611.6 8.4 copy-start.25
  1611.6 8.4 copy-start.27
  1643.2 16.8 copy-start.8
  1765.4 20.4 %copy-start.7 = (bf16[2,256,2048]{2,1,0:T(8,128)(2,1)S(1)}, bf16[2,256,2048]{2,1,0:T(8,128)(2,1)}, u32[]{:S(2)}) copy-start(bf16[2,256,2048]{2,1,0:T(8,128)(2,1)} %all_to_all.119) | copy-start | bytes 6291460
  1765.4 20.4 %copy-start.10 = (f32[4608]{0:T(1024)S(1)}, f32[4608]{0:T(1024)}, u32[]{:S(2)}) copy-start(f32[4608]{0:T(1024)} %copy-done.9) | copy-start | bytes 55300
  1765.4 20.4 %copy-start.18 = (f32[2,256]{1,0:T(2,128)S(1)}, f32[2,256]{1,0:T(2,128)}, u32[]{:S(2)}) copy-start(f32[2,256]{1,0:T(2,128)} %copy-done.17) | copy-start | bytes 6148
  1765.4 20.4 %copy-start.20 = (f32[2,256]{1,0:T(2,128)S(1)}, f32[2,256]{1,0:T(2,128)}, u32[]{:S(2)}) copy-start(f32[2,256]{1,0:T(2,128)} %copy-done.19) | copy-start | bytes 6148
  1785.8 25.8 %copy-start.14 = (f32[4608]{0:T(1024)S(1)}, f32[4608]{0:T(1024)}, u32[]{:S(2)}) copy-start(f32[4608]{0:T(1024)} %add.133) | copy-start | bytes 55300
  1785.8 25.8 %copy-start.30 = (f32[128]{0:T(128)S(1)}, f32[128]{0:T(128)}, u32[]{:S(2)}) copy-start(f32[128]{0:T(128)} %add.134) | copy-start | bytes 1540
  1785.8 25.8 %copy-start.31 = (f32[128]{0:T(128)S(1)}, f32[128]{0:T(128)}, u32[]{:S(2)}) copy-start(f32[128]{0:T(128)} %add.135) | copy-start | bytes 1540
  1785.8 49.8 %copy-start.22 = (f32[2,256]{1,0:T(2,128)S(1)}, f32[2,256]{1,0:T(2,128)}, u32[]{:S(2)}) copy-start(f32[2,256]{1,0:T(2,128)} %copy-done.21) | copy-start | bytes 6148
  1785.8 49.8 %copy-start.24 = (f32[2,256]{1,0:T(2,128)S(1)}, f32[2,256]{1,0:T(2,128)}, u32[]{:S(2)}) copy-start(f32[2,256]{1,0:T(2,128)} %copy-done.23) | copy-start | bytes 6148
  1909.0 18.9 copy-start.2
Sparse Core Ops, SparseCore 0:
  19.1 175.9 all-gather.9
  197.6 217.6 all-gather.11
  656.5 172.2 all-gather.15
  831.1 173.1 all-gather.13
  1167.9 96.7 all-gather.21
  1266.3 115.8 all-gather.19
  1384.0 304.8 all-gather.23
  1690.8 192.5 all-gather.17

commit v2 on v1

v2 whole, which is shorter than its diff:
```python
import functools
import jax
import jax.numpy as jnp
from jax import lax
from jax.experimental import pallas as pl
from jax.experimental.pallas import tpu as pltpu
from jax.sharding import PartitionSpec as P

EPS = 1e-6
ROPE_BASE = 1000000.0
ROPE_SCALE = 8.0
NEG_BIG = -1e30
LOG2E = 1.4426950408889634
CHUNKS = (2, 1, 1)


def rms_scale(x_f32, weight):
    inv_rms = lax.rsqrt(jnp.mean(x_f32 * x_f32, axis=-1, keepdims=True) + EPS)
    return x_f32 * inv_rms * (1.0 + weight)


def pre_norm(x_f32, weight):
    return rms_scale(x_f32, weight).astype(jnp.bfloat16)


def post_norm(proj, weight):
    return rms_scale(proj.astype(jnp.float32), weight)


def rope_tables(positions, head):
    half_dim = head // 2
    inv_freq = ROPE_BASE ** (-jnp.arange(half_dim, dtype=jnp.float32) * 2.0 / head)
    angles = (positions.astype(jnp.float32) / ROPE_SCALE)[:, None] * inv_freq[None, :]
    cosines = jnp.cos(angles)
    sines = jnp.sin(angles)
    return jnp.concatenate([cosines, cosines], axis=-1), jnp.concatenate([-sines, sines], axis=-1)


def dot_nt(a, b):
    return lax.dot_general(a, b, (((1,), (1,)), ((), ())), preferred_element_type=jnp.float32)


def dot_tn(a, b):
    return lax.dot_general(a, b, (((0,), (0,)), ((), ())), preferred_element_type=jnp.float32)


def dot_nn(a, b):
    return lax.dot_general(a, b, (((1,), (0,)), ((), ())), preferred_element_type=jnp.float32)


def rotate(x_bf, weight, cos_t, sin_t):
    normed = rms_scale(x_bf.astype(jnp.float32), weight)
    return (normed * cos_t + pltpu.roll(normed, normed.shape[-1] // 2, 1) * sin_t).astype(jnp.bfloat16)


def rotate_bwd(d_rot, x_bf, weight, cos_t, sin_t):
    d_f32 = d_rot.astype(jnp.float32)
    d_norm = d_f32 * cos_t - pltpu.roll(d_f32, d_f32.shape[-1] // 2, 1) * sin_t
    x = x_bf.astype(jnp.float32)
    inv_rms = lax.rsqrt(jnp.mean(x * x, axis=-1, keepdims=True) + EPS)
    unit = x * inv_rms
    scaled = d_norm * (1.0 + weight)
    dx = (scaled - unit * jnp.mean(scaled * unit, axis=-1, keepdims=True)) * inv_rms
    d_weight = jnp.sum((d_norm * unit).reshape(-1, 8, x.shape[-1]), axis=0)
    return dx.astype(jnp.bfloat16), d_weight


def causal(scores, fill):
    row_ids = lax.broadcasted_iota(jnp.int32, scores.shape, 0)
    col_ids = lax.broadcasted_iota(jnp.int32, scores.shape, 1)
    return jnp.where(row_ids >= col_ids, scores, fill)


def prefix(ref, count):
    block = ref[:count, 0]
    return block.reshape(count * block.shape[1], block.shape[2])


def fwd_kernel(group, q_ref, k_ref, v_ref, cos_ref, sin_ref, wq_ref, wk_ref, o_ref, lse_ref, k_rot):
    n_blk, _, rows, head = q_ref.shape
    member = lax.rem(pl.program_id(1), group)
    coef = head ** -0.5 * LOG2E
    wq = wq_ref[...]

    @pl.when(member == 0)
    def _():
        for j in range(n_blk):
            k_rot[j, 0] = rotate(k_ref[j, 0], wk_ref[...], cos_ref[j], sin_ref[j])

    for j in range(n_blk):
        q_rot = rotate(q_ref[j, 0], wq, cos_ref[j], sin_ref[j])
        s_diag = causal(dot_nt(q_rot, k_rot[j, 0]), NEG_BIG)
        row_max = jnp.max(s_diag, axis=-1, keepdims=True)
        if j:
            s_off = dot_nt(q_rot, prefix(k_rot, j))
            row_max = jnp.maximum(row_max, jnp.max(s_off, axis=-1, keepdims=True))
        e_diag = jnp.exp2((s_diag - row_max) * coef)
        row_sum = jnp.sum(e_diag, axis=-1, keepdims=True)
        if j:
            e_off = jnp.exp2((s_off - row_max) * coef)
            row_sum = row_sum + jnp.sum(e_off, axis=-1, keepdims=True)
        inv_sum = 1.0 / row_sum
        out = dot_nn((e_diag * inv_sum).astype(jnp.bfloat16), v_ref[j, 0])
        if j:
            out = out + dot_nn((e_off * inv_sum).astype(jnp.bfloat16), prefix(v_ref, j))
        o_ref[j, 0] = out.astype(jnp.bfloat16)
        lse = jnp.broadcast_to(row_max * coef + jnp.log2(row_sum), (rows, head))
        lanes = lax.broadcasted_iota(jnp.int32, (rows, head), 1)
        owner = lax.div(lanes, head // group)
        lse_ref[0, 0, j] = jnp.where(owner >= member, lse, lse_ref[0, 0, j])


def bwd_kernel(group, heads, n_deps, q_ref, k_ref, v_ref, do_ref, lse_ref, cos_ref, sin_ref, wq_ref, wk_ref, *refs):
    d_ref, dwq_ref, dwk_ref, k_rot, dk_acc, dv_acc = refs[n_deps:]
    n_blk, _, rows, head = q_ref.shape
    member = lax.rem(pl.program_id(1), group)
    pair = lax.div(pl.program_id(1), group)
    q_lanes = pl.ds(pl.multiple_of(pl.program_id(1) * head, head), head)
    k_lanes = pl.ds(pl.multiple_of((heads + pair) * head, head), head)
    v_lanes = pl.ds(pl.multiple_of((heads + heads // group + pair) * head, head), head)
    scale = head ** -0.5
    coef = scale * LOG2E
    wq = wq_ref[...]
    wk = wk_ref[...]

    @pl.when(jnp.logical_and(pl.program_id(0) == 0, pl.program_id(1) == 0))
    def _():
        dwq_ref[...] = jnp.zeros_like(dwq_ref)
        dwk_ref[...] = jnp.zeros_like(dwk_ref)

    @pl.when(member == 0)
    def _():
        dk_acc[...] = jnp.zeros_like(dk_acc)
        dv_acc[...] = jnp.zeros_like(dv_acc)
        for j in range(n_blk):
            k_rot[j, 0] = rotate(k_ref[j, 0], wk, cos_ref[j], sin_ref[j])

    for j in range(n_blk):
        here = slice(j * rows, (j + 1) * rows)
        before = slice(0, j * rows)
        q_raw = q_ref[j, 0]
        q_rot = rotate(q_raw, wq, cos_ref[j], sin_ref[j])
        d_out = do_ref[j, 0]
        lse_all = lse_ref[0, 0, j]
        lse = lse_all[:, :1]
        for other in range(1, group):
            at = other * (head // group)
            lse = jnp.where(member == other, lse_all[:, at:at + 1], lse)
        p_diag = causal(jnp.exp2(dot_nt(q_rot, k_rot[j, 0]) * coef - lse), 0.0)
        dp_diag = dot_nt(d_out, v_ref[j, 0])
        delta = jnp.sum(p_diag * dp_diag, axis=-1, keepdims=True)
        if j:
            p_off = jnp.exp2(dot_nt(q_rot, prefix(k_rot, j)) * coef - lse)
            dp_off = dot_nt(d_out, prefix(v_ref, j))
            delta = delta + jnp.sum(p_off * dp_off, axis=-1, keepdims=True)
        ds_diag = (p_diag * (dp_diag - delta) * scale).astype(jnp.bfloat16)
        dq = dot_nn(ds_diag, k_rot[j, 0])
        dk_acc[here, :] += dot_tn(ds_diag, q_rot)
        dv_acc[here, :] += dot_tn(p_diag.astype(jnp.bfloat16), d_out)
        if j:
            ds_off = (p_off * (dp_off - delta) * scale).astype(jnp.bfloat16)
            dq = dq + dot_nn(ds_off, prefix(k_rot, j))
            dk_acc[before, :] += dot_tn(ds_off, q_rot)
            dv_acc[before, :] += dot_tn(p_off.astype(jnp.bfloat16), d_out)
        d_ref[j, 0, :, q_lanes], dw = rotate_bwd(dq.astype(jnp.bfloat16), q_raw, wq, cos_ref[j], sin_ref[j])
        dwq_ref[...] += dw

    @pl.when(member == group - 1)
    def _():
        for j in range(n_blk):
            here = slice(j * rows, (j + 1) * rows)
            d_ref[j, 0, :, k_lanes], dw = rotate_bwd(dk_acc[here, :].astype(jnp.bfloat16), k_ref[j, 0], wk, cos_ref[j], sin_ref[j])
            dwk_ref[...] += dw
            d_ref[j, 0, :, v_lanes] = dv_acc[here, :].astype(jnp.bfloat16)


def attention_specs(n_blk, rows, head, heads, group):
    kv = heads // group
    block = (n_blk, 1, rows, head)
    q_spec = pl.BlockSpec(block, lambda b, h: (0, b, 0, h))
    k_spec = pl.BlockSpec(block, lambda b, h: (0, b, 0, heads + h // group))
    v_spec = pl.BlockSpec(block, lambda b, h: (0, b, 0, heads + kv + h // group))
    lse_spec = pl.BlockSpec((1, 1, n_blk, rows, head), lambda b, h: (b, h // group, 0, 0, 0))
    tab_spec = pl.BlockSpec((n_blk, rows, head), lambda b, h: (0, 0, 0))
    w_spec = pl.BlockSpec((1, head), lambda b, h: (0, 0))
    dw_spec = pl.BlockSpec((8, head), lambda b, h: (0, 0))
    return q_spec, k_spec, v_spec, lse_spec, tab_spec, w_spec, dw_spec


def kernel_params():
    return pltpu.CompilerParams(dimension_semantics=('arbitrary', 'arbitrary'), vmem_limit_bytes=56 * 2 ** 20)


def attention_fwd(qkv, cos_t, sin_t, wq, wk, heads, group):
    n_blk, batch, rows, _ = qkv.shape
    head = cos_t.shape[2]
    pairs = batch * heads * (n_blk * rows) ** 2 // 2
    q_spec, k_spec, v_spec, lse_spec, tab_spec, w_spec, _ = attention_specs(n_blk, rows, head, heads, group)
    return pl.pallas_call(
        functools.partial(fwd_kernel, group),
        grid=(batch, heads),
        in_specs=[q_spec, k_spec, v_spec, tab_spec, tab_spec, w_spec, w_spec],
        out_specs=[q_spec, lse_spec],
        out_shape=[jax.ShapeDtypeStruct((n_blk, batch, rows, heads * head), jnp.bfloat16),
                   jax.ShapeDtypeStruct((batch, heads // group, n_blk, rows, head), jnp.float32)],
        scratch_shapes=[pltpu.VMEM((n_blk, 1, rows, head), jnp.bfloat16)],
        compiler_params=kernel_params(),
        cost_estimate=pl.CostEstimate(flops=pairs * head * 4, bytes_accessed=batch * n_blk * rows * 3000, transcendentals=pairs),
        name='attention_fwd',
    )(qkv, qkv, qkv, cos_t, sin_t, wq, wk)


def attention_bwd(qkv, d_out, lse, cos_t, sin_t, wq, wk, heads, group, deps=()):
    n_blk, batch, rows, cols = qkv.shape
    head = cos_t.shape[2]
    pairs = batch * heads * (n_blk * rows) ** 2 // 2
    d_spec = pl.BlockSpec((n_blk, 1, rows, cols), lambda b, h: (0, b, 0, 0))
    q_spec, k_spec, v_spec, lse_spec, tab_spec, w_spec, dw_spec = attention_specs(n_blk, rows, head, heads, group)
    return pl.pallas_call(
        functools.partial(bwd_kernel, group, heads, len(deps)),
        grid=(batch, heads),
        in_specs=[q_spec, k_spec, v_spec, q_spec, lse_spec, tab_spec, tab_spec, w_spec, w_spec] + [pl.BlockSpec(memory_space=pl.ANY)] * len(deps),
        out_specs=[d_spec, dw_spec, dw_spec],
        out_shape=[jax.ShapeDtypeStruct(qkv.shape, jnp.bfloat16),
                   jax.ShapeDtypeStruct((8, head), jnp.float32),
                   jax.ShapeDtypeStruct((8, head), jnp.float32)],
        scratch_shapes=[pltpu.VMEM((n_blk, 1, rows, head), jnp.bfloat16), pltpu.VMEM((n_blk * rows, head), jnp.float32), pltpu.VMEM((n_blk * rows, head), jnp.float32)],
        compiler_params=kernel_params(),
        cost_estimate=pl.CostEstimate(flops=pairs * head * 10, bytes_accessed=batch * n_blk * rows * 6000, transcendentals=pairs),
        name='attention_bwd',
    )(qkv, qkv, qkv, d_out, lse, cos_t, sin_t, wq, wk, *deps)


def copy_kernel(src_ref, dst_ref):
    dst_ref[...] = src_ref[...]


def settle(arr):
    rows, cols = arr.shape
    spec = pl.BlockSpec((256, cols), lambda i: (i, 0))
    return pl.pallas_call(
        copy_kernel, grid=(rows // 256,), in_specs=[spec], out_specs=spec,
        out_shape=jax.ShapeDtypeStruct(arr.shape, arr.dtype),
        cost_estimate=pl.CostEstimate(flops=rows * cols * 400, bytes_accessed=rows * cols * 4, transcendentals=0),
        name='settle',
    )(arr)


def split_kernel(n_dev, src_ref, k_ref, v_ref):
    half = k_ref.shape[1] // n_dev
    for j in range(n_dev):
        k_ref[:, j * half:(j + 1) * half] = src_ref[:, 2 * j * half:(2 * j + 1) * half]
        v_ref[:, j * half:(j + 1) * half] = src_ref[:, (2 * j + 1) * half:(2 * j + 2) * half]


def split_kv(arr, n_dev):
    rows, cols = arr.shape
    out = pl.BlockSpec((256, cols // 2), lambda i: (i, 0))
    shape = jax.ShapeDtypeStruct((rows, cols // 2), arr.dtype)
    return pl.pallas_call(
        functools.partial(split_kernel, n_dev), grid=(rows // 256,),
        in_specs=[pl.BlockSpec((256, cols), lambda i: (i, 0))], out_specs=[out, out], out_shape=[shape, shape],
        cost_estimate=pl.CostEstimate(flops=rows * cols * 400, bytes_accessed=rows * cols * 4, transcendentals=0),
        name='split_kv',
    )(arr)


def ein(spec, a, b):
    return jnp.einsum(spec, a, b, preferred_element_type=jnp.float32)


def solution(mesh):
    n_dev = mesh.shape['sp']

    def swap(arr):
        return lax.all_to_all(arr, 'sp', 0, 0, tiled=True)

    def gather(arr):
        return lax.all_gather(arr, 'sp', axis=0, tiled=False)

    def join(arr):
        n_blk, batch, rows, cols = arr.shape
        return jnp.transpose(arr, (1, 2, 0, 3)).reshape(batch, rows, n_blk * cols)

    def layer(x_in, dy_in, positions, w_q, w_k, w_v, w_o, w_pre, w_post, q_norm, k_norm):
        head = q_norm.shape[0]
        q_cols = w_q.shape[1] // n_dev
        kv_cols = w_k.shape[1] // n_dev
        heads = q_cols // head
        group = q_cols // kv_cols
        me = lax.axis_index('sp')
        bounds = []
        at = 0
        for size in CHUNKS:
            bounds.append((at, at + size))
            at += size
        parts = range(len(bounds))

        x_f32 = [x_in[lo:hi].astype(jnp.float32) for lo, hi in bounds]
        pre = [jax.vjp(pre_norm, x, w_pre) for x in x_f32]
        normed = [gather(pre[c][0]) for c in parts]
        cos_t, sin_t = rope_tables(lax.all_gather(positions, 'sp', axis=0, tiled=True), head)
        cos_t = cos_t.reshape(n_dev, -1, head)
        sin_t = sin_t.reshape(n_dev, -1, head)
        w_loc = jnp.concatenate([lax.dynamic_slice_in_dim(w_q, me * q_cols, q_cols, 1),
                                 lax.dynamic_slice_in_dim(w_k, me * kv_cols, kv_cols, 1),
                                 lax.dynamic_slice_in_dim(w_v, me * kv_cols, kv_cols, 1)], axis=1)
        wo_loc = lax.dynamic_slice_in_dim(w_o, me * q_cols, q_cols, 0)
        wq_row = q_norm[None, :]
        wk_row = k_norm[None, :]

        qkv, o_loc, lse, y_parts, d_proj_all = [], [], [], [], []
        dw_post = 0.0
        d_c = None
        for c in parts:
            lo, hi = bounds[c]
            qkv.append(ein('jbsd,dn->jbsn', normed[c], w_loc).astype(jnp.bfloat16))
            o_c, lse_c = attention_fwd(qkv[c], cos_t, sin_t, wq_row, wk_row, heads, group)
            o_loc.append(o_c)
            lse.append(lse_c)
            o_tok = swap(o_c)
            proj = ein('bsn,nd->bsd', join(o_tok), w_o).astype(jnp.bfloat16)
            post, post_pull = jax.vjp(post_norm, proj, w_post)
            y_parts.append((x_f32[c] + post).astype(jnp.bfloat16))
            d_c, dwp = post_pull(dy_in[lo:hi].astype(jnp.float32))
            dw_post = dw_post + dwp
            d_proj_all.append(gather(d_c))

        d_tok, d_head = [], []
        dw_o = 0.0
        dq_norm = 0.0
        dk_norm = 0.0
        last = len(bounds) - 1
        for c in parts:
            dw_o = dw_o + ein('jbsn,jbsd->nd', o_loc[c], d_proj_all[c])
            deps = (d_head[c - 1],) if c else (d_c,)
            if c == last:
                dw_o = dw_o.astype(jnp.bfloat16)
                deps += (dw_o,)
            d_o = ein('jbsd,nd->jbsn', d_proj_all[c], wo_loc).astype(jnp.bfloat16)
            d_qkv, dwq, dwk = attention_bwd(qkv[c], d_o, lse[c], cos_t, sin_t, wq_row, wk_row, heads, group, deps)
            dq_norm = dq_norm + jnp.sum(dwq, axis=0)
            dk_norm = dk_norm + jnp.sum(dwk, axis=0)
            d_head.append(d_qkv)
            d_tok.append(swap(d_qkv))

        def gather_to(axis):
            return lambda arr: lax.all_gather(arr, 'sp', axis=axis, tiled=True)

        dw_o = settle(gather_to(0)(dw_o))
        dw_q = sum(ein('jbsd,jbsn->dn', normed[c], d_head[c][..., :q_cols]) for c in parts).astype(jnp.bfloat16)
        dw_q = settle(gather_to(1)(dw_q))
        dw_kv = sum(ein('jbsd,jbsn->dn', normed[c], d_head[c][..., q_cols:]) for c in parts).astype(jnp.bfloat16)
        dw_k, dw_v = split_kv(gather_to(1)(dw_kv), n_dev)

        dx_parts = []
        dw_pre = 0.0
        for c in parts:
            lo, hi = bounds[c]
            dq = join(d_tok[c][..., :q_cols])
            dk = join(d_tok[c][..., q_cols:q_cols + kv_cols])
            dv = join(d_tok[c][..., q_cols + kv_cols:])
            d_normed = (ein('bsn,dn->bsd', dq, w_q) + ein('bsn,dn->bsd', dk, w_k) + ein('bsn,dn->bsd', dv, w_v)).astype(jnp.bfloat16)
            dx_norm, dwp = pre[c][1](d_normed)
            dw_pre = dw_pre + dwp
            dx_parts.append((dy_in[lo:hi].astype(jnp.float32) + dx_norm).astype(jnp.bfloat16))

        sums = lax.psum((dw_pre, dw_post, dq_norm, dk_norm), 'sp')
        return (jnp.concatenate(y_parts, axis=0), jnp.concatenate(dx_parts, axis=0), dw_q, dw_k, dw_v, dw_o) + sums

    token_spec = P('dp', 'sp', None)
    return jax.shard_map(layer, mesh=mesh,
                         in_specs=(token_spec, token_spec, P(('dp', 'sp')), P(None, None), P(None, None), P(None, None), P(None, None), P(None), P(None), P(None), P(None)),
                         out_specs=(token_spec, token_spec, P('dp', None), P('dp', None), P('dp', None), P('dp', None), P('dp'), P('dp'), P('dp'), P('dp')),
                         check_vma=False)
```

time: 1980 us -> 1860 us (0.939)
  waiting for transfers between devices: 735 us -> 438 us
  blocking collectives: 37.6 us -> 210 us
  local copies, waits for them, and re-layouts: 238 us -> 72.4 us
  Pallas kernels: 320 us -> 422 us
  matrix products: 525 us -> 583 us
  other arithmetic: 70.6 us -> 94.3 us
    all_gather x8 -> x9, waiting for transfers between devices: 496 us -> 277 us  [the longest x6 277 us: gather(): return lax.all_gather(arr, 'sp', axis=0, tiled=False)]
    all_to_all x0 -> x2, blocking collectives: none -> 173 us  [swap(): return lax.all_to_all(arr, 'sp', 0, 0, tiled=True)]
    pallas_call x2 -> x6, Pallas kernels: 195 us -> 294 us  [the longest x3 203 us: attention_bwd(): pl.pallas_call(functools.partial(bwd_kernel, group, heads, len(deps)), gr...]
    all_to_all x8 -> x4, waiting for transfers between devices: 238 us -> 159 us  [swap(): return lax.all_to_all(arr, 'sp', 0, 0, tiled=True)]
    all_to_all x16 -> x0, local copies, waits for them, and re-layouts: 77.8 us -> none  [to_tokens(): return lax.all_to_all(arr, 'sp', 1, 2, tiled=True)]
    unnamed x74 -> x113, local copies, waits for them, and re-layouts: 78.5 us -> 2.54 us
    pallas_call x8 -> x0, local copies, waits for them, and re-layouts: 72.1 us -> none  [the longest x6 51.8 us: attention_bwd(): pl.pallas_call(functools.partial(bwd_kernel, group), grid=(batch, heads),...]
    dot_general x20 -> x27, matrix products: 525 us -> 583 us  [ein(): return jnp.einsum(spec, a, b, preferred_element_type=jnp.float32)]
  transfers between devices with their start and end apart: 16 -> 13, of which waited for: 12 -> 7; matrix products, arithmetic and copies ran while one was open for 29% -> 38% of each run, Pallas kernels for 11% -> 21%
where the time goes in v2:
time: 1860 us; the launch traced here: 1850 us
  matrix products  583 us (31%)
  waiting for transfers between devices  438 us (24%)
  Pallas kernels  422 us (23%)
  blocking collectives  210 us (11%)
  other arithmetic  94.3 us (5%)
  local copies, waits for them, and re-layouts  72.4 us (4%)
    dot_general x27, matrix products, ein(): return jnp.einsum(spec, a, b, preferred_element_type=jnp.float32)  583 us
    all_gather x6, waiting for transfers between devices, gather(): return lax.all_gather(arr, 'sp', axis=0, tiled=False)  277 us
    pallas_call x3, Pallas kernels, attention_bwd(): pl.pallas_call(functools.partial(bwd_kernel, group, heads, len(deps)), gr...  203 us
    all_to_all x2, blocking collectives, swap(): return lax.all_to_all(arr, 'sp', 0, 0, tiled=True)  173 us
    all_to_all x4, waiting for transfers between devices, swap(): return lax.all_to_all(arr, 'sp', 0, 0, tiled=True)  159 us
    pallas_call x3, Pallas kernels, attention_fwd(): pl.pallas_call(functools.partial(fwd_kernel, group), grid=(batch, heads),...  128 us
    pallas_call x2, Pallas kernels, settle(): pl.pallas_call(copy_kernel, grid=(rows // 256,), in_specs=[spec], out_spe...  60 us
    transpose x18, local copies, waits for them, and re-layouts, join(): return jnp.transpose(arr, (1, 2, 0, 3)).reshape(batch, rows, n_blk * cols)  52.3 us
  transfers between devices with their start and end apart: 13, of which 7 were waited for; matrix products, arithmetic and copies ran while one was open for 38% of the time, Pallas kernels for 21%

profile of v2, /device:TPU:0, one launch (start us, length us, event | category | flops | bytes accessed | tf_op | source)
XLA Modules:
  0.0 1849.5 jit_solution(15652380439685513678)
XLA Ops:
  11.2 6.1 fusion.68
  22.6 7.0 fusion.18
  30.3 12.5 all-gather.6
  55.1 5.8 constant_dynamic-slice_fusion.2
  60.9 52.5 %all-gather.25.cloned.1.call-done = bf16[8,256,4608]{2,1,0:T(8,128)(2,1)} async-done(((bf16[1,256,4608]{2,1,0:T(8,128)(2,1)}), bf16[8,256,4608]{2,1,0:T(8,128)(2,1)}) %all-gather.25.cloned.1.call-update) | async-done | bytes 18874384 | tf_op jit(solution)/shard_map/all_gather | solution.py:279
  113.4 27.1 %convert_bitcast_fusion.3.q_ref.k_ref.v_ref = bf16[8,1,256,1024]{3,2,1,0:T(8,128)(2,1)} fusion(bf16[8,256,4608]{2,1,0:T(8,128)(2,1)} %all-gather.25.cloned.1.call-done, bf16[4608,256]{1,0:T(8,128)(2,1)} %constant_dynamic-slice_fusion, bf16[4608,256]{1,0:T(8,128)(2,1)S(1)} %constant_dynamic-slice_fusion.1, bf16[4608,512]{1,0:T(8,128)(2,1)} %constant_dynamic-slice_fusion.2), kind=kOutput, calls=%fused_computation.150 | convolution fusion | flops 19357761536 | bytes 32505856 | tf_op jit(solution)/shard_map/jbsd,dn->jbsn/dot_general | solution.py:269
  140.5 32.6 %attention_fwd.4 = (bf16[8,1,256,512]{3,2,1,0:T(8,128)(2,1)}, f32[1,2,8,256,128]{4,3,2,1,0:T(8,128)}) custom-call(bf16[8,1,256,1024]{3,2,1,0:T(8,128)(2,1)} %convert_bitcast_fusion.3.q_ref.k_ref.v_ref, bf16[8,1,256,1024]{3,2,1,0:T(8,128)(2,1)} %convert_bitcast_fusion.3.q_ref.k_ref.v_ref, bf16[8,1,256,1024]{3,2,1,0:T(8,128)(2,1)} %convert_bitcast_fusion.3.q_ref.k_ref.v_ref, ...), custom_call_target="tpu_custom_call" | custom-call | flops 4294967296 | bytes 6144000 | tf_op jit(solution)/shard_map/attention_fwd/pallas_call | solution.py:199
  175.9 55.4 %all-gather.27.cloned.1.call-done = bf16[8,256,4608]{2,1,0:T(8,128)(2,1)} async-done(((bf16[1,256,4608]{2,1,0:T(8,128)(2,1)}), bf16[8,256,4608]{2,1,0:T(8,128)(2,1)}) %all-gather.27.cloned.1.call-update) | async-done | bytes 18874384 | tf_op jit(solution)/shard_map/all_gather | solution.py:279
  231.3 30.2 %convert_bitcast_fusion.2.q_ref.k_ref.v_ref = bf16[8,1,256,1024]{3,2,1,0:T(8,128)(2,1)} fusion(bf16[8,256,4608]{2,1,0:T(8,128)(2,1)} %all-gather.27.cloned.1.call-done, bf16[4608,256]{1,0:T(8,128)(2,1)} %constant_dynamic-slice_fusion, bf16[4608,256]{1,0:T(8,128)(2,1)} %copy-done.7, bf16[4608,512]{1,0:T(8,128)(2,1)} %constant_dynamic-slice_fusion.2), kind=kOutput, calls=%fused_computation.149 | convolution fusion | flops 19357761536 | bytes 32505856 | tf_op jit(solution)/shard_map/jbsd,dn->jbsn/dot_general | solution.py:269
  261.5 32.6 %attention_fwd.5 = (bf16[8,1,256,512]{3,2,1,0:T(8,128)(2,1)}, f32[1,2,8,256,128]{4,3,2,1,0:T(8,128)}) custom-call(bf16[8,1,256,1024]{3,2,1,0:T(8,128)(2,1)} %convert_bitcast_fusion.2.q_ref.k_ref.v_ref, bf16[8,1,256,1024]{3,2,1,0:T(8,128)(2,1)} %convert_bitcast_fusion.2.q_ref.k_ref.v_ref, bf16[8,1,256,1024]{3,2,1,0:T(8,128)(2,1)} %convert_bitcast_fusion.2.q_ref.k_ref.v_ref, ...), custom_call_target="tpu_custom_call" | custom-call | flops 4294967296 | bytes 6144000 | tf_op jit(solution)/shard_map/attention_fwd/pallas_call | solution.py:199
  300.4 44.3 %all-to-all-done.2 = bf16[8,1,256,512]{3,2,1,0:T(8,128)(2,1)} async-done(((bf16[8,1,256,512]{3,2,1,0:T(8,128)(2,1)}), bf16[8,1,256,512]{3,2,1,0:T(8,128)(2,1)}, u32[]{:S(2)}, u32[]{:S(2)}) %all-to-all-start.2) | async-done | bytes 2097184 | tf_op jit(solution)/shard_map/all_to_all | solution.py:276
  348.6 17.5 fusion.80
  366.1 18.9 %fusion.82 = (f32[256]{0:T(256)S(1)}, bf16[256,4608]{1,0:T(8,128)(2,1)S(1)}) fusion(bf16[256,4096]{0,1:T(8,128)(2,1)} %bitcast.246, bf16[4096,4608]{1,0:T(8,128)(2,1)} %param.17), kind=kOutput, calls=%fused_computation.131 | convolution fusion | flops 9668395008 | bytes 42206208 | tf_op jit(solution)/shard_map/bsn,nd->bsd/dot_general | solution.py:269
  385.1 7.8 fusion.75
  393.0 6.0 fusion.79
  399.6 28.3 %all-gather.23.cloned.1.call-done = bf16[16,256,4608]{2,1,0:T(8,128)(2,1)} async-done(((bf16[2,256,4608]{2,1,0:T(8,128)(2,1)}), bf16[16,256,4608]{2,1,0:T(8,128)(2,1)}) %all-gather.23.cloned.1.call-update) | async-done | bytes 37748752 | tf_op jit(solution)/shard_map/all_gather | solution.py:279
  427.9 46.9 %fusion.47.q_ref.k_ref.v_ref = bf16[8,2,256,1024]{3,2,1,0:T(8,128)(2,1)} fusion(bf16[8,2,256,4608]{3,2,1,0:T(8,128)(2,1)} %bitcast.260, bf16[4608,256]{1,0:T(8,128)(2,1)} %constant_dynamic-slice_fusion, bf16[4608,256]{1,0:T(8,128)(2,1)S(1)} %copy-done.8, bf16[4608,512]{1,0:T(8,128)(2,1)} %constant_dynamic-slice_fusion.2), kind=kOutput, calls=%fused_computation.92 | convolution fusion | flops 38687211520 | bytes 55574528 | tf_op jit(solution)/shard_map/jbsd,dn->jbsn/dot_general | solution.py:269
  474.8 62.7 %attention_fwd.3 = (bf16[8,2,256,512]{3,2,1,0:T(8,128)(2,1)}, f32[2,2,8,256,128]{4,3,2,1,0:T(8,128)}) custom-call(bf16[8,2,256,1024]{3,2,1,0:T(8,128)(2,1)} %fusion.47.q_ref.k_ref.v_ref, bf16[8,2,256,1024]{3,2,1,0:T(8,128)(2,1)} %fusion.47.q_ref.k_ref.v_ref, bf16[8,2,256,1024]{3,2,1,0:T(8,128)(2,1)} %fusion.47.q_ref.k_ref.v_ref, ...), custom_call_target="tpu_custom_call" | custom-call | flops 8589934592 | bytes 12288000 | tf_op jit(solution)/shard_map/attention_fwd/pallas_call | solution.py:199
  537.6 75.6 %all_to_all.30 = bf16[8,2,256,512]{3,2,1,0:T(8,128)(2,1)} all-to-all(bf16[8,2,256,512]{3,2,1,0:T(8,128)(2,1)} %get-tuple-element.27), channel_id=1, replica_groups=mesh['dp'=1,'sp'=8] {'sp'}, dimensions={0} | all-to-all | bytes 8388608 | tf_op jit(solution)/shard_map/all_to_all | solution.py:276
  613.1 6.3 copy.61
  619.5 27.6 %fusion.23 = (f32[2,256]{1,0:T(2,128)S(1)}, bf16[2,256,4608]{2,1,0:T(8,128)(2,1)}) fusion(bf16[2,256,4096]{1,2,0:T(8,128)(2,1)} %bitcast.249, bf16[4096,4608]{1,0:T(8,128)(2,1)} %param.17), kind=kOutput, calls=%fused_computation.39 | convolution fusion | flops 19336790016 | bytes 46663680 | tf_op jit(solution)/shard_map/bsn,nd->bsd/dot_general | solution.py:269
  647.1 7.7 fusion.21
  654.9 4.2 fusion.22
  659.2 17.4 fusion.115
  676.6 16.1 fusion.117
  692.8 141.0 %all-gather.29.cloned.1.call-done = bf16[16,256,4608]{2,1,0:T(8,128)(2,1)} async-done(((bf16[2,256,4608]{2,1,0:T(8,128)(2,1)}), bf16[16,256,4608]{2,1,0:T(8,128)(2,1)}) %all-gather.29.cloned.1.call-update) | async-done | bytes 37748752 | tf_op jit(solution)/shard_map/all_gather | solution.py:279
  833.7 30.9 %fusion.33.refs_1_ = bf16[512,4608]{1,0:T(8,128)(2,1)} fusion(f32[512,4608,1]{1,0,2:T(8,128)} %fusion.115, f32[512,4608,1]{1,0,2:T(8,128)} %fusion.117, bf16[8,2,256,4608]{3,2,1,0:T(8,128)(2,1)} %bitcast.263, bf16[8,2,256,512]{3,2,1,0:T(8,128)(2,1)} %get-tuple-element.27), kind=kOutput, calls=%fused_computation.55 | convolution fusion | flops 19334430720 | bytes 65536000 | tf_op jit(solution)/shard_map/jbsn,jbsd->nd/dot_general | solution.py:269
  864.7 17.4 convert_bitcast_fusion.4.do_ref
  882.1 16.1 convert_bitcast_fusion.5.do_ref
  898.3 26.3 %fusion.106.do_ref = bf16[8,2,256,512]{3,2,1,0:T(8,128)(2,1)} fusion(bf16[8,2,256,4608]{3,2,1,0:T(8,128)(2,1)} %bitcast.264, bf16[4096,4608]{1,0:T(8,128)(2,1)} %param.17, s32[]{:T(128)S(6)} %select_n.8), kind=kOutput, calls=%fused_computation.154 | convolution fusion | flops 19329449984 | bytes 46661636 | tf_op jit(solution)/shard_map/jbsd,nd->jbsn/dot_general | solution.py:269
  924.5 99.2 %attention_bwd.3 = (bf16[8,2,256,1024]{3,2,1,0:T(8,128)(2,1)}, f32[8,128]{1,0:T(8,128)}, f32[8,128]{1,0:T(8,128)}) custom-call(bf16[8,2,256,1024]{3,2,1,0:T(8,128)(2,1)} %fusion.47.q_ref.k_ref.v_ref, bf16[8,2,256,1024]{3,2,1,0:T(8,128)(2,1)} %fusion.47.q_ref.k_ref.v_ref, bf16[8,2,256,1024]{3,2,1,0:T(8,128)(2,1)} %fusion.47.q_ref.k_ref.v_ref, ...), custom_call_target="tpu_custom_call" | custom-call | flops 21474836480 | bytes 24576000 | tf_op jit(solution)/shard_map/attention_bwd/pallas_call | solution.py:219
  1023.8 5.8 fusion.137
  1029.6 51.6 %attention_bwd.4 = (bf16[8,1,256,1024]{3,2,1,0:T(8,128)(2,1)}, f32[8,128]{1,0:T(8,128)}, f32[8,128]{1,0:T(8,128)}) custom-call(bf16[8,1,256,1024]{3,2,1,0:T(8,128)(2,1)} %convert_bitcast_fusion.3.q_ref.k_ref.v_ref, bf16[8,1,256,1024]{3,2,1,0:T(8,128)(2,1)} %convert_bitcast_fusion.3.q_ref.k_ref.v_ref, ...), custom_call_target="tpu_custom_call" | custom-call | flops 10737418240 | bytes 12288000 | tf_op jit(solution)/shard_map/attention_bwd/pallas_call | solution.py:219
  1081.3 52.0 %attention_bwd.5 = (bf16[8,1,256,1024]{3,2,1,0:T(8,128)(2,1)}, f32[8,128]{1,0:T(8,128)}, f32[8,128]{1,0:T(8,128)}) custom-call(bf16[8,1,256,1024]{3,2,1,0:T(8,128)(2,1)} %convert_bitcast_fusion.2.q_ref.k_ref.v_ref, bf16[8,1,256,1024]{3,2,1,0:T(8,128)(2,1)} %convert_bitcast_fusion.2.q_ref.k_ref.v_ref, ...), custom_call_target="tpu_custom_call" | custom-call | flops 10737418240 | bytes 12288000 | tf_op jit(solution)/shard_map/attention_bwd/pallas_call | solution.py:219
  1133.3 16.5 fusion.113
  1149.8 27.8 %fusion.8 = f32[4608,512,1,1]{1,0,3,2:T(8,128)} fusion(bf16[8,2,256,4608]{3,2,1,0:T(8,128)(2,1)} %bitcast.261, bf16[8,2,256,512]{3,2,1,0:T(8,128)(2,1)} %get-tuple-element.79), kind=kOutput, calls=%fused_computation.8 | convolution fusion | flops 19327352832 | bytes 51380224 | tf_op jit(solution)/shard_map/jbsd,jbsn->dn/dot_general | solution.py:269
  1177.6 20.5 %fusion.31 = bf16[4608,512]{1,0:T(8,128)(2,1)} fusion(f32[4608,512,1,1]{1,0,3,2:T(8,128)} %fusion.8, f32[4608,512,1]{1,0,2:T(8,128)} %fusion.113, bf16[8,256,4608]{2,1,0:T(8,128)(2,1)} %all-gather.27.cloned.1.call-done, bf16[8,1,256,1024]{3,2,1,0:T(8,128)(2,1)} %get-tuple-element.35), kind=kOutput, calls=%fused_computation.52 | convolution fusion | flops 9670754304 | bytes 44564480 | tf_op jit(solution)/shard_map/jbsd,jbsn->dn/dot_general | solution.py:269
  1198.2 17.4 fusion.110
  1215.6 28.4 %fusion.6 = f32[4608,512,1,1]{1,0,3,2:T(8,128)} fusion(bf16[8,2,256,4608]{3,2,1,0:T(8,128)(2,1)} %bitcast.262, bf16[8,2,256,512]{3,2,1,0:T(8,128)(2,1)} %get-tuple-element.78), kind=kOutput, calls=%fused_computation.6 | convolution fusion | flops 19327352832 | bytes 51380224 | tf_op jit(solution)/shard_map/jbsd,jbsn->dn/dot_general | solution.py:269
  1244.0 20.4 %fusion.29 = bf16[4608,512]{1,0:T(8,128)(2,1)} fusion(f32[4608,512,1,1]{1,0,3,2:T(8,128)} %fusion.6, f32[4608,512,1]{1,0,2:T(8,128)} %fusion.110, bf16[8,256,4608]{2,1,0:T(8,128)(2,1)} %all-gather.27.cloned.1.call-done, bf16[8,1,256,1024]{3,2,1,0:T(8,128)(2,1)} %get-tuple-element.35), kind=kOutput, calls=%fused_computation.49 | convolution fusion | flops 9670754304 | bytes 44564480 | tf_op jit(solution)/shard_map/jbsd,jbsn->dn/dot_general | solution.py:269
  1264.4 97.8 %all_to_all.31 = bf16[8,1,256,1024]{3,2,1,0:T(8,128)(2,1)} all-to-all(bf16[8,1,256,1024]{3,2,1,0:T(8,128)(2,1)} %get-tuple-element.33.refs_0_), channel_id=1, replica_groups=mesh['dp'=1,'sp'=8] {'sp'}, dimensions={0} | all-to-all | bytes 8388608 | tf_op jit(solution)/shard_map/all_to_all | solution.py:276
  1375.4 83.4 %all-to-all-done.5 = bf16[8,1,256,1024]{3,2,1,0:T(8,128)(2,1)} async-done(((bf16[8,1,256,1024]{3,2,1,0:T(8,128)(2,1)}), bf16[8,1,256,1024]{3,2,1,0:T(8,128)(2,1)}, u32[]{:S(2)}, u32[]{:S(2)}) %all-to-all-start.5) | async-done | bytes 4194336 | tf_op jit(solution)/shard_map/all_to_all | solution.py:276
  1458.8 4.3 all-to-all-start.3
  1471.7 21.2 %fusion.139 = f32[256,4608]{1,0:T(8,128)} fusion(bf16[256,4096]{0,1:T(8,128)(2,1)} %bitcast.252, bf16[4608,4096]{1,0:T(8,128)(2,1)} %param.14), kind=kOutput, calls=%fused_computation.219 | convolution fusion | flops 9663676416 | bytes 44564480 | tf_op jit(solution)/shard_map/bsn,dn->bsd/dot_general | solution.py:269
  1492.9 13.6 convolution_add_fusion.1
  1506.5 17.9 fusion.138
  1524.5 11.4 convolution_add_fusion.3
  1535.9 12.1 fusion.51
  1548.1 15.7 fusion.67
  1563.9 12.1 fusion.77
  1576.0 31.7 %all-to-all-done.3 = bf16[8,2,256,1024]{3,2,1,0:T(8,128)(2,1)} async-done(((bf16[8,2,256,1024]{3,2,1,0:T(8,128)(2,1)}), bf16[8,2,256,1024]{3,2,1,0:T(8,128)(2,1)}, u32[]{:S(2)}, u32[]{:S(2)}) %all-to-all-start.3) | async-done | bytes 8388640 | tf_op jit(solution)/shard_map/all_to_all | solution.py:276
  1607.7 4.5 slice_bitcast_fusion.4
  1616.3 4.7 slice_bitcast_fusion
  1621.1 6.3 copy.65
  1629.7 17.1 fusion.10
  1646.9 28.0 %fusion = f32[2,256,4608]{2,1,0:T(8,128)} fusion(bf16[2,256,4096]{1,2,0:T(8,128)(2,1)} %bitcast.248, bf16[4608,4096]{1,0:T(8,128)(2,1)} %param.14), kind=kOutput, calls=%fused_computation | convolution fusion | flops 19327352832 | bytes 51380224 | tf_op jit(solution)/shard_map/bsn,dn->bsd/dot_general | solution.py:269
  1674.9 22.6 %fusion.19 = (f32[4608]{0:T(1024)S(1)}, f32[2,256]{1,0:T(2,128)S(1)}, bf16[2,256,4608]{2,1,0:T(8,128)(2,1)}) fusion(f32[2,256]{1,0:T(2,128)S(1)} %copy-done.29, bf16[4,256,4608]{2,1,0:T(8,128)(2,1)} %param.11, f32[4608]{0:T(1024)S(1)} %copy-done.19, f32[2,256,4608]{2,1,0:T(8,128)} %fusion.10, f32[2,256,4608]{2,1,0:T(8,128)} %fusion, ...), kind=kOutput, calls=%fused_computation.35 | convolution fusion | flops 9689624576 | bytes 49324032 | tf_op jit(solution)/shard_map/bsn,dn->bsd/dot_general | solution.py:269
  1697.6 24.4 %all-reduce = (f32[4608]{0:T(1024)}, f32[4608]{0:T(1024)}, f32[128]{0:T(128)}, f32[128]{0:T(128)}) all-reduce(f32[4608]{0:T(1024)S(1)} %add_add_fusion.7, f32[4608]{0:T(1024)S(1)} %copy-done.23, f32[128]{0:T(128)S(1)} %copy-done.51, f32[128]{0:T(128)S(1)} %copy-done.50), channel_id=1, replica_groups=mesh['dp'=1,'sp'=8] {'sp'}, use_global_device_ids=true, to_apply=%region_15.0 | all-reduce | flops 9472 | bytes 75776 | tf_op jit(solution)/shard_map/psum | solution.py:368
  1722.0 13.1 fusion.20
  1735.0 8.7 pad_maximum_fusion.2
  1743.8 7.1 pad_maximum_fusion.1
  1750.9 29.5 %settle.3 = bf16[4096,4608]{1,0:T(8,128)(2,1)} custom-call(bf16[4096,4608]{1,0:T(8,128)(2,1)} %all-gather.21.cloned.1.call-done.src_ref), custom_call_target="tpu_custom_call" | custom-call | flops 7549747200 | bytes 75497472 | tf_op jit(solution)/shard_map/settle/pallas_call | solution.py:241
  1780.4 30.5 %settle.2 = bf16[4608,4096]{1,0:T(8,128)(2,1)} custom-call(bf16[4608,4096]{1,0:T(8,128)(2,1)} %all-gather.17.cloned.1.call-done.src_ref), custom_call_target="tpu_custom_call" | custom-call | flops 7549747200 | bytes 75497472 | tf_op jit(solution)/shard_map/settle/pallas_call | solution.py:241
  1810.9 31.6 %split_kv.1 = (bf16[4608,2048]{1,0:T(8,128)(2,1)}, bf16[4608,2048]{1,0:T(8,128)(2,1)}) custom-call(bf16[4608,4096]{1,0:T(8,128)(2,1)} %all-gather.19.cloned.1.call-done.src_ref), custom_call_target="tpu_custom_call" | custom-call | flops 7549747200 | bytes 75497472 | tf_op jit(solution)/shard_map/split_kv/pallas_call | solution.py:260
  (186 shorter events, 64.4 us)
Async XLA Ops:
  7.2 4.0 copy-start.26
  7.2 106.2 %all-gather.25.cloned.1.call-start = ((), (), s32[]{:S(2)}) async-start(), calls=%async_computation.10 | async-start | bytes 21233664 | tf_op jit(solution)/shard_map/all_gather | solution.py:279
  10.6 6.7 copy-start.36
  11.2 6.1 copy-start.38
  11.2 10.8 copy-start.18
  17.4 213.9 %all-gather.27.cloned.1.call-start = ((), (), s32[]{:S(2)}) async-start(), calls=%async_computation.11 | async-start | bytes 21233664 | tf_op jit(solution)/shard_map/all_gather | solution.py:279
  18.1 409.8 %all-gather.23.cloned.1.call-start = ((), (), s32[]{:S(2)}) async-start(), calls=%async_computation.9 | async-start | bytes 42467328 | tf_op jit(solution)/shard_map/all_gather | solution.py:279
  51.0 62.3 %copy-start.7 = (bf16[4608,256]{1,0:T(8,128)(2,1)}, bf16[4608,256]{1,0:T(8,128)(2,1)S(1)}, u32[]{:S(2)}) copy-start(bf16[4608,256]{1,0:T(8,128)(2,1)S(1)} %constant_dynamic-slice_fusion.1) | copy-start | bytes 7077892
  173.1 121.0 %all-to-all-start.1 = ((bf16[8,1,256,512]{3,2,1,0:T(8,128)(2,1)}), bf16[8,1,256,512]{3,2,1,0:T(8,128)(2,1)S(1)}, u32[]{:S(2)}, u32[]{:S(2)}) async-start(bf16[8,1,256,512]{3,2,1,0:T(8,128)(2,1)} %get-tuple-element.28), calls=%async_computation.1 | async-start | bytes 4194304 | tf_op jit(solution)/shard_map/all_to_all | solution.py:276
  261.5 35.9 %copy-start.27 = (f32[4608]{0:T(1024)S(1)}, f32[4608]{0:T(1024)}, u32[]{:S(2)}) copy-start(f32[4608]{0:T(1024)} %param.19) | copy-start | bytes 55300
  294.1 3.3 copy-start.5
  294.1 50.6 %all-to-all-start.2 = ((bf16[8,1,256,512]{3,2,1,0:T(8,128)(2,1)}), bf16[8,1,256,512]{3,2,1,0:T(8,128)(2,1)}, u32[]{:S(2)}, u32[]{:S(2)}) async-start(bf16[8,1,256,512]{3,2,1,0:T(8,128)(2,1)} %get-tuple-element.29), calls=%async_computation.2 | async-start | bytes 4194304 | tf_op jit(solution)/shard_map/all_to_all | solution.py:276
  297.3 361.9 %all-gather.33.cloned.1.call-start = ((), (), s32[]{:S(2)}) async-start(), calls=%async_computation.14 | async-start | bytes 21233664 | tf_op jit(solution)/shard_map/all_gather | solution.py:279
  297.4 357.5 %copy-start.16 = (f32[4608]{0:T(1024)}, f32[4608]{0:T(1024)S(1)}, u32[]{:S(2)}) copy-start(f32[4608]{0:T(1024)S(1)} %broadcast_add_fusion) | copy-start | bytes 55300
  366.1 26.8 %copy-start.1 = (bf16[256,4608]{1,0:T(8,128)(2,1)}, bf16[256,4608]{1,0:T(8,128)(2,1)S(1)}, u32[]{:S(2)}) copy-start(bf16[256,4608]{1,0:T(8,128)(2,1)S(1)} %get-tuple-element.92) | copy-start | bytes 7077892
  366.1 26.8 %copy-start.32 = (f32[256]{0:T(256)}, f32[256]{0:T(256)S(1)}, u32[]{:S(2)}) copy-start(f32[256]{0:T(256)S(1)} %fusion.134) | copy-start | bytes 3076
  385.1 7.8 copy-start.3
  385.1 7.8 copy-start.34
  399.0 29.0 %copy-start.8 = (bf16[4608,256]{1,0:T(8,128)(2,1)S(1)}, bf16[4608,256]{1,0:T(8,128)(2,1)}, u32[]{:S(2)}) copy-start(bf16[4608,256]{1,0:T(8,128)(2,1)} %copy-done.7) | copy-start | bytes 7077892
  399.0 277.6 %all-gather.31.cloned.1.call-start = ((), (), s32[]{:S(2)}) async-start(), calls=%async_computation.13 | async-start | bytes 21233664 | tf_op jit(solution)/shard_map/all_gather | solution.py:279
  399.6 434.2 %all-gather.29.cloned.1.call-start = ((), (), s32[]{:S(2)}) async-start(), calls=%async_computation.12 | async-start | bytes 42467328 | tf_op jit(solution)/shard_map/all_gather | solution.py:279
  613.1 33.9 %slice-start = ((s8[9437184]{0:T(1024)(128)(4,1)}), s8[1048576]{0:T(1024)(128)(4,1)S(1)}, s32[]{:S(2)}) async-start(s8[9437184]{0:T(1024)(128)(4,1)} %bitcast.242), calls=%async_computation.15 | async-start | bytes 2097152
  619.5 27.6 %slice-start.1 = ((s8[9437184]{0:T(1024)(128)(4,1)}), s8[4194304]{0:T(1024)(128)(4,1)S(1)}, s32[]{:S(2)}) async-start(s8[9437184]{0:T(1024)(128)(4,1)} %bitcast.242), calls=%async_computation.16 | async-start | bytes 8388608
  619.5 27.6 %slice-start.2 = ((s8[9437184]{0:T(1024)(128)(4,1)}), s8[4194304]{0:T(1024)(128)(4,1)S(1)}, s32[]{:S(2)}) async-start(s8[9437184]{0:T(1024)(128)(4,1)} %bitcast.242), calls=%async_computation.17 | async-start | bytes 8388608
  647.0 7.8 copy-start.24
  647.1 7.8 copy-start
  659.2 17.5 copy-start.9
  659.2 1091.7 %all-gather.21.cloned.1.call-start = ((), (), s32[]{:S(2)}) async-start(), calls=%async_computation.8 | async-start | bytes 42467328 | tf_op jit(solution)/shard_map/all_gather | solution.py:348
  864.7 915.7 %all-gather.17.cloned.1.call-start = ((), (), s32[]{:S(2)}) async-start(), calls=%async_computation.6 | async-start | bytes 42467328 | tf_op jit(solution)/shard_map/all_gather | solution.py:348
  1081.3 52.0 %copy-start.6 = (bf16[8,1,256,1024]{3,2,1,0:T(8,128)(2,1)S(1)}, bf16[8,1,256,1024]{3,2,1,0:T(8,128)(2,1)}, u32[]{:S(2)}) copy-start(bf16[8,1,256,1024]{3,2,1,0:T(8,128)(2,1)} %get-tuple-element.33.refs_0_) | copy-start | bytes 12582916
  1198.2 612.7 %all-gather.19.cloned.1.call-start = ((), (), s32[]{:S(2)}) async-start(), calls=%async_computation.7 | async-start | bytes 42467328 | tf_op jit(solution)/shard_map/all_gather | solution.py:348
  1362.2 3.4 copy-start.20
  1362.2 3.4 copy-start.21
  1362.2 3.4 copy-start.22
  1362.2 4.1 copy-start.49
  1362.2 4.1 copy-start.48
  1362.2 4.1 copy-start.45
  1362.2 4.1 copy-start.44
  1362.2 4.1 copy-start.46
  1362.2 4.1 copy-start.47
  1362.2 96.6 %all-to-all-start.5 = ((bf16[8,1,256,1024]{3,2,1,0:T(8,128)(2,1)}), bf16[8,1,256,1024]{3,2,1,0:T(8,128)(2,1)}, u32[]{:S(2)}, u32[]{:S(2)}) async-start(bf16[8,1,256,1024]{3,2,1,0:T(8,128)(2,1)} %get-tuple-element.35), calls=%async_computation.5 | async-start | bytes 8388608 | tf_op jit(solution)/shard_map/all_to_all | solution.py:276
  1458.8 148.9 %all-to-all-start.3 = ((bf16[8,2,256,1024]{3,2,1,0:T(8,128)(2,1)}), bf16[8,2,256,1024]{3,2,1,0:T(8,128)(2,1)}, u32[]{:S(2)}, u32[]{:S(2)}) async-start(bf16[8,2,256,1024]{3,2,1,0:T(8,128)(2,1)} %get-tuple-element.31.refs_0_), calls=%async_computation.3 | async-start | bytes 16777216 | tf_op jit(solution)/shard_map/all_to_all | solution.py:276
  1471.7 21.2 %copy-start.15 = (bf16[1,256,8,256]{1,3,2,0:T(8,128)(2,1)S(1)}, bf16[1,256,8,256]{1,3,2,0:T(8,128)(2,1)}, u32[]{:S(2)}) copy-start(bf16[1,256,8,256]{1,3,2,0:T(8,128)(2,1)} %copy.79) | copy-start | bytes 3145732
  1492.9 13.6 copy-start.10
  1506.5 17.9 copy-start.13
  1524.5 11.4 copy-start.12
  1535.9 12.2 copy-start.14
  1535.9 12.2 copy-start.19
  1535.9 12.2 copy-start.37
  1535.9 12.2 copy-start.39
  1548.1 15.8 copy-start.41
  1548.1 15.8 copy-start.43
  1548.1 15.8 copy-start.2
  1548.1 15.8 copy-start.17
  1548.1 15.8 copy-start.33
  1548.1 15.8 copy-start.35
  1646.9 28.0 %copy-start.11 = (bf16[2,256,8,256]{1,3,2,0:T(8,128)(2,1)S(1)}, bf16[2,256,8,256]{1,3,2,0:T(8,128)(2,1)}, u32[]{:S(2)}) copy-start(bf16[2,256,8,256]{1,3,2,0:T(8,128)(2,1)} %copy.67) | copy-start | bytes 6291460
  1646.9 28.0 %copy-start.29 = (f32[2,256]{1,0:T(2,128)S(1)}, f32[2,256]{1,0:T(2,128)}, u32[]{:S(2)}) copy-start(f32[2,256]{1,0:T(2,128)} %copy-done.28) | copy-start | bytes 6148
  1674.9 22.7 %copy-start.23 = (f32[4608]{0:T(1024)S(1)}, f32[4608]{0:T(1024)}, u32[]{:S(2)}) copy-start(f32[4608]{0:T(1024)} %add_add_fusion.6) | copy-start | bytes 55300
  1674.9 22.7 %copy-start.50 = (f32[128]{0:T(128)S(1)}, f32[128]{0:T(128)}, u32[]{:S(2)}) copy-start(f32[128]{0:T(128)} %get-tuple-element.99) | copy-start | bytes 1540
  1674.9 22.7 %copy-start.51 = (f32[128]{0:T(128)S(1)}, f32[128]{0:T(128)}, u32[]{:S(2)}) copy-start(f32[128]{0:T(128)} %get-tuple-element.100) | copy-start | bytes 1540
  1674.9 47.0 %copy-start.31 = (f32[2,256]{1,0:T(2,128)S(1)}, f32[2,256]{1,0:T(2,128)}, u32[]{:S(2)}) copy-start(f32[2,256]{1,0:T(2,128)} %copy-done.30) | copy-start | bytes 6148
  1674.9 47.0 %copy-start.25 = (f32[2,256]{1,0:T(2,128)S(1)}, f32[2,256]{1,0:T(2,128)}, u32[]{:S(2)}) copy-start(f32[2,256]{1,0:T(2,128)} %copy-done.24) | copy-start | bytes 6148
  1735.0 8.7 copy-start.4
  (5 other events, 3.0 us)
Sparse Core Ops, SparseCore 0:
  17.5 95.8 all-gather.24
  115.7 115.4 all-gather.26
  233.7 194.1 all-gather.22
  429.6 93.0 all-gather.32
  524.3 133.1 all-gather.30
  659.8 173.8 all-gather.28
  864.8 173.8 all-gather.20
  1198.3 270.5 all-gather.16
  1470.7 254.1 all-gather.18

commit v3 on v2

--- a/solution.py
+++ b/solution.py
@@ -11,7 +11,8 @@
 ROPE_SCALE = 8.0
 NEG_BIG = -1e30
 LOG2E = 1.4426950408889634
-CHUNKS = (2, 1, 1)
+NORM_CHUNKS = (2, 2)
+GRAD_CHUNKS = (2, 1, 1)
 
 
 def rms_scale(x_f32, weight):
@@ -174,33 +175,35 @@
             d_ref[j, 0, :, v_lanes] = dv_acc[here, :].astype(jnp.bfloat16)
 
 
-def attention_specs(n_blk, rows, head, heads, group):
+def attention_specs(n_blk, rows, head, heads, group, first, do_first=0):
     kv = heads // group
     block = (n_blk, 1, rows, head)
-    q_spec = pl.BlockSpec(block, lambda b, h: (0, b, 0, h))
-    k_spec = pl.BlockSpec(block, lambda b, h: (0, b, 0, heads + h // group))
-    v_spec = pl.BlockSpec(block, lambda b, h: (0, b, 0, heads + kv + h // group))
+    o_spec = pl.BlockSpec(block, lambda b, h: (0, do_first + b, 0, h))
+    q_spec = pl.BlockSpec(block, lambda b, h: (0, first + b, 0, h))
+    k_spec = pl.BlockSpec(block, lambda b, h: (0, first + b, 0, heads + h // group))
+    v_spec = pl.BlockSpec(block, lambda b, h: (0, first + b, 0, heads + kv + h // group))
     lse_spec = pl.BlockSpec((1, 1, n_blk, rows, head), lambda b, h: (b, h // group, 0, 0, 0))
     tab_spec = pl.BlockSpec((n_blk, rows, head), lambda b, h: (0, 0, 0))
     w_spec = pl.BlockSpec((1, head), lambda b, h: (0, 0))
     dw_spec = pl.BlockSpec((8, head), lambda b, h: (0, 0))
-    return q_spec, k_spec, v_spec, lse_spec, tab_spec, w_spec, dw_spec
+    return o_spec, q_spec, k_spec, v_spec, lse_spec, tab_spec, w_spec, dw_spec
 
 
 def kernel_params():
     return pltpu.CompilerParams(dimension_semantics=('arbitrary', 'arbitrary'), vmem_limit_bytes=56 * 2 ** 20)
 
 
-def attention_fwd(qkv, cos_t, sin_t, wq, wk, heads, group):
-    n_blk, batch, rows, _ = qkv.shape
+def attention_fwd(qkv, first, cos_t, sin_t, wq, wk, heads, group):
+    n_blk, _, rows, _ = qkv.shape
+    batch = 1
     head = cos_t.shape[2]
     pairs = batch * heads * (n_blk * rows) ** 2 // 2
-    q_spec, k_spec, v_spec, lse_spec, tab_spec, w_spec, _ = attention_specs(n_blk, rows, head, heads, group)
+    o_spec, q_spec, k_spec, v_spec, lse_spec, tab_spec, w_spec, _ = attention_specs(n_blk, rows, head, heads, group, first)
     return pl.pallas_call(
         functools.partial(fwd_kernel, group),
         grid=(batch, heads),
         in_specs=[q_spec, k_spec, v_spec, tab_spec, tab_spec, w_spec, w_spec],
-        out_specs=[q_spec, lse_spec],
+        out_specs=[o_spec, lse_spec],
         out_shape=[jax.ShapeDtypeStruct((n_blk, batch, rows, heads * head), jnp.bfloat16),
                    jax.ShapeDtypeStruct((batch, heads // group, n_blk, rows, head), jnp.float32)],
         scratch_shapes=[pltpu.VMEM((n_blk, 1, rows, head), jnp.bfloat16)],
@@ -210,18 +213,19 @@
     )(qkv, qkv, qkv, cos_t, sin_t, wq, wk)
 
 
-def attention_bwd(qkv, d_out, lse, cos_t, sin_t, wq, wk, heads, group, deps=()):
-    n_blk, batch, rows, cols = qkv.shape
+def attention_bwd(qkv, first, d_out, do_first, lse, cos_t, sin_t, wq, wk, heads, group, deps=()):
+    n_blk, _, rows, cols = qkv.shape
+    batch = 1
     head = cos_t.shape[2]
     pairs = batch * heads * (n_blk * rows) ** 2 // 2
     d_spec = pl.BlockSpec((n_blk, 1, rows, cols), lambda b, h: (0, b, 0, 0))
-    q_spec, k_spec, v_spec, lse_spec, tab_spec, w_spec, dw_spec = attention_specs(n_blk, rows, head, heads, group)
+    o_spec, q_spec, k_spec, v_spec, lse_spec, tab_spec, w_spec, dw_spec = attention_specs(n_blk, rows, head, heads, group, first, do_first)
     return pl.pallas_call(
         functools.partial(bwd_kernel, group, heads, len(deps)),
         grid=(batch, heads),
-        in_specs=[q_spec, k_spec, v_spec, q_spec, lse_spec, tab_spec, tab_spec, w_spec, w_spec] + [pl.BlockSpec(memory_space=pl.ANY)] * len(deps),
+        in_specs=[q_spec, k_spec, v_spec, o_spec, lse_spec, tab_spec, tab_spec, w_spec, w_spec] + [pl.BlockSpec(memory_space=pl.ANY)] * len(deps),
         out_specs=[d_spec, dw_spec, dw_spec],
-        out_shape=[jax.ShapeDtypeStruct(qkv.shape, jnp.bfloat16),
+        out_shape=[jax.ShapeDtypeStruct((n_blk, batch, rows, cols), jnp.bfloat16),
                    jax.ShapeDtypeStruct((8, head), jnp.float32),
                    jax.ShapeDtypeStruct((8, head), jnp.float32)],
         scratch_shapes=[pltpu.VMEM((n_blk, 1, rows, head), jnp.bfloat16), pltpu.VMEM((n_blk * rows, head), jnp.float32), pltpu.VMEM((n_blk * rows, head), jnp.float32)],
@@ -235,38 +239,48 @@
     dst_ref[...] = src_ref[...]
 
 
-def settle(arr):
+def settle(arr, steps):
     rows, cols = arr.shape
-    spec = pl.BlockSpec((256, cols), lambda i: (i, 0))
+    spec = pl.BlockSpec((rows // steps, cols), lambda i: (i, 0))
     return pl.pallas_call(
-        copy_kernel, grid=(rows // 256,), in_specs=[spec], out_specs=spec,
+        copy_kernel, grid=(steps,), compiler_params=pltpu.CompilerParams(vmem_limit_bytes=56 * 2 ** 20), in_specs=[spec], out_specs=spec,
         out_shape=jax.ShapeDtypeStruct(arr.shape, arr.dtype),
         cost_estimate=pl.CostEstimate(flops=rows * cols * 400, bytes_accessed=rows * cols * 4, transcendentals=0),
         name='settle',
     )(arr)
 
 
-def split_kernel(n_dev, src_ref, k_ref, v_ref):
-    half = k_ref.shape[1] // n_dev
+def split_kernel(n_dev, src_ref, q_ref, k_ref):
+    q_cols = q_ref.shape[1] // n_dev
+    k_cols = k_ref.shape[1] // n_dev
     for j in range(n_dev):
-        k_ref[:, j * half:(j + 1) * half] = src_ref[:, 2 * j * half:(2 * j + 1) * half]
-        v_ref[:, j * half:(j + 1) * half] = src_ref[:, (2 * j + 1) * half:(2 * j + 2) * half]
-
-
-def split_kv(arr, n_dev):
+        at = j * (q_cols + k_cols)
+        q_ref[:, j * q_cols:(j + 1) * q_cols] = src_ref[:, at:at + q_cols]
+        k_ref[:, j * k_cols:(j + 1) * k_cols] = src_ref[:, at + q_cols:at + q_cols + k_cols]
+
+
+def split_qk(arr, n_dev, q_wide, k_wide, steps):
     rows, cols = arr.shape
-    out = pl.BlockSpec((256, cols // 2), lambda i: (i, 0))
-    shape = jax.ShapeDtypeStruct((rows, cols // 2), arr.dtype)
     return pl.pallas_call(
-        functools.partial(split_kernel, n_dev), grid=(rows // 256,),
-        in_specs=[pl.BlockSpec((256, cols), lambda i: (i, 0))], out_specs=[out, out], out_shape=[shape, shape],
+        functools.partial(split_kernel, n_dev), grid=(steps,), compiler_params=pltpu.CompilerParams(vmem_limit_bytes=56 * 2 ** 20),
+        in_specs=[pl.BlockSpec((rows // steps, cols), lambda i: (i, 0))],
+        out_specs=[pl.BlockSpec((rows // steps, q_wide), lambda i: (i, 0)), pl.BlockSpec((rows // steps, k_wide), lambda i: (i, 0))],
+        out_shape=[jax.ShapeDtypeStruct((rows, q_wide), arr.dtype), jax.ShapeDtypeStruct((rows, k_wide), arr.dtype)],
         cost_estimate=pl.CostEstimate(flops=rows * cols * 400, bytes_accessed=rows * cols * 4, transcendentals=0),
-        name='split_kv',
+        name='split_qk',
     )(arr)
 
 
 def ein(spec, a, b):
     return jnp.einsum(spec, a, b, preferred_element_type=jnp.float32)
+
+
+AFTER_DWO = 2
+
+
+def spans(sizes):
+    ends = [sum(sizes[:i + 1]) for i in range(len(sizes))]
+    return [(end - size, end) for size, end in zip(sizes, ends)]
 
 
 def solution(mesh):
@@ -289,16 +303,15 @@
         heads = q_cols // head
         group = q_cols // kv_cols
         me = lax.axis_index('sp')
-        bounds = []
-        at = 0
-        for size in CHUNKS:
-            bounds.append((at, at + size))
-            at += size
-        parts = range(len(bounds))
-
-        x_f32 = [x_in[lo:hi].astype(jnp.float32) for lo, hi in bounds]
-        pre = [jax.vjp(pre_norm, x, w_pre) for x in x_f32]
-        normed = [gather(pre[c][0]) for c in parts]
+        batch = x_in.shape[0]
+        wide = spans(NORM_CHUNKS)
+        steps = spans(GRAD_CHUNKS)
+        seqs = range(batch)
+        home = [next((g, i - lo) for g, (lo, hi) in enumerate(wide) if lo <= i < hi) for i in seqs]
+        turn = [next((g, i - lo) for g, (lo, hi) in enumerate(steps) if lo <= i < hi) for i in seqs]
+
+        x_f32 = [x_in[i:i + 1].astype(jnp.float32) for i in seqs]
+        normed = [gather(pre_norm(x_in[lo:hi].astype(jnp.float32), w_pre)) for lo, hi in wide]
         cos_t, sin_t = rope_tables(lax.all_gather(positions, 'sp', axis=0, tiled=True), head)
         cos_t = cos_t.reshape(n_dev, -1, head)
         sin_t = sin_t.reshape(n_dev, -1, head)
@@ -309,36 +322,49 @@
         wq_row = q_norm[None, :]
         wk_row = k_norm[None, :]
 
-        qkv, o_loc, lse, y_parts, d_proj_all = [], [], [], [], []
+        o_tok, qkv, o_loc, lse, y_parts, d_parts, d_proj_all = [], [], [], [], [], [], []
         dw_post = 0.0
-        d_c = None
-        for c in parts:
-            lo, hi = bounds[c]
-            qkv.append(ein('jbsd,dn->jbsn', normed[c], w_loc).astype(jnp.bfloat16))
-            o_c, lse_c = attention_fwd(qkv[c], cos_t, sin_t, wq_row, wk_row, heads, group)
-            o_loc.append(o_c)
-            lse.append(lse_c)
-            o_tok = swap(o_c)
-            proj = ein('bsn,nd->bsd', join(o_tok), w_o).astype(jnp.bfloat16)
+        for i in seqs:
+            g, first = home[i]
+            if not first:
+                qkv.append(ein('jbsd,dn->jbsn', normed[g], w_loc).astype(jnp.bfloat16))
+            o_i, lse_i = attention_fwd(qkv[g], first, cos_t, sin_t, wq_row, wk_row, heads, group)
+            o_loc.append(o_i)
+            lse.append(lse_i)
+            o_tok.append(swap(o_i))
+            proj = ein('bsn,nd->bsd', join(o_tok[i]), w_o).astype(jnp.bfloat16)
+            if i:
+                proj, _ = lax.optimization_barrier((proj, d_parts[-1]))
             post, post_pull = jax.vjp(post_norm, proj, w_post)
-            y_parts.append((x_f32[c] + post).astype(jnp.bfloat16))
-            d_c, dwp = post_pull(dy_in[lo:hi].astype(jnp.float32))
+            d_i, dwp = post_pull(dy_in[i:i + 1].astype(jnp.float32))
             dw_post = dw_post + dwp
-            d_proj_all.append(gather(d_c))
+            d_parts.append(d_i)
+            y_parts.append((x_f32[i] + post).astype(jnp.bfloat16))
+            step, _ = turn[i]
+            lo, hi = steps[step]
+            own = d_parts[lo:] if hi - lo == 1 else [jnp.concatenate(d_parts[lo:], axis=0)]
+            if i + 1 == hi:
+                d_proj_all.append(gather(own[0]))
+
+        d_o = []
+        dw_o = 0.0
+        for step, (lo, hi) in enumerate(steps):
+            for k in range(lo, hi):
+                d_k = d_proj_all[step] if hi - lo == 1 else d_proj_all[step][:, k - lo:k - lo + 1]
+                dw_o = dw_o + ein('jbsn,jbsd->nd', o_loc[k], d_k)
+            dw_o = dw_o.astype(jnp.bfloat16) if hi == batch else lax.optimization_barrier(dw_o)
+            d_o.append(ein('jbsd,nd->jbsn', d_proj_all[step], wo_loc).astype(jnp.bfloat16))
 
         d_tok, d_head = [], []
-        dw_o = 0.0
         dq_norm = 0.0
         dk_norm = 0.0
-        last = len(bounds) - 1
-        for c in parts:
-            dw_o = dw_o + ein('jbsn,jbsd->nd', o_loc[c], d_proj_all[c])
-            deps = (d_head[c - 1],) if c else (d_c,)
-            if c == last:
-                dw_o = dw_o.astype(jnp.bfloat16)
+        for i in seqs:
+            g, first = home[i]
+            step, place = turn[i]
+            deps = (d_head[i - 1],) if i else (d_parts[-1],)
+            if i == AFTER_DWO:
                 deps += (dw_o,)
-            d_o = ein('jbsd,nd->jbsn', d_proj_all[c], wo_loc).astype(jnp.bfloat16)
-            d_qkv, dwq, dwk = attention_bwd(qkv[c], d_o, lse[c], cos_t, sin_t, wq_row, wk_row, heads, group, deps)
+            d_qkv, dwq, dwk = attention_bwd(qkv[g], first, d_o[step], place, lse[i], cos_t, sin_t, wq_row, wk_row, heads, group, deps)
             dq_norm = dq_norm + jnp.sum(dwq, axis=0)
             dk_norm = dk_norm + jnp.sum(dwk, axis=0)
             d_head.append(d_qkv)
@@ -347,21 +373,32 @@
         def gather_to(axis):
             return lambda arr: lax.all_gather(arr, 'sp', axis=axis, tiled=True)
 
-        dw_o = settle(gather_to(0)(dw_o))
-        dw_q = sum(ein('jbsd,jbsn->dn', normed[c], d_head[c][..., :q_cols]) for c in parts).astype(jnp.bfloat16)
-        dw_q = settle(gather_to(1)(dw_q))
-        dw_kv = sum(ein('jbsd,jbsn->dn', normed[c], d_head[c][..., q_cols:]) for c in parts).astype(jnp.bfloat16)
-        dw_k, dw_v = split_kv(gather_to(1)(dw_kv), n_dev)
+        dw_o = settle(gather_to(0)(dw_o), 8)
+        qk = q_cols + kv_cols
+        dw_qk, dw_v = 0.0, 0.0
+        for g in range(len(wide)):
+            own = [d_head[i] for i in seqs if home[i][0] == g]
+            for i, d in enumerate(own):
+                n_g = normed[g] if len(own) == 1 else normed[g][:, i:i + 1]
+                dw_qk = dw_qk + ein('jbsd,jbsn->dn', n_g, d[..., :qk])
+            for i, d in enumerate(own):
+                n_g = normed[g] if len(own) == 1 else normed[g][:, i:i + 1]
+                dw_v = dw_v + ein('jbsd,jbsn->dn', n_g, d[..., qk:])
+            if g == 0:
+                dw_qk = lax.optimization_barrier(dw_qk)
+                dw_v = lax.optimization_barrier(dw_v)
+        dw_q, dw_k = split_qk(gather_to(1)(dw_qk.astype(jnp.bfloat16)), n_dev, w_q.shape[1], w_k.shape[1], 9)
+        dw_v = settle(gather_to(1)(dw_v.astype(jnp.bfloat16)), 6)
 
         dx_parts = []
         dw_pre = 0.0
-        for c in parts:
-            lo, hi = bounds[c]
-            dq = join(d_tok[c][..., :q_cols])
-            dk = join(d_tok[c][..., q_cols:q_cols + kv_cols])
-            dv = join(d_tok[c][..., q_cols + kv_cols:])
+        for lo, hi in wide:
+            tok = jnp.concatenate(d_tok[lo:hi], axis=1)
+            dq = join(tok[..., :q_cols])
+            dk = join(tok[..., q_cols:qk])
+            dv = join(tok[..., qk:])
             d_normed = (ein('bsn,dn->bsd', dq, w_q) + ein('bsn,dn->bsd', dk, w_k) + ein('bsn,dn->bsd', dv, w_v)).astype(jnp.bfloat16)
-            dx_norm, dwp = pre[c][1](d_normed)
+            dx_norm, dwp = jax.vjp(pre_norm, x_in[lo:hi].astype(jnp.float32), w_pre)[1](d_normed)
             dw_pre = dw_pre + dwp
             dx_parts.append((dy_in[lo:hi].astype(jnp.float32) + dx_norm).astype(jnp.bfloat16))
 

time: 1860 us -> 2090 us (1.12)
  blocking collectives: 210 us -> 351 us
  waiting for transfers between devices: 438 us -> 540 us
    all_gather x6 -> x5, waiting for transfers between devices: 277 us -> 493 us  [gather(): return lax.all_gather(arr, 'sp', axis=0, tiled=False)]
    all_to_all x2 -> x4, blocking collectives: 173 us -> 314 us  [swap(): return lax.all_to_all(arr, 'sp', 0, 0, tiled=True)]
    all_to_all x4, waiting for transfers between devices: 159 us -> 33.6 us  [swap(): return lax.all_to_all(arr, 'sp', 0, 0, tiled=True)]
    pallas_call x3 -> x4, Pallas kernels: 203 us -> 207 us  [attention_bwd(): pl.pallas_call(functools.partial(bwd_kernel, group, heads, len(deps)), gr...]
    transpose x18 -> x14, local copies, waits for them, and re-layouts: 52.3 us -> 56.5 us  [join(): return jnp.transpose(arr, (1, 2, 0, 3)).reshape(batch, rows, n_blk * cols)]
    pallas_call x3 -> x4, Pallas kernels: 128 us -> 132 us  [attention_fwd(): pl.pallas_call(functools.partial(fwd_kernel, group), grid=(batch, heads),...]
  transfers between devices with their start and end apart: 13 -> 12, of which waited for: 7 -> 6; matrix products, arithmetic and copies ran while one was open for 38% -> 27% of each run, Pallas kernels for 21% -> 8%
where the time goes in v3:
time: 2090 us; the launch traced here: 2080 us
  matrix products  568 us (27%)
  waiting for transfers between devices  540 us (26%)
  Pallas kernels  416 us (20%)
  blocking collectives  351 us (17%)
  other arithmetic  93.8 us (4%)
  local copies, waits for them, and re-layouts  84.9 us (4%)
    dot_general x27, matrix products, ein(): return jnp.einsum(spec, a, b, preferred_element_type=jnp.float32)  568 us
    all_gather x5, waiting for transfers between devices, gather(): return lax.all_gather(arr, 'sp', axis=0, tiled=False)  493 us
    all_to_all x4, blocking collectives, swap(): return lax.all_to_all(arr, 'sp', 0, 0, tiled=True)  314 us
    pallas_call x4, Pallas kernels, attention_bwd(): pl.pallas_call(functools.partial(bwd_kernel, group, heads, len(deps)), gr...  207 us
    pallas_call x4, Pallas kernels, attention_fwd(): pl.pallas_call(functools.partial(fwd_kernel, group), grid=(batch, heads),...  132 us
    transpose x14, local copies, waits for them, and re-layouts, join(): return jnp.transpose(arr, (1, 2, 0, 3)).reshape(batch, rows, n_blk * cols)  56.5 us
  transfers between devices with their start and end apart: 12, of which 6 were waited for; matrix products, arithmetic and copies ran while one was open for 27% of the time, Pallas kernels for 8%

profile of v3, /device:TPU:0, one launch (start us, length us, event | category | flops | bytes accessed | tf_op | source)
XLA Modules:
  0.0 2081.7 jit_solution(1124222551682920173)
XLA Ops:
  7.2 4.9 fusion.35
  13.7 5.2 fusion.28
  19.8 12.1 all-gather.5
  44.8 4.8 constant_dynamic-slice_fusion.2
  49.7 146.2 %all-gather.21.cloned.1.call-done = bf16[16,256,4608]{2,1,0:T(8,128)(2,1)} async-done(((bf16[2,256,4608]{2,1,0:T(8,128)(2,1)}), bf16[16,256,4608]{2,1,0:T(8,128)(2,1)}) %all-gather.21.cloned.1.call-update) | async-done | bytes 37748752 | tf_op jit(solution)/shard_map/all_gather | solution.py:293
  195.8 46.8 %convolution_convert_fusion.1.q_ref.k_ref.v_ref = bf16[8,2,256,1024]{3,2,1,0:T(8,128)(2,1)} fusion(bf16[8,2,256,4608]{3,2,1,0:T(8,128)(2,1)} %bitcast.285, bf16[4608,256]{1,0:T(8,128)(2,1)S(1)} %constant_dynamic-slice_fusion, bf16[4608,256]{1,0:T(8,128)(2,1)} %constant_dynamic-slice_fusion.1, bf16[4608,512]{1,0:T(8,128)(2,1)} %constant_dynamic-slice_fusion.2), kind=kOutput, calls=%fused_computation.92 | convolution fusion | flops 38687211520 | bytes 55574528 | tf_op jit(solution)/shard_map/jbsd,dn->jbsn/dot_general | solution.py:275
  242.7 32.7 %attention_fwd.4 = (bf16[8,1,256,512]{3,2,1,0:T(8,128)(2,1)}, f32[1,2,8,256,128]{4,3,2,1,0:T(8,128)}) custom-call(bf16[8,2,256,1024]{3,2,1,0:T(8,128)(2,1)} %convolution_convert_fusion.1.q_ref.k_ref.v_ref, bf16[8,2,256,1024]{3,2,1,0:T(8,128)(2,1)} %convolution_convert_fusion.1.q_ref.k_ref.v_ref, ...), custom_call_target="tpu_custom_call" | custom-call | flops 4294967296 | bytes 6144000 | tf_op jit(solution)/shard_map/attention_fwd/pallas_call | solution.py:202
  277.9 116.7 %all-gather.23.cloned.1.call-done = bf16[16,256,4608]{2,1,0:T(8,128)(2,1)} async-done(((bf16[2,256,4608]{2,1,0:T(8,128)(2,1)}), bf16[16,256,4608]{2,1,0:T(8,128)(2,1)}) %all-gather.23.cloned.1.call-update) | async-done | bytes 37748752 | tf_op jit(solution)/shard_map/all_gather | solution.py:293
  394.7 47.6 %convolution_convert_fusion.q_ref.k_ref.v_ref = bf16[8,2,256,1024]{3,2,1,0:T(8,128)(2,1)} fusion(bf16[8,2,256,4608]{3,2,1,0:T(8,128)(2,1)} %bitcast.290, bf16[4608,256]{1,0:T(8,128)(2,1)} %copy-done.14, bf16[4608,256]{1,0:T(8,128)(2,1)} %constant_dynamic-slice_fusion.1, bf16[4608,512]{1,0:T(8,128)(2,1)} %constant_dynamic-slice_fusion.2), kind=kOutput, calls=%fused_computation.91 | convolution fusion | flops 38687211520 | bytes 55574528 | tf_op jit(solution)/shard_map/jbsd,dn->jbsn/dot_general | solution.py:275
  442.2 32.7 %attention_fwd.5 = (bf16[8,1,256,512]{3,2,1,0:T(8,128)(2,1)}, f32[1,2,8,256,128]{4,3,2,1,0:T(8,128)}) custom-call(bf16[8,2,256,1024]{3,2,1,0:T(8,128)(2,1)} %convolution_convert_fusion.1.q_ref.k_ref.v_ref, bf16[8,2,256,1024]{3,2,1,0:T(8,128)(2,1)} %convolution_convert_fusion.1.q_ref.k_ref.v_ref, ...), custom_call_target="tpu_custom_call" | custom-call | flops 4294967296 | bytes 6144000 | tf_op jit(solution)/shard_map/attention_fwd/pallas_call | solution.py:202
  474.9 33.1 %attention_fwd.6 = (bf16[8,1,256,512]{3,2,1,0:T(8,128)(2,1)}, f32[1,2,8,256,128]{4,3,2,1,0:T(8,128)}) custom-call(bf16[8,2,256,1024]{3,2,1,0:T(8,128)(2,1)} %convolution_convert_fusion.q_ref.k_ref.v_ref, bf16[8,2,256,1024]{3,2,1,0:T(8,128)(2,1)} %convolution_convert_fusion.q_ref.k_ref.v_ref, ...), custom_call_target="tpu_custom_call" | custom-call | flops 4294967296 | bytes 6144000 | tf_op jit(solution)/shard_map/attention_fwd/pallas_call | solution.py:202
  514.2 17.0 fusion.83
  531.3 5.8 fusion.75
  548.8 17.5 fusion.52
  566.8 4.9 fusion.76
  580.1 17.7 fusion.53
  598.4 5.2 fusion.77
  608.2 33.2 %attention_fwd.7 = (bf16[8,1,256,512]{3,2,1,0:T(8,128)(2,1)}, f32[1,2,8,256,128]{4,3,2,1,0:T(8,128)}) custom-call(bf16[8,2,256,1024]{3,2,1,0:T(8,128)(2,1)} %convolution_convert_fusion.q_ref.k_ref.v_ref, bf16[8,2,256,1024]{3,2,1,0:T(8,128)(2,1)} %convolution_convert_fusion.q_ref.k_ref.v_ref, ...), custom_call_target="tpu_custom_call" | custom-call | flops 4294967296 | bytes 6144000 | tf_op jit(solution)/shard_map/attention_fwd/pallas_call | solution.py:202
  641.4 51.1 %all_to_all.40 = bf16[8,1,256,512]{3,2,1,0:T(8,128)(2,1)} all-to-all(bf16[8,1,256,512]{3,2,1,0:T(8,128)(2,1)} %get-tuple-element.40), channel_id=1, replica_groups=mesh['dp'=1,'sp'=8] {'sp'}, dimensions={0} | all-to-all | bytes 4194304 | tf_op jit(solution)/shard_map/all_to_all | solution.py:290
  696.5 17.6 fusion.54
  714.6 5.4 fusion.78
  720.0 10.3 fusion.73
  730.4 5.4 pad_maximum_fusion.2
  735.8 17.3 convert_bitcast_fusion.2.do_ref
  753.1 69.6 %all-gather.29.cloned.1.call-done = bf16[8,256,4608]{2,1,0:T(8,128)(2,1)} async-done(((bf16[1,256,4608]{2,1,0:T(8,128)(2,1)}), bf16[8,256,4608]{2,1,0:T(8,128)(2,1)}) %all-gather.29.cloned.1.call-update) | async-done | bytes 18874384 | tf_op jit(solution)/shard_map/all_gather | solution.py:293
  822.7 16.1 convert_bitcast_fusion.1.do_ref
  838.8 160.1 %all-gather.25.cloned.1.call-done = bf16[16,256,4608]{2,1,0:T(8,128)(2,1)} async-done(((bf16[2,256,4608]{2,1,0:T(8,128)(2,1)}), bf16[16,256,4608]{2,1,0:T(8,128)(2,1)}) %all-gather.25.cloned.1.call-update) | async-done | bytes 37748752 | tf_op jit(solution)/shard_map/all_gather | solution.py:293
  998.9 16.2 fusion.4
  1015.1 26.9 %fusion.108.do_ref = bf16[8,2,256,512]{3,2,1,0:T(8,128)(2,1)} fusion(bf16[8,2,256,4608]{3,2,1,0:T(8,128)(2,1)} %bitcast.257, bf16[4096,4608]{1,0:T(8,128)(2,1)} %param.17, s32[]{:T(128)S(6)} %select_n.8), kind=kOutput, calls=%fused_computation.172 | convolution fusion | flops 19329449984 | bytes 46661636 | tf_op jit(solution)/shard_map/jbsd,nd->jbsn/dot_general | solution.py:275
  1042.0 17.5 bitcast_add_fusion.5
  1059.5 18.1 bitcast_add_fusion.4
  1077.6 51.8 %attention_bwd.4 = (bf16[8,1,256,1024]{3,2,1,0:T(8,128)(2,1)}, f32[8,128]{1,0:T(8,128)}, f32[8,128]{1,0:T(8,128)}) custom-call(bf16[8,2,256,1024]{3,2,1,0:T(8,128)(2,1)} %convolution_convert_fusion.1.q_ref.k_ref.v_ref, bf16[8,2,256,1024]{3,2,1,0:T(8,128)(2,1)} %convolution_convert_fusion.1.q_ref.k_ref.v_ref, ...), custom_call_target="tpu_custom_call" | custom-call | flops 10737418240 | bytes 12288000 | tf_op jit(solution)/shard_map/attention_bwd/pallas_call | solution.py:223
  1129.3 10.8 fusion.50
  1140.2 52.0 %attention_bwd.5 = (bf16[8,1,256,1024]{3,2,1,0:T(8,128)(2,1)}, f32[8,128]{1,0:T(8,128)}, f32[8,128]{1,0:T(8,128)}) custom-call(bf16[8,2,256,1024]{3,2,1,0:T(8,128)(2,1)} %convolution_convert_fusion.1.q_ref.k_ref.v_ref, bf16[8,2,256,1024]{3,2,1,0:T(8,128)(2,1)} %convolution_convert_fusion.1.q_ref.k_ref.v_ref, ...), custom_call_target="tpu_custom_call" | custom-call | flops 10737418240 | bytes 12288000 | tf_op jit(solution)/shard_map/attention_bwd/pallas_call | solution.py:223
  1192.2 12.8 fusion.49
  1205.0 15.7 fusion.39.refs_1_
  1220.7 51.8 %attention_bwd.6 = (bf16[8,1,256,1024]{3,2,1,0:T(8,128)(2,1)}, f32[8,128]{1,0:T(8,128)}, f32[8,128]{1,0:T(8,128)}) custom-call(bf16[8,2,256,1024]{3,2,1,0:T(8,128)(2,1)} %convolution_convert_fusion.q_ref.k_ref.v_ref, bf16[8,2,256,1024]{3,2,1,0:T(8,128)(2,1)} %convolution_convert_fusion.q_ref.k_ref.v_ref, ...), custom_call_target="tpu_custom_call" | custom-call | flops 10737418240 | bytes 12288000 | tf_op jit(solution)/shard_map/attention_bwd/pallas_call | solution.py:223
  1272.5 11.2 fusion.47
  1283.7 51.6 %attention_bwd.7 = (bf16[8,1,256,1024]{3,2,1,0:T(8,128)(2,1)}, f32[8,128]{1,0:T(8,128)}, f32[8,128]{1,0:T(8,128)}) custom-call(bf16[8,2,256,1024]{3,2,1,0:T(8,128)(2,1)} %convolution_convert_fusion.q_ref.k_ref.v_ref, bf16[8,2,256,1024]{3,2,1,0:T(8,128)(2,1)} %convolution_convert_fusion.q_ref.k_ref.v_ref, ...), custom_call_target="tpu_custom_call" | custom-call | flops 10737418240 | bytes 12288000 | tf_op jit(solution)/shard_map/attention_bwd/pallas_call | solution.py:223
  1335.4 10.6 fusion.51
  1346.8 22.1 %fusion.15 = f32[4608,768,1]{1,0,2:T(8,128)} fusion(bf16[8,2,256,4608]{3,2,1,0:T(8,128)(2,1)} %bitcast.288, bf16[8,1,256,1024]{3,2,1,0:T(8,128)(2,1)} %get-tuple-element.43.refs_0_), kind=kOutput, calls=%fused_computation.21 | convolution fusion | flops 14495514624 | bytes 36175872 | tf_op jit(solution)/shard_map/jbsd,jbsn->dn/dot_general | solution.py:275
  1368.9 23.2 %bitcast_add_fusion.2 = f32[4608,768]{1,0:T(8,128)} fusion(f32[4608,768,1]{1,0,2:T(8,128)} %fusion.15, bf16[8,2,256,4608]{3,2,1,0:T(8,128)(2,1)} %bitcast.289, bf16[8,1,256,1024]{3,2,1,0:T(8,128)(2,1)S(1)} %copy-done.6), kind=kOutput, calls=%fused_computation.39 | convolution fusion | flops 14499053568 | bytes 50331648 | tf_op jit(solution)/shard_map/jbsd,jbsn->dn/dot_general | solution.py:275
  1392.1 20.9 %fusion.19 = f32[4608,768,1]{1,0,2:T(8,128)} fusion(bf16[8,2,256,4608]{3,2,1,0:T(8,128)(2,1)} %bitcast.293, bf16[8,1,256,1024]{3,2,1,0:T(8,128)(2,1)S(1)} %copy-done.12), kind=kOutput, calls=%fused_computation.25 | convolution fusion | flops 14495514624 | bytes 36175872 | tf_op jit(solution)/shard_map/jbsd,jbsn->dn/dot_general | solution.py:275
  1413.0 25.1 %fusion.22 = bf16[4608,768]{1,0:T(8,128)(2,1)} fusion(f32[4608,768]{1,0:T(8,128)} %bitcast_add_fusion.2, f32[4608,768,1]{1,0,2:T(8,128)} %fusion.19, bf16[8,2,256,4608]{3,2,1,0:T(8,128)(2,1)} %bitcast.294, bf16[8,1,256,1024]{3,2,1,0:T(8,128)(2,1)} %get-tuple-element.49), kind=kOutput, calls=%fused_computation.37 | convolution fusion | flops 14506131456 | bytes 57409536 | tf_op jit(solution)/shard_map/jbsd,jbsn->dn/dot_general | solution.py:275
  1438.2 86.4 %all_to_all.41 = bf16[8,1,256,1024]{3,2,1,0:T(8,128)(2,1)} all-to-all(bf16[8,1,256,1024]{3,2,1,0:T(8,128)(2,1)} %get-tuple-element.43.refs_0_), channel_id=1, replica_groups=mesh['dp'=1,'sp'=8] {'sp'}, dimensions={0} | all-to-all | bytes 8388608 | tf_op jit(solution)/shard_map/all_to_all | solution.py:290
  1524.6 80.4 %all_to_all.42 = bf16[8,1,256,1024]{3,2,1,0:T(8,128)(2,1)} all-to-all(bf16[8,1,256,1024]{3,2,1,0:T(8,128)(2,1)S(1)} %copy-done.7), channel_id=1, replica_groups=mesh['dp'=1,'sp'=8] {'sp'}, dimensions={0} | all-to-all | bytes 8388608 | tf_op jit(solution)/shard_map/all_to_all | solution.py:290
  1605.0 96.4 %all_to_all.43 = bf16[8,1,256,1024]{3,2,1,0:T(8,128)(2,1)} all-to-all(bf16[8,1,256,1024]{3,2,1,0:T(8,128)(2,1)S(1)} %copy-done.13), channel_id=1, replica_groups=mesh['dp'=1,'sp'=8] {'sp'}, dimensions={0} | all-to-all | bytes 8388608 | tf_op jit(solution)/shard_map/all_to_all | solution.py:290
  1706.0 7.2 pad_maximum_fusion
  1723.3 6.2 copy.65
  1744.4 33.6 %all-to-all-done.7 = bf16[8,1,256,1024]{3,2,1,0:T(8,128)(2,1)} async-done(((bf16[8,1,256,1024]{3,2,1,0:T(8,128)(2,1)}), bf16[8,1,256,1024]{3,2,1,0:T(8,128)(2,1)}, u32[]{:S(2)}, u32[]{:S(2)}) %all-to-all-start.7) | async-done | bytes 4194336 | tf_op jit(solution)/shard_map/all_to_all | solution.py:290
  1787.2 6.9 copy.75
  1794.1 4.6 slice_bitcast_fusion.41
  1805.3 16.8 fusion.8
  1822.1 16.4 fusion.6
  1838.5 27.6 %fusion.2 = f32[2,256,4608]{2,1,0:T(8,128)} fusion(bf16[2,256,4096]{1,2,0:T(8,128)(2,1)} %bitcast.261, bf16[4608,4096]{1,0:T(8,128)(2,1)} %param.14), kind=kOutput, calls=%fused_computation.2 | convolution fusion | flops 19327352832 | bytes 51380224 | tf_op jit(solution)/shard_map/bsn,dn->bsd/dot_general | solution.py:275
  1866.1 30.8 %fusion = f32[2,256,4608]{2,1,0:T(8,128)} fusion(bf16[2,256,4096]{1,2,0:T(8,128)(2,1)} %bitcast.262, bf16[4608,4096]{1,0:T(8,128)(2,1)} %param.14), kind=kOutput, calls=%fused_computation | convolution fusion | flops 19327352832 | bytes 51380224 | tf_op jit(solution)/shard_map/bsn,dn->bsd/dot_general | solution.py:275
  1897.0 20.2 add_convert_fusion
  1917.2 27.4 %fusion.29 = (f32[4608]{0:T(1024)S(1)}, f32[2,256]{1,0:T(2,128)S(1)}, f32[2,256]{1,0:T(2,128)S(1)}, f32[4608]{0:T(1024)S(1)}, bf16[2,256,4608]{2,1,0:T(8,128)(2,1)}) fusion(f32[2,256]{1,0:T(2,128)S(1)} %copy-done.30, bf16[4,256,4608]{2,1,0:T(8,128)(2,1)} %param.11, f32[4608]{0:T(1024)S(1)} %copy-done.21, bf16[2,256,4608]{2,1,0:T(8,128)(2,1)} %add_convert_fusion, ...), kind=kOutput, calls=%fused_computation.52 | convolution fusion | flops 9708494848 | bytes 58783744 | tf_op jit(solution)/shard_map/bsn,dn->bsd/dot_general | solution.py:275
  1944.7 24.6 %all-reduce = (f32[4608]{0:T(1024)}, f32[4608]{0:T(1024)}, f32[128]{0:T(128)}, f32[128]{0:T(128)}) all-reduce(f32[4608]{0:T(1024)S(1)} %add.210, f32[4608]{0:T(1024)S(1)} %copy-done.22, f32[128]{0:T(128)S(1)} %copy-done.46, f32[128]{0:T(128)S(1)} %copy-done.45), channel_id=1, replica_groups=mesh['dp'=1,'sp'=8] {'sp'}, use_global_device_ids=true, to_apply=%region_14.0 | all-reduce | flops 9472 | bytes 75776 | tf_op jit(solution)/shard_map/psum | solution.py:405
  1969.3 11.6 fusion.32
  1985.4 13.8 settle.2
  1999.2 24.9 %settle.3 = bf16[4096,4608]{1,0:T(8,128)(2,1)} custom-call(bf16[4096,4608]{1,0:T(8,128)(2,1)} %all-gather.19.cloned.1.call-done.src_ref), custom_call_target="tpu_custom_call" | custom-call | flops 7549747200 | bytes 75497472 | tf_op jit(solution)/shard_map/settle/pallas_call | solution.py:245
  2024.1 12.3 all-gather.15.cloned.1.call-done.src_ref
  2036.3 38.1 %split_qk.1 = (bf16[4608,4096]{1,0:T(8,128)(2,1)}, bf16[4608,2048]{1,0:T(8,128)(2,1)}) custom-call(bf16[4608,6144]{1,0:T(8,128)(2,1)} %all-gather.15.cloned.1.call-done.src_ref), custom_call_target="tpu_custom_call" | custom-call | flops 11324620800 | bytes 113246208 | tf_op jit(solution)/shard_map/split_qk/pallas_call | solution.py:264
  (190 shorter events, 104.8 us)
Async XLA Ops:
  7.2 5.5 copy-start.27
  7.2 188.7 %all-gather.21.cloned.1.call-start = ((), (), s32[]{:S(2)}) async-start(), calls=%async_computation.11 | async-start | bytes 42467328 | tf_op jit(solution)/shard_map/all_gather | solution.py:293
  7.2 6.5 copy-start
  12.2 6.8 copy-start.29
  12.7 6.2 copy-start.31
  13.7 5.3 copy-start.20
  18.9 0.8 copy-start.47
  19.0 375.7 %all-gather.23.cloned.1.call-start = ((), (), s32[]{:S(2)}) async-start(), calls=%async_computation.12 | async-start | bytes 42467328 | tf_op jit(solution)/shard_map/all_gather | solution.py:293
  19.7 18.6 copy-start.28
  40.7 155.1 %copy-start.14 = (bf16[4608,256]{1,0:T(8,128)(2,1)}, bf16[4608,256]{1,0:T(8,128)(2,1)S(1)}, u32[]{:S(2)}) copy-start(bf16[4608,256]{1,0:T(8,128)(2,1)S(1)} %constant_dynamic-slice_fusion) | copy-start | bytes 7077892
  275.4 232.6 %all-to-all-start = ((bf16[8,1,256,512]{3,2,1,0:T(8,128)(2,1)}), bf16[8,1,256,512]{3,2,1,0:T(8,128)(2,1)S(1)}, u32[]{:S(2)}, u32[]{:S(2)}) async-start(bf16[8,1,256,512]{3,2,1,0:T(8,128)(2,1)} %get-tuple-element.35), calls=%async_computation | async-start | bytes 4194304 | tf_op jit(solution)/shard_map/all_to_all | solution.py:290
  508.0 3.4 copy-start.11
  508.0 33.5 %all-to-all-start.1 = ((bf16[8,1,256,512]{3,2,1,0:T(8,128)(2,1)}), bf16[8,1,256,512]{3,2,1,0:T(8,128)(2,1)}, u32[]{:S(2)}, u32[]{:S(2)}) async-start(bf16[8,1,256,512]{3,2,1,0:T(8,128)(2,1)} %get-tuple-element.36), calls=%async_computation.1 | async-start | bytes 4194304 | tf_op jit(solution)/shard_map/all_to_all | solution.py:290
  514.2 17.0 copy-start.19
  531.2 5.9 copy-start.3
  541.6 34.7 %all-to-all-start.2 = ((bf16[8,1,256,512]{3,2,1,0:T(8,128)(2,1)}), bf16[8,1,256,512]{3,2,1,0:T(8,128)(2,1)}, u32[]{:S(2)}, u32[]{:S(2)}) async-start(bf16[8,1,256,512]{3,2,1,0:T(8,128)(2,1)} %get-tuple-element.38), calls=%async_computation.2 | async-start | bytes 4194304 | tf_op jit(solution)/shard_map/all_to_all | solution.py:290
  544.6 191.2 %all-gather.27.cloned.1.call-start = ((), (), s32[]{:S(2)}) async-start(), calls=%async_computation.14 | async-start | bytes 21233664 | tf_op jit(solution)/shard_map/all_gather | solution.py:293
  597.8 5.8 copy-start.1
  608.1 214.6 %all-gather.29.cloned.1.call-start = ((), (), s32[]{:S(2)}) async-start(), calls=%async_computation.15 | async-start | bytes 21233664 | tf_op jit(solution)/shard_map/all_gather | solution.py:293
  714.0 6.0 copy-start.2
  714.0 6.0 copy-start.4
  730.3 268.6 %all-gather.25.cloned.1.call-start = ((), (), s32[]{:S(2)}) async-start(), calls=%async_computation.13 | async-start | bytes 42467328 | tf_op jit(solution)/shard_map/all_gather | solution.py:293
  735.8 1249.6 %all-gather.17.cloned.1.call-start = ((), (), s32[]{:S(2)}) async-start(), calls=%async_computation.9 | async-start | bytes 21233664 | tf_op jit(solution)/shard_map/all_gather | solution.py:374
  753.1 245.8 %copy-start.15 = (bf16[8,1,256,512]{3,2,1,0:T(8,128)(2,1)S(1)}, bf16[8,1,256,512]{3,2,1,0:T(8,128)(2,1)}, u32[]{:S(2)}) copy-start(bf16[8,1,256,512]{3,2,1,0:T(8,128)(2,1)} %get-tuple-element.36) | copy-start | bytes 6291460
  1015.1 26.9 %copy-start.10 = (bf16[8,1,256,512]{3,2,1,0:T(8,128)(2,1)S(1)}, bf16[8,1,256,512]{3,2,1,0:T(8,128)(2,1)}, u32[]{:S(2)}) copy-start(bf16[8,1,256,512]{3,2,1,0:T(8,128)(2,1)} %get-tuple-element.35) | copy-start | bytes 6291460
  1140.2 64.8 %slice-start = ((s8[9437184]{0:T(1024)(128)(4,1)}), s8[1048576]{0:T(1024)(128)(4,1)S(1)}, s32[]{:S(2)}) async-start(s8[9437184]{0:T(1024)(128)(4,1)} %bitcast.254), calls=%async_computation.16 | async-start | bytes 2097152
  1140.2 64.8 %slice-start.1 = ((s8[9437184]{0:T(1024)(128)(4,1)}), s8[4194304]{0:T(1024)(128)(4,1)S(1)}, s32[]{:S(2)}) async-start(s8[9437184]{0:T(1024)(128)(4,1)} %bitcast.254), calls=%async_computation.17 | async-start | bytes 8388608
  1192.2 12.8 slice-start.2
  1192.2 12.8 copy-start.16
  1205.0 67.5 %slice-start.3 = ((s8[4718592]{0:T(1024)(128)(4,1)}), s8[524288]{0:T(1024)(128)(4,1)S(1)}, s32[]{:S(2)}) async-start(s8[4718592]{0:T(1024)(128)(4,1)} %bitcast.295), calls=%async_computation.19 | async-start | bytes 1048576
  1220.7 51.8 %slice-start.4 = ((s8[4718592]{0:T(1024)(128)(4,1)}), s8[4194304]{0:T(1024)(128)(4,1)S(1)}, s32[]{:S(2)}) async-start(s8[4718592]{0:T(1024)(128)(4,1)} %bitcast.295), calls=%async_computation.20 | async-start | bytes 8388608
  1283.7 51.6 %copy-start.48 = (f32[4608,256]{1,0:T(8,128)S(1)}, f32[4608,256]{1,0:T(8,128)}, u32[]{:S(2)}) copy-start(f32[4608,256]{1,0:T(8,128)} %fusion.47) | copy-start | bytes 14155780
  1346.0 653.2 %all-gather.19.cloned.1.call-start = ((), (), s32[]{:S(2)}) async-start(), calls=%async_computation.10 | async-start | bytes 42467328 | tf_op jit(solution)/shard_map/all_gather | solution.py:374
  1346.7 689.6 %all-gather.15.cloned.1.call-start = ((), (), s32[]{:S(2)}) async-start(), calls=%async_computation.8 | async-start | bytes 63700992 | tf_op jit(solution)/shard_map/all_gather | solution.py:374
  1346.8 22.2 %copy-start.6 = (bf16[8,1,256,1024]{3,2,1,0:T(8,128)(2,1)S(1)}, bf16[8,1,256,1024]{3,2,1,0:T(8,128)(2,1)}, u32[]{:S(2)}) copy-start(bf16[8,1,256,1024]{3,2,1,0:T(8,128)(2,1)} %get-tuple-element.45.refs_0_) | copy-start | bytes 12582916
  1368.9 23.2 %copy-start.12 = (bf16[8,1,256,1024]{3,2,1,0:T(8,128)(2,1)S(1)}, bf16[8,1,256,1024]{3,2,1,0:T(8,128)(2,1)}, u32[]{:S(2)}) copy-start(bf16[8,1,256,1024]{3,2,1,0:T(8,128)(2,1)} %get-tuple-element.47.refs_0_) | copy-start | bytes 12582916
  1438.2 86.4 %copy-start.7 = (bf16[8,1,256,1024]{3,2,1,0:T(8,128)(2,1)S(1)}, bf16[8,1,256,1024]{3,2,1,0:T(8,128)(2,1)}, u32[]{:S(2)}) copy-start(bf16[8,1,256,1024]{3,2,1,0:T(8,128)(2,1)} %get-tuple-element.45.refs_0_) | copy-start | bytes 12582916
  1524.6 80.4 %copy-start.13 = (bf16[8,1,256,1024]{3,2,1,0:T(8,128)(2,1)S(1)}, bf16[8,1,256,1024]{3,2,1,0:T(8,128)(2,1)}, u32[]{:S(2)}) copy-start(bf16[8,1,256,1024]{3,2,1,0:T(8,128)(2,1)} %get-tuple-element.47.refs_0_) | copy-start | bytes 12582916
  1701.4 3.9 copy-start.23
  1701.4 3.9 copy-start.24
  1701.4 3.9 copy-start.25
  1701.4 3.9 copy-start.26
  1701.4 4.5 copy-start.9
  1701.4 76.6 %all-to-all-start.7 = ((bf16[8,1,256,1024]{3,2,1,0:T(8,128)(2,1)}), bf16[8,1,256,1024]{3,2,1,0:T(8,128)(2,1)}, u32[]{:S(2)}, u32[]{:S(2)}) async-start(bf16[8,1,256,1024]{3,2,1,0:T(8,128)(2,1)} %get-tuple-element.49), calls=%async_computation.7 | async-start | bytes 8388608 | tf_op jit(solution)/shard_map/all_to_all | solution.py:290
  1705.9 7.3 copy-start.44
  1705.9 7.3 copy-start.43
  1705.9 7.3 copy-start.42
  1706.0 7.3 copy-start.41
  1706.0 7.3 copy-start.40
  1706.0 7.4 copy-start.39
  1706.0 7.4 copy-start.38
  1706.0 7.4 copy-start.37
  1713.4 3.5 copy-start.8
  1717.3 3.4 copy-start.5
  1805.2 16.8 copy-start.18
  1896.9 20.2 copy-start.17
  1896.9 20.2 copy-start.21
  1896.9 20.2 copy-start.30
  1896.9 20.2 copy-start.32
  1917.2 27.5 %copy-start.22 = (f32[4608]{0:T(1024)S(1)}, f32[4608]{0:T(1024)}, u32[]{:S(2)}) copy-start(f32[4608]{0:T(1024)} %add_add_fusion.6) | copy-start | bytes 55300
  1917.2 27.5 %copy-start.45 = (f32[128]{0:T(128)S(1)}, f32[128]{0:T(128)}, u32[]{:S(2)}) copy-start(f32[128]{0:T(128)} %get-tuple-element.101) | copy-start | bytes 1540
  1917.2 27.5 %copy-start.46 = (f32[128]{0:T(128)S(1)}, f32[128]{0:T(128)}, u32[]{:S(2)}) copy-start(f32[128]{0:T(128)} %get-tuple-element.102) | copy-start | bytes 1540
  1917.2 52.1 %copy-start.34 = (f32[2,256]{1,0:T(2,128)S(1)}, f32[2,256]{1,0:T(2,128)}, u32[]{:S(2)}) copy-start(f32[2,256]{1,0:T(2,128)} %copy-done.33) | copy-start | bytes 6148
  1917.2 52.1 %copy-start.36 = (f32[2,256]{1,0:T(2,128)S(1)}, f32[2,256]{1,0:T(2,128)}, u32[]{:S(2)}) copy-start(f32[2,256]{1,0:T(2,128)} %copy-done.35) | copy-start | bytes 6148
  (2 other events, 1.1 us)
Sparse Core Ops, SparseCore 0:
  19.1 176.6 all-gather.20
  198.2 196.3 all-gather.22
  608.2 115.1 all-gather.26
  730.5 92.2 all-gather.28
  825.0 173.8 all-gather.24
  1346.1 96.7 all-gather.16
  1444.7 324.9 all-gather.18
  1772.1 264.1 all-gather.14

commit v4 on v3

--- a/solution.py
+++ b/solution.py
@@ -235,6 +235,24 @@
     )(qkv, qkv, qkv, d_out, lse, cos_t, sin_t, wq, wk, *deps)
 
 
+def norm_kernel(x_ref, w_ref, out_ref):
+    out_ref[...] = pre_norm(x_ref[...].astype(jnp.float32), w_ref[...])
+
+
+def pre_norm_rows(x, weight, lo, hi):
+    batch = hi - lo
+    _, rows, width = x.shape
+    return pl.pallas_call(
+        norm_kernel, grid=(batch, 2),
+        in_specs=[pl.BlockSpec((1, rows // 2, width), lambda b, i: (lo + b, i, 0)), pl.BlockSpec((1, width), lambda b, i: (0, 0))],
+        out_specs=pl.BlockSpec((1, rows // 2, width), lambda b, i: (b, i, 0)),
+        out_shape=jax.ShapeDtypeStruct((batch, rows, width), jnp.bfloat16),
+        compiler_params=pltpu.CompilerParams(vmem_limit_bytes=60 * 2 ** 20),
+        cost_estimate=pl.CostEstimate(flops=batch * rows * width * 8, bytes_accessed=batch * rows * width * 4, transcendentals=0),
+        name='pre_norm',
+    )(x, weight[None, :])
+
+
 def copy_kernel(src_ref, dst_ref):
     dst_ref[...] = src_ref[...]
 
@@ -311,7 +329,7 @@
         turn = [next((g, i - lo) for g, (lo, hi) in enumerate(steps) if lo <= i < hi) for i in seqs]
 
         x_f32 = [x_in[i:i + 1].astype(jnp.float32) for i in seqs]
-        normed = [gather(pre_norm(x_in[lo:hi].astype(jnp.float32), w_pre)) for lo, hi in wide]
+        normed = [gather(pre_norm_rows(x_in, w_pre, lo, hi)) for lo, hi in wide]
         cos_t, sin_t = rope_tables(lax.all_gather(positions, 'sp', axis=0, tiled=True), head)
         cos_t = cos_t.reshape(n_dev, -1, head)
         sin_t = sin_t.reshape(n_dev, -1, head)

time: 2090 us -> 2080 us (level)
  transfers between devices with their start and end apart: 12 -> 12, of which waited for: 6 -> 6; matrix products, arithmetic and copies ran while one was open for 27% -> 27% of each run, Pallas kernels for 8% -> 9%
where the time goes in v4:
time: 2080 us
  matrix products  568 us (27%)
  waiting for transfers between devices  531 us (26%)
  Pallas kernels  428 us (21%)
  blocking collectives  351 us (17%)
  other arithmetic  85.9 us (4%)
  local copies, waits for them, and re-layouts  84.4 us (4%)
    dot_general x27, matrix products, ein(): return jnp.einsum(spec, a, b, preferred_element_type=jnp.float32)  568 us
    all_gather x5, waiting for transfers between devices, gather(): return lax.all_gather(arr, 'sp', axis=0, tiled=False)  489 us
    all_to_all x4, blocking collectives, swap(): return lax.all_to_all(arr, 'sp', 0, 0, tiled=True)  314 us
    pallas_call x4, Pallas kernels, attention_bwd(): pl.pallas_call(functools.partial(bwd_kernel, group, heads, len(deps)), gr...  207 us
    pallas_call x4, Pallas kernels, attention_fwd(): pl.pallas_call(functools.partial(fwd_kernel, group), grid=(batch, heads),...  132 us
    transpose x14, local copies, waits for them, and re-layouts, join(): return jnp.transpose(arr, (1, 2, 0, 3)).reshape(batch, rows, n_blk * cols)  56.5 us
  transfers between devices with their start and end apart: 12, of which 6 were waited for; matrix products, arithmetic and copies ran while one was open for 27% of the time, Pallas kernels for 9%

profile of v4, /device:TPU:0, one launch (start us, length us, event | category | flops | bytes accessed | tf_op | source)
XLA Modules:
  0.0 2076.8 jit_solution(5463565146509416089)
XLA Ops:
  8.6 6.3 pre_norm.2
  14.9 6.3 pre_norm.3
  21.9 12.4 all-gather.5
  40.6 4.8 constant_dynamic-slice_fusion.2
  49.5 142.2 %all-gather.21.cloned.1.call-done = bf16[16,256,4608]{2,1,0:T(8,128)(2,1)} async-done(((bf16[2,256,4608]{2,1,0:T(8,128)(2,1)}), bf16[16,256,4608]{2,1,0:T(8,128)(2,1)}) %all-gather.21.cloned.1.call-update) | async-done | bytes 37748752 | tf_op jit(solution)/shard_map/all_gather | solution.py:311
  191.7 46.8 %convolution_convert_fusion.1.q_ref.k_ref.v_ref = bf16[8,2,256,1024]{3,2,1,0:T(8,128)(2,1)} fusion(bf16[8,2,256,4608]{3,2,1,0:T(8,128)(2,1)} %bitcast.285, bf16[4608,256]{1,0:T(8,128)(2,1)S(1)} %get-tuple-element.97, bf16[4608,256]{1,0:T(8,128)(2,1)} %get-tuple-element.98, bf16[4608,512]{1,0:T(8,128)(2,1)} %constant_dynamic-slice_fusion.2), kind=kOutput, calls=%fused_computation.88 | convolution fusion | flops 38687211520 | bytes 55574528 | tf_op jit(solution)/shard_map/jbsd,dn->jbsn/dot_general | solution.py:293
  238.5 32.7 %attention_fwd.4 = (bf16[8,1,256,512]{3,2,1,0:T(8,128)(2,1)}, f32[1,2,8,256,128]{4,3,2,1,0:T(8,128)}) custom-call(bf16[8,2,256,1024]{3,2,1,0:T(8,128)(2,1)} %convolution_convert_fusion.1.q_ref.k_ref.v_ref, bf16[8,2,256,1024]{3,2,1,0:T(8,128)(2,1)} %convolution_convert_fusion.1.q_ref.k_ref.v_ref, ...), custom_call_target="tpu_custom_call" | custom-call | flops 4294967296 | bytes 6144000 | tf_op jit(solution)/shard_map/attention_fwd/pallas_call | solution.py:202
  273.8 116.8 %all-gather.23.cloned.1.call-done = bf16[16,256,4608]{2,1,0:T(8,128)(2,1)} async-done(((bf16[2,256,4608]{2,1,0:T(8,128)(2,1)}), bf16[16,256,4608]{2,1,0:T(8,128)(2,1)}) %all-gather.23.cloned.1.call-update) | async-done | bytes 37748752 | tf_op jit(solution)/shard_map/all_gather | solution.py:311
  390.5 47.5 %convolution_convert_fusion.q_ref.k_ref.v_ref = bf16[8,2,256,1024]{3,2,1,0:T(8,128)(2,1)} fusion(bf16[8,2,256,4608]{3,2,1,0:T(8,128)(2,1)} %bitcast.290, bf16[4608,256]{1,0:T(8,128)(2,1)} %copy-done.16, bf16[4608,256]{1,0:T(8,128)(2,1)} %get-tuple-element.98, bf16[4608,512]{1,0:T(8,128)(2,1)} %constant_dynamic-slice_fusion.2), kind=kOutput, calls=%fused_computation.87 | convolution fusion | flops 38687211520 | bytes 55574528 | tf_op jit(solution)/shard_map/jbsd,dn->jbsn/dot_general | solution.py:293
  438.0 32.7 %attention_fwd.5 = (bf16[8,1,256,512]{3,2,1,0:T(8,128)(2,1)}, f32[1,2,8,256,128]{4,3,2,1,0:T(8,128)}) custom-call(bf16[8,2,256,1024]{3,2,1,0:T(8,128)(2,1)} %convolution_convert_fusion.1.q_ref.k_ref.v_ref, bf16[8,2,256,1024]{3,2,1,0:T(8,128)(2,1)} %convolution_convert_fusion.1.q_ref.k_ref.v_ref, ...), custom_call_target="tpu_custom_call" | custom-call | flops 4294967296 | bytes 6144000 | tf_op jit(solution)/shard_map/attention_fwd/pallas_call | solution.py:202
  470.6 33.1 %attention_fwd.6 = (bf16[8,1,256,512]{3,2,1,0:T(8,128)(2,1)}, f32[1,2,8,256,128]{4,3,2,1,0:T(8,128)}) custom-call(bf16[8,2,256,1024]{3,2,1,0:T(8,128)(2,1)} %convolution_convert_fusion.q_ref.k_ref.v_ref, bf16[8,2,256,1024]{3,2,1,0:T(8,128)(2,1)} %convolution_convert_fusion.q_ref.k_ref.v_ref, ...), custom_call_target="tpu_custom_call" | custom-call | flops 4294967296 | bytes 6144000 | tf_op jit(solution)/shard_map/attention_fwd/pallas_call | solution.py:202
  510.0 17.0 fusion.79
  527.0 5.8 fusion.71
  544.6 17.5 fusion.48
  562.6 4.9 fusion.72
  575.9 17.7 fusion.49
  594.2 5.2 fusion.73
  603.9 33.1 %attention_fwd.7 = (bf16[8,1,256,512]{3,2,1,0:T(8,128)(2,1)}, f32[1,2,8,256,128]{4,3,2,1,0:T(8,128)}) custom-call(bf16[8,2,256,1024]{3,2,1,0:T(8,128)(2,1)} %convolution_convert_fusion.q_ref.k_ref.v_ref, bf16[8,2,256,1024]{3,2,1,0:T(8,128)(2,1)} %convolution_convert_fusion.q_ref.k_ref.v_ref, ...), custom_call_target="tpu_custom_call" | custom-call | flops 4294967296 | bytes 6144000 | tf_op jit(solution)/shard_map/attention_fwd/pallas_call | solution.py:202
  637.1 51.1 %all_to_all.40 = bf16[8,1,256,512]{3,2,1,0:T(8,128)(2,1)} all-to-all(bf16[8,1,256,512]{3,2,1,0:T(8,128)(2,1)} %get-tuple-element.40), channel_id=1, replica_groups=mesh['dp'=1,'sp'=8] {'sp'}, dimensions={0} | all-to-all | bytes 4194304 | tf_op jit(solution)/shard_map/all_to_all | solution.py:308
  692.1 17.6 fusion.50
  710.2 5.4 fusion.74
  715.6 10.3 fusion.69
  726.0 5.3 pad_maximum_fusion.2
  731.4 17.3 convert_bitcast_fusion.2.do_ref
  748.7 69.5 %all-gather.29.cloned.1.call-done = bf16[8,256,4608]{2,1,0:T(8,128)(2,1)} async-done(((bf16[1,256,4608]{2,1,0:T(8,128)(2,1)}), bf16[8,256,4608]{2,1,0:T(8,128)(2,1)}) %all-gather.29.cloned.1.call-update) | async-done | bytes 18874384 | tf_op jit(solution)/shard_map/all_gather | solution.py:311
  818.2 16.1 convert_bitcast_fusion.1.do_ref
  834.3 160.1 %all-gather.25.cloned.1.call-done = bf16[16,256,4608]{2,1,0:T(8,128)(2,1)} async-done(((bf16[2,256,4608]{2,1,0:T(8,128)(2,1)}), bf16[16,256,4608]{2,1,0:T(8,128)(2,1)}) %all-gather.25.cloned.1.call-update) | async-done | bytes 37748752 | tf_op jit(solution)/shard_map/all_gather | solution.py:311
  994.4 16.1 fusion.4
  1010.6 26.9 %fusion.104.do_ref = bf16[8,2,256,512]{3,2,1,0:T(8,128)(2,1)} fusion(bf16[8,2,256,4608]{3,2,1,0:T(8,128)(2,1)} %bitcast.257, bf16[4096,4608]{1,0:T(8,128)(2,1)} %param.17, s32[]{:T(128)S(6)} %select_n.8), kind=kOutput, calls=%fused_computation.168 | convolution fusion | flops 19329449984 | bytes 46661636 | tf_op jit(solution)/shard_map/jbsd,nd->jbsn/dot_general | solution.py:293
  1037.5 17.5 bitcast_add_fusion.5
  1055.0 18.1 bitcast_add_fusion.4
  1073.1 51.7 %attention_bwd.4 = (bf16[8,1,256,1024]{3,2,1,0:T(8,128)(2,1)}, f32[8,128]{1,0:T(8,128)}, f32[8,128]{1,0:T(8,128)}) custom-call(bf16[8,2,256,1024]{3,2,1,0:T(8,128)(2,1)} %convolution_convert_fusion.1.q_ref.k_ref.v_ref, bf16[8,2,256,1024]{3,2,1,0:T(8,128)(2,1)} %convolution_convert_fusion.1.q_ref.k_ref.v_ref, ...), custom_call_target="tpu_custom_call" | custom-call | flops 10737418240 | bytes 12288000 | tf_op jit(solution)/shard_map/attention_bwd/pallas_call | solution.py:223
  1124.7 10.8 fusion.46
  1135.6 52.0 %attention_bwd.5 = (bf16[8,1,256,1024]{3,2,1,0:T(8,128)(2,1)}, f32[8,128]{1,0:T(8,128)}, f32[8,128]{1,0:T(8,128)}) custom-call(bf16[8,2,256,1024]{3,2,1,0:T(8,128)(2,1)} %convolution_convert_fusion.1.q_ref.k_ref.v_ref, bf16[8,2,256,1024]{3,2,1,0:T(8,128)(2,1)} %convolution_convert_fusion.1.q_ref.k_ref.v_ref, ...), custom_call_target="tpu_custom_call" | custom-call | flops 10737418240 | bytes 12288000 | tf_op jit(solution)/shard_map/attention_bwd/pallas_call | solution.py:223
  1187.6 12.8 fusion.45
  1200.4 15.7 fusion.35.refs_1_
  1216.1 51.8 %attention_bwd.6 = (bf16[8,1,256,1024]{3,2,1,0:T(8,128)(2,1)}, f32[8,128]{1,0:T(8,128)}, f32[8,128]{1,0:T(8,128)}) custom-call(bf16[8,2,256,1024]{3,2,1,0:T(8,128)(2,1)} %convolution_convert_fusion.q_ref.k_ref.v_ref, bf16[8,2,256,1024]{3,2,1,0:T(8,128)(2,1)} %convolution_convert_fusion.q_ref.k_ref.v_ref, ...), custom_call_target="tpu_custom_call" | custom-call | flops 10737418240 | bytes 12288000 | tf_op jit(solution)/shard_map/attention_bwd/pallas_call | solution.py:223
  1267.9 11.2 fusion.43
  1279.1 51.6 %attention_bwd.7 = (bf16[8,1,256,1024]{3,2,1,0:T(8,128)(2,1)}, f32[8,128]{1,0:T(8,128)}, f32[8,128]{1,0:T(8,128)}) custom-call(bf16[8,2,256,1024]{3,2,1,0:T(8,128)(2,1)} %convolution_convert_fusion.q_ref.k_ref.v_ref, bf16[8,2,256,1024]{3,2,1,0:T(8,128)(2,1)} %convolution_convert_fusion.q_ref.k_ref.v_ref, ...), custom_call_target="tpu_custom_call" | custom-call | flops 10737418240 | bytes 12288000 | tf_op jit(solution)/shard_map/attention_bwd/pallas_call | solution.py:223
  1330.8 10.6 fusion.47
  1342.2 22.1 %fusion.15 = f32[4608,768,1]{1,0,2:T(8,128)} fusion(bf16[8,2,256,4608]{3,2,1,0:T(8,128)(2,1)} %bitcast.288, bf16[8,1,256,1024]{3,2,1,0:T(8,128)(2,1)} %get-tuple-element.43.refs_0_), kind=kOutput, calls=%fused_computation.21 | convolution fusion | flops 14495514624 | bytes 36175872 | tf_op jit(solution)/shard_map/jbsd,jbsn->dn/dot_general | solution.py:293
  1364.3 23.0 %bitcast_add_fusion.2 = f32[4608,768]{1,0:T(8,128)} fusion(f32[4608,768,1]{1,0,2:T(8,128)} %fusion.15, bf16[8,2,256,4608]{3,2,1,0:T(8,128)(2,1)} %bitcast.289, bf16[8,1,256,1024]{3,2,1,0:T(8,128)(2,1)S(1)} %copy-done.5), kind=kOutput, calls=%fused_computation.39 | convolution fusion | flops 14499053568 | bytes 50331648 | tf_op jit(solution)/shard_map/jbsd,jbsn->dn/dot_general | solution.py:293
  1387.4 20.9 %fusion.19 = f32[4608,768,1]{1,0,2:T(8,128)} fusion(bf16[8,2,256,4608]{3,2,1,0:T(8,128)(2,1)} %bitcast.293, bf16[8,1,256,1024]{3,2,1,0:T(8,128)(2,1)S(1)} %copy-done.14), kind=kOutput, calls=%fused_computation.25 | convolution fusion | flops 14495514624 | bytes 36175872 | tf_op jit(solution)/shard_map/jbsd,jbsn->dn/dot_general | solution.py:293
  1408.3 25.1 %fusion.22 = bf16[4608,768]{1,0:T(8,128)(2,1)} fusion(f32[4608,768]{1,0:T(8,128)} %bitcast_add_fusion.2, f32[4608,768,1]{1,0,2:T(8,128)} %fusion.19, bf16[8,2,256,4608]{3,2,1,0:T(8,128)(2,1)} %bitcast.294, bf16[8,1,256,1024]{3,2,1,0:T(8,128)(2,1)} %get-tuple-element.49), kind=kOutput, calls=%fused_computation.37 | convolution fusion | flops 14506131456 | bytes 57409536 | tf_op jit(solution)/shard_map/jbsd,jbsn->dn/dot_general | solution.py:293
  1433.4 86.3 %all_to_all.41 = bf16[8,1,256,1024]{3,2,1,0:T(8,128)(2,1)} all-to-all(bf16[8,1,256,1024]{3,2,1,0:T(8,128)(2,1)} %get-tuple-element.43.refs_0_), channel_id=1, replica_groups=mesh['dp'=1,'sp'=8] {'sp'}, dimensions={0} | all-to-all | bytes 8388608 | tf_op jit(solution)/shard_map/all_to_all | solution.py:308
  1519.7 80.3 %all_to_all.42 = bf16[8,1,256,1024]{3,2,1,0:T(8,128)(2,1)} all-to-all(bf16[8,1,256,1024]{3,2,1,0:T(8,128)(2,1)S(1)} %copy-done.6), channel_id=1, replica_groups=mesh['dp'=1,'sp'=8] {'sp'}, dimensions={0} | all-to-all | bytes 8388608 | tf_op jit(solution)/shard_map/all_to_all | solution.py:308
  1600.0 96.4 %all_to_all.43 = bf16[8,1,256,1024]{3,2,1,0:T(8,128)(2,1)} all-to-all(bf16[8,1,256,1024]{3,2,1,0:T(8,128)(2,1)S(1)} %copy-done.15), channel_id=1, replica_groups=mesh['dp'=1,'sp'=8] {'sp'}, dimensions={0} | all-to-all | bytes 8388608 | tf_op jit(solution)/shard_map/all_to_all | solution.py:308
  1700.3 5.5 fusion.31
  1722.2 6.2 copy.65
  1743.3 30.0 %all-to-all-done.7 = bf16[8,1,256,1024]{3,2,1,0:T(8,128)(2,1)} async-done(((bf16[8,1,256,1024]{3,2,1,0:T(8,128)(2,1)}), bf16[8,1,256,1024]{3,2,1,0:T(8,128)(2,1)}, u32[]{:S(2)}, u32[]{:S(2)}) %all-to-all-start.7) | async-done | bytes 4194336 | tf_op jit(solution)/shard_map/all_to_all | solution.py:308
  1773.3 4.6 constant_dynamic-update-slice_fusion.2
  1782.5 6.9 copy.75
  1800.6 16.9 fusion.8
  1817.5 16.3 fusion.6
  1833.8 27.8 %fusion.2 = f32[2,256,4608]{2,1,0:T(8,128)} fusion(bf16[2,256,4096]{1,2,0:T(8,128)(2,1)} %bitcast.261, bf16[4608,4096]{1,0:T(8,128)(2,1)} %param.14), kind=kOutput, calls=%fused_computation.2 | convolution fusion | flops 19327352832 | bytes 51380224 | tf_op jit(solution)/shard_map/bsn,dn->bsd/dot_general | solution.py:293
  1861.6 31.0 %fusion = f32[2,256,4608]{2,1,0:T(8,128)} fusion(bf16[2,256,4096]{1,2,0:T(8,128)(2,1)} %bitcast.262, bf16[4608,4096]{1,0:T(8,128)(2,1)} %param.14), kind=kOutput, calls=%fused_computation | convolution fusion | flops 19327352832 | bytes 51380224 | tf_op jit(solution)/shard_map/bsn,dn->bsd/dot_general | solution.py:293
  1892.6 20.2 add_convert_fusion
  1912.9 27.4 %fusion.25 = (f32[4608]{0:T(1024)S(1)}, f32[2,256]{1,0:T(2,128)S(1)}, f32[2,256]{1,0:T(2,128)S(1)}, f32[4608]{0:T(1024)S(1)}, bf16[2,256,4608]{2,1,0:T(8,128)(2,1)}) fusion(f32[2,256]{1,0:T(2,128)S(1)} %get-tuple-element.101, bf16[4,256,4608]{2,1,0:T(8,128)(2,1)} %x_ref.3, f32[4608]{0:T(1024)S(1)} %broadcast_add_fusion, ...), kind=kOutput, calls=%fused_computation.48 | convolution fusion | flops 9708494848 | bytes 58783744 | tf_op jit(solution)/shard_map/bsn,dn->bsd/dot_general | solution.py:293
  1940.3 24.6 %all-reduce = (f32[4608]{0:T(1024)}, f32[4608]{0:T(1024)}, f32[128]{0:T(128)}, f32[128]{0:T(128)}) all-reduce(f32[4608]{0:T(1024)S(1)} %add.206, f32[4608]{0:T(1024)S(1)} %copy-done.23, f32[128]{0:T(128)S(1)} %copy-done.42, f32[128]{0:T(128)S(1)} %copy-done.41), channel_id=1, replica_groups=mesh['dp'=1,'sp'=8] {'sp'}, use_global_device_ids=true, to_apply=%region_14.0 | all-reduce | flops 9472 | bytes 75776 | tf_op jit(solution)/shard_map/psum | solution.py:423
  1964.9 11.6 fusion.28
  1981.0 13.8 settle.2
  1994.8 25.0 %settle.3 = bf16[4096,4608]{1,0:T(8,128)(2,1)} custom-call(bf16[4096,4608]{1,0:T(8,128)(2,1)} %all-gather.19.cloned.1.call-done.src_ref), custom_call_target="tpu_custom_call" | custom-call | flops 7549747200 | bytes 75497472 | tf_op jit(solution)/shard_map/settle/pallas_call | solution.py:263
  2019.9 11.8 all-gather.15.cloned.1.call-done.src_ref
  2031.6 38.1 %split_qk.1 = (bf16[4608,4096]{1,0:T(8,128)(2,1)}, bf16[4608,2048]{1,0:T(8,128)(2,1)}) custom-call(bf16[4608,6144]{1,0:T(8,128)(2,1)} %all-gather.15.cloned.1.call-done.src_ref), custom_call_target="tpu_custom_call" | custom-call | flops 11324620800 | bytes 113246208 | tf_op jit(solution)/shard_map/split_qk/pallas_call | solution.py:282
  (183 shorter events, 107.5 us)
Async XLA Ops:
  7.2 184.5 %all-gather.21.cloned.1.call-start = ((), (), s32[]{:S(2)}) async-start(), calls=%async_computation.11 | async-start | bytes 42467328 | tf_op jit(solution)/shard_map/all_gather | solution.py:311
  14.8 375.7 %all-gather.23.cloned.1.call-start = ((), (), s32[]{:S(2)}) async-start(), calls=%async_computation.12 | async-start | bytes 42467328 | tf_op jit(solution)/shard_map/all_gather | solution.py:311
  21.2 0.7 copy-start.43
  21.2 18.7 copy-start.28
  49.5 189.0 %copy-start.16 = (bf16[4608,256]{1,0:T(8,128)(2,1)}, bf16[4608,256]{1,0:T(8,128)(2,1)S(1)}, u32[]{:S(2)}) copy-start(bf16[4608,256]{1,0:T(8,128)(2,1)S(1)} %get-tuple-element.97) | copy-start | bytes 7077892
  271.2 232.5 %all-to-all-start = ((bf16[8,1,256,512]{3,2,1,0:T(8,128)(2,1)}), bf16[8,1,256,512]{3,2,1,0:T(8,128)(2,1)S(1)}, u32[]{:S(2)}, u32[]{:S(2)}) async-start(bf16[8,1,256,512]{3,2,1,0:T(8,128)(2,1)} %get-tuple-element.35), calls=%async_computation | async-start | bytes 4194304 | tf_op jit(solution)/shard_map/all_to_all | solution.py:308
  503.7 3.4 copy-start.13
  503.7 33.5 %all-to-all-start.1 = ((bf16[8,1,256,512]{3,2,1,0:T(8,128)(2,1)}), bf16[8,1,256,512]{3,2,1,0:T(8,128)(2,1)}, u32[]{:S(2)}, u32[]{:S(2)}) async-start(bf16[8,1,256,512]{3,2,1,0:T(8,128)(2,1)} %get-tuple-element.36), calls=%async_computation.1 | async-start | bytes 4194304 | tf_op jit(solution)/shard_map/all_to_all | solution.py:308
  510.0 17.0 copy-start.21
  527.0 5.9 copy-start.2
  537.3 34.7 %all-to-all-start.2 = ((bf16[8,1,256,512]{3,2,1,0:T(8,128)(2,1)}), bf16[8,1,256,512]{3,2,1,0:T(8,128)(2,1)}, u32[]{:S(2)}, u32[]{:S(2)}) async-start(bf16[8,1,256,512]{3,2,1,0:T(8,128)(2,1)} %get-tuple-element.38), calls=%async_computation.2 | async-start | bytes 4194304 | tf_op jit(solution)/shard_map/all_to_all | solution.py:308
  540.4 191.0 %all-gather.27.cloned.1.call-start = ((), (), s32[]{:S(2)}) async-start(), calls=%async_computation.14 | async-start | bytes 21233664 | tf_op jit(solution)/shard_map/all_gather | solution.py:311
  593.6 5.8 copy-start
  603.9 214.4 %all-gather.29.cloned.1.call-start = ((), (), s32[]{:S(2)}) async-start(), calls=%async_computation.15 | async-start | bytes 21233664 | tf_op jit(solution)/shard_map/all_gather | solution.py:311
  709.6 6.0 copy-start.1
  709.6 6.0 copy-start.3
  725.9 268.5 %all-gather.25.cloned.1.call-start = ((), (), s32[]{:S(2)}) async-start(), calls=%async_computation.13 | async-start | bytes 42467328 | tf_op jit(solution)/shard_map/all_gather | solution.py:311
  731.4 1249.6 %all-gather.17.cloned.1.call-start = ((), (), s32[]{:S(2)}) async-start(), calls=%async_computation.9 | async-start | bytes 21233664 | tf_op jit(solution)/shard_map/all_gather | solution.py:392
  748.7 245.7 %copy-start.17 = (bf16[8,1,256,512]{3,2,1,0:T(8,128)(2,1)S(1)}, bf16[8,1,256,512]{3,2,1,0:T(8,128)(2,1)}, u32[]{:S(2)}) copy-start(bf16[8,1,256,512]{3,2,1,0:T(8,128)(2,1)} %get-tuple-element.36) | copy-start | bytes 6291460
  1010.6 26.9 %copy-start.12 = (bf16[8,1,256,512]{3,2,1,0:T(8,128)(2,1)S(1)}, bf16[8,1,256,512]{3,2,1,0:T(8,128)(2,1)}, u32[]{:S(2)}) copy-start(bf16[8,1,256,512]{3,2,1,0:T(8,128)(2,1)} %get-tuple-element.35) | copy-start | bytes 6291460
  1135.6 64.8 %slice-start = ((s8[9437184]{0:T(1024)(128)(4,1)}), s8[1048576]{0:T(1024)(128)(4,1)S(1)}, s32[]{:S(2)}) async-start(s8[9437184]{0:T(1024)(128)(4,1)} %bitcast.254), calls=%async_computation.16 | async-start | bytes 2097152
  1135.6 64.8 %slice-start.1 = ((s8[9437184]{0:T(1024)(128)(4,1)}), s8[4194304]{0:T(1024)(128)(4,1)S(1)}, s32[]{:S(2)}) async-start(s8[9437184]{0:T(1024)(128)(4,1)} %bitcast.254), calls=%async_computation.17 | async-start | bytes 8388608
  1187.6 12.8 slice-start.2
  1187.6 12.8 copy-start.18
  1200.4 67.5 %slice-start.3 = ((s8[4718592]{0:T(1024)(128)(4,1)}), s8[524288]{0:T(1024)(128)(4,1)S(1)}, s32[]{:S(2)}) async-start(s8[4718592]{0:T(1024)(128)(4,1)} %bitcast.295), calls=%async_computation.19 | async-start | bytes 1048576
  1216.1 51.8 %slice-start.4 = ((s8[4718592]{0:T(1024)(128)(4,1)}), s8[4194304]{0:T(1024)(128)(4,1)S(1)}, s32[]{:S(2)}) async-start(s8[4718592]{0:T(1024)(128)(4,1)} %bitcast.295), calls=%async_computation.20 | async-start | bytes 8388608
  1279.1 51.6 %copy-start.44 = (f32[4608,256]{1,0:T(8,128)S(1)}, f32[4608,256]{1,0:T(8,128)}, u32[]{:S(2)}) copy-start(f32[4608,256]{1,0:T(8,128)} %fusion.43) | copy-start | bytes 14155780
  1341.4 653.4 %all-gather.19.cloned.1.call-start = ((), (), s32[]{:S(2)}) async-start(), calls=%async_computation.10 | async-start | bytes 42467328 | tf_op jit(solution)/shard_map/all_gather | solution.py:392
  1342.2 689.5 %all-gather.15.cloned.1.call-start = ((), (), s32[]{:S(2)}) async-start(), calls=%async_computation.8 | async-start | bytes 63700992 | tf_op jit(solution)/shard_map/all_gather | solution.py:392
  1342.2 22.1 %copy-start.5 = (bf16[8,1,256,1024]{3,2,1,0:T(8,128)(2,1)S(1)}, bf16[8,1,256,1024]{3,2,1,0:T(8,128)(2,1)}, u32[]{:S(2)}) copy-start(bf16[8,1,256,1024]{3,2,1,0:T(8,128)(2,1)} %get-tuple-element.45.refs_0_) | copy-start | bytes 12582916
  1364.3 23.0 %copy-start.14 = (bf16[8,1,256,1024]{3,2,1,0:T(8,128)(2,1)S(1)}, bf16[8,1,256,1024]{3,2,1,0:T(8,128)(2,1)}, u32[]{:S(2)}) copy-start(bf16[8,1,256,1024]{3,2,1,0:T(8,128)(2,1)} %get-tuple-element.47.refs_0_) | copy-start | bytes 12582916
  1433.4 86.3 %copy-start.6 = (bf16[8,1,256,1024]{3,2,1,0:T(8,128)(2,1)S(1)}, bf16[8,1,256,1024]{3,2,1,0:T(8,128)(2,1)}, u32[]{:S(2)}) copy-start(bf16[8,1,256,1024]{3,2,1,0:T(8,128)(2,1)} %get-tuple-element.45.refs_0_) | copy-start | bytes 12582916
  1519.7 80.3 %copy-start.15 = (bf16[8,1,256,1024]{3,2,1,0:T(8,128)(2,1)S(1)}, bf16[8,1,256,1024]{3,2,1,0:T(8,128)(2,1)}, u32[]{:S(2)}) copy-start(bf16[8,1,256,1024]{3,2,1,0:T(8,128)(2,1)} %get-tuple-element.47.refs_0_) | copy-start | bytes 12582916
  1696.4 9.5 copy-start.22
  1696.4 9.5 copy-start.27
  1696.4 76.9 %all-to-all-start.7 = ((bf16[8,1,256,1024]{3,2,1,0:T(8,128)(2,1)}), bf16[8,1,256,1024]{3,2,1,0:T(8,128)(2,1)}, u32[]{:S(2)}, u32[]{:S(2)}) async-start(bf16[8,1,256,1024]{3,2,1,0:T(8,128)(2,1)} %get-tuple-element.49), calls=%async_computation.7 | async-start | bytes 8388608 | tf_op jit(solution)/shard_map/all_to_all | solution.py:308
  1700.3 5.6 copy-start.24
  1700.3 5.6 copy-start.25
  1700.3 5.6 copy-start.26
  1700.3 6.3 copy-start.8
  1700.3 6.2 copy-start.9
  1700.3 6.4 copy-start.10
  1700.3 7.1 copy-start.11
  1705.8 5.9 copy-start.29
  1705.8 5.9 copy-start.31
  1707.4 4.3 copy-start.40
  1707.4 4.3 copy-start.38
  1707.4 4.3 copy-start.36
  1707.4 4.3 copy-start.34
  1707.4 4.3 copy-start.39
  1707.5 4.4 copy-start.37
  1707.5 4.4 copy-start.35
  1707.5 4.4 copy-start.33
  1711.9 3.9 copy-start.7
  1716.3 3.4 copy-start.4
  1800.6 17.0 copy-start.20
  1892.6 20.2 copy-start.19
  1912.8 27.5 %copy-start.23 = (f32[4608]{0:T(1024)S(1)}, f32[4608]{0:T(1024)}, u32[]{:S(2)}) copy-start(f32[4608]{0:T(1024)} %add_add_fusion.6) | copy-start | bytes 55300
  1912.8 27.5 %copy-start.41 = (f32[128]{0:T(128)S(1)}, f32[128]{0:T(128)}, u32[]{:S(2)}) copy-start(f32[128]{0:T(128)} %add_add_fusion.7) | copy-start | bytes 1540
  1912.8 27.5 %copy-start.42 = (f32[128]{0:T(128)S(1)}, f32[128]{0:T(128)}, u32[]{:S(2)}) copy-start(f32[128]{0:T(128)} %add_add_fusion.8) | copy-start | bytes 1540
  1912.8 52.1 %copy-start.32 = (f32[2,256]{1,0:T(2,128)S(1)}, f32[2,256]{1,0:T(2,128)}, u32[]{:S(2)}) copy-start(f32[2,256]{1,0:T(2,128)} %copy-done.31) | copy-start | bytes 6148
  1912.8 52.1 %copy-start.30 = (f32[2,256]{1,0:T(2,128)S(1)}, f32[2,256]{1,0:T(2,128)}, u32[]{:S(2)}) copy-start(f32[2,256]{1,0:T(2,128)} %copy-done.29) | copy-start | bytes 6148
Sparse Core Ops, SparseCore 0:
  15.0 176.6 all-gather.20
  194.1 196.3 all-gather.22
  604.0 115.0 all-gather.26
  726.1 92.1 all-gather.28
  820.5 173.8 all-gather.24
  1341.5 96.7 all-gather.16
  1440.2 324.7 all-gather.18
  1767.4 264.1 all-gather.14
